TPU v7x, 256 devices: a 8x8x2 block of a 8x8x16 slice. The times are simulated.
256 devices in a mesh: parts: 2 (over z), row: 128 (over y, x, core).
Axes of the slice: x: 8, y: 8, z: 2, core: 2. Of those that a mesh axis runs over, the one named last changes fastest.
The devices are a block of a 8x8x16 slice.
Arguments:
- sigma_top: bfloat16 [4096, 2048], P(('parts', 'row')), parts along dimension 0, may hold values from -2 to 8, as said below
- panel_par: bfloat16 [4096, 1024], P(('parts', 'row')), parts along dimension 0, may hold values from -0.25 to 0.25
- dinv_par: float32 [2048, 1024], P(('parts', 'row')), parts along dimension 0, may hold values from -2 to 8, as said below
- panel_kid_top: bfloat16 [4, 2048, 1024], P('parts', 'row'), parts along dimension 0, may hold values from -0.25 to 0.25
- panel_kid_par: bfloat16 [4, 1024, 1024], P('parts', 'row'), parts along dimension 0, may hold values from -0.375 to 0.375
- dvar_kid: float32 [4, 1024], P('parts'), parts along dimension 0, may hold values from 0.5 to 2
- mask_par: int32 [16, 4], P('parts'), parts along dimension 0, may hold values 0 or 1
- mask_kid_top: int32 [4, 8, 4], P('parts'), parts along dimension 0, may hold values 0 or 1
- mask_kid_par: int32 [4, 4, 4], P('parts'), parts along dimension 0, may hold values 0 or 1
Outputs:
- cross_par: bfloat16 [4096, 1024], P(('parts', 'row')), parts along dimension 0
- sigma_par: bfloat16 [2048, 1024], P(('parts', 'row')), parts along dimension 0
- cross_kid_top: bfloat16 [4, 2048, 1024], P('parts', 'row'), parts along dimension 0
- cross_kid_par: bfloat16 [4, 1024, 1024], P('parts', 'row'), parts along dimension 0
- variance_kid: float32 [4, 1024], P('parts'), parts along dimension 0
There are 2 independent parts, one for each index of `parts`. A program takes and returns all parts, laid end to end along the dimension named above; each array names one. Nothing has to cross between parts.
Inputs may be any that keep to these rules, and one draw needn't show every extreme that they name: `sigma_top`: symmetric positive definite. `dinv_par`: symmetric positive definite.
All inputs are finite; a program needn't handle non-finite values.
Results may differ from a plain program's by a relative error of at most 0.0052.
Values may be sent and summed in bfloat16 or wider, within the bound.
No kernel may reach another device: no remote copies, remote signals or barrier semaphores. Data moves between devices by JAX's collectives and lax.ppermute only.
A program may use at most 64 MiB of HBM per device.

v0:
```python
import jax
import jax.numpy as jnp
from jax import lax
from jax.sharding import Mesh
from jax.sharding import PartitionSpec as P

BLK = 256
ROW = ("row_0", "row_1", "row_2")
PARTS_ROW = ("parts", "row_0", "row_1", "row_2")


def laid_out(tiles, dim):
    shape = list(tiles.shape[1:])
    shape[dim] *= tiles.shape[0]
    return jnp.moveaxis(tiles, 0, dim).reshape(shape)


def stacked_from(x, axes, order):
    tiles = x
    for k in order:
        tiles = lax.all_gather(tiles, axes[k])
    done = order[::-1]
    back = [done.index(k) for k in range(len(axes))]
    tiles = tiles.transpose(*back, *range(len(axes), tiles.ndim))
    return tiles.reshape(-1, *x.shape)


def gather_axes(x, axes, order, dim):
    return laid_out(stacked_from(x, axes, order), dim)


def sent_to_all(x, axis):
    copies = jnp.broadcast_to(x, (lax.axis_size(axis), *x.shape))
    return lax.all_to_all(copies, axis, split_axis=0, concat_axis=0, tiled=True)


def gathered_by_axis(x, axes, dim):
    far, near = axes
    leading = sent_to_all(x, far)
    tiles = jnp.swapaxes(sent_to_all(leading, near), 0, 1)
    return laid_out(tiles.reshape(-1, *x.shape), dim)


def over_copies(x, axis):
    return sent_to_all(x, axis).sum(axis=0)


def by_axis(x, axes):
    far, near = axes
    nearer = over_copies(x, near)
    return over_copies(nearer, far)


def block_mask(mask, rows, first):
    index = (first + jnp.arange(rows, dtype=jnp.int32)) // BLK
    picker = (index[:, None] == jnp.arange(mask.shape[-2], dtype=jnp.int32)[None, :]).astype(
        jnp.float32
    )
    picked = jnp.einsum("rb,...bc->...rc", picker, mask.astype(jnp.float32))
    return jnp.repeat(picked, BLK, axis=-1).astype(jnp.bfloat16)


def shards(
    sigma_top,
    panel_par,
    dinv_par,
    panel_kid_top,
    panel_kid_par,
    dvar_kid,
    mask_par,
    mask_kid_top,
    mask_kid_par,
):
    rows_top = sigma_top.shape[0]
    rows_par = dinv_par.shape[0]
    position = lax.axis_index(ROW)
    par_masked = panel_par * block_mask(mask_par, rows_top, position * rows_top)
    kid_top_masked = panel_kid_top * block_mask(mask_kid_top, rows_top, position * rows_top)
    kid_par_masked = panel_kid_par * block_mask(mask_kid_par, rows_par, position * rows_par)
    columns = sigma_top
    cross_wide = jnp.dot(
        columns, gather_axes(par_masked, ROW, (0, 1, 2), 0), preferred_element_type=jnp.float32
    )
    cross_par = cross_wide.astype(jnp.bfloat16)
    turned = lax.all_to_all(par_masked, ROW, split_axis=1, concat_axis=0, tiled=True)
    panel_rows = turned.T
    columns = panel_rows
    diag_sum = jnp.dot(
        columns,
        gathered_by_axis(cross_par, (("row_0", "row_1"), "row_2"), 0),
        preferred_element_type=jnp.float32,
    )
    sigma_par = (dinv_par + diag_sum).astype(jnp.bfloat16)
    turned_cross = lax.all_to_all(cross_par, ROW, split_axis=1, concat_axis=0, tiled=True)
    cross_rows_par = turned_cross.T
    piece = lax.all_gather(kid_top_masked, ROW, axis=1, tiled=True)
    upper = jnp.einsum("rc,kcw->krw", sigma_top, piece, preferred_element_type=jnp.float32)
    lower = jnp.einsum("rc,kcw->krw", cross_rows_par, piece, preferred_element_type=jnp.float32)
    acc_top = upper
    acc_par = lower
    piece = gathered_by_axis(kid_par_masked, (("row_0", "row_1"), "row_2"), 1)
    upper = acc_top + jnp.einsum(
        "rc,kcw->krw", cross_par, piece, preferred_element_type=jnp.float32
    )
    lower = acc_par + jnp.einsum(
        "rc,kcw->krw", sigma_par, piece, preferred_element_type=jnp.float32
    )
    cross_kid_top = upper.astype(jnp.bfloat16)
    cross_kid_par = lower.astype(jnp.bfloat16)
    partial_var = jnp.sum(
        kid_top_masked.astype(jnp.float32) * cross_kid_top.astype(jnp.float32), axis=1
    )
    partial_var = partial_var + jnp.sum(
        kid_par_masked.astype(jnp.float32) * cross_kid_par.astype(jnp.float32), axis=1
    )
    variance_kid = dvar_kid + by_axis(partial_var, (("row_0", "row_1"), "row_2"))
    return (cross_par, sigma_par, cross_kid_top, cross_kid_par, variance_kid)


def solution(mesh):
    finer = Mesh(
        mesh.devices.reshape(mesh.shape["parts"], 8, 8, 2), ("parts", "row_0", "row_1", "row_2")
    )
    return jax.shard_map(
        shards,
        mesh=finer,
        in_specs=(
            P(PARTS_ROW, None),
            P(PARTS_ROW, None),
            P(PARTS_ROW, None),
            P("parts", ROW, None),
            P("parts", ROW, None),
            P("parts", None),
            P("parts", None),
            P("parts", None, None),
            P("parts", None, None),
        ),
        out_specs=(
            P(PARTS_ROW, None),
            P(PARTS_ROW, None),
            P("parts", ROW, None),
            P("parts", ROW, None),
            P("parts", None),
        ),
        check_vma=False,
    )
```

profile of v0, /device:TPU:513, one launch (start us, length us, event | category | flops | bytes accessed | tf_op | source)
XLA Modules:
  0.0 339.7 jit_solution(4356895538441311231)
XLA Ops:
  7.2 0.0 copy-start
  7.2 0.1 all-gather.9.cloned.1.call-start
  7.3 0.8 convolution_convert_fusion.1
  8.1 0.1 copy.67
  8.2 0.1 broadcast_in_dim.33
  8.3 0.8 mul.31
  9.1 30.3 %all-gather = bf16[128,1024]{1,0:T(8,128)(2,1)} all-gather(bf16[16,1024]{1,0:T(8,128)(2,1)S(1)} %mul.31), channel_id=2, replica_groups=mesh['parts'=2,'row_0'=8,'row_1'=8,'row_2'=2] {'row_0'}, dimensions={0}, use_global_device_ids=true | all-gather | bytes 294912 | tf_op jit(solution)/shard_map/all_gather | solution.py:21
  39.3 0.1 all-gather.9.cloned.1.call-update
  39.4 0.1 all-gather.11.cloned.1.call-start
  39.5 53.2 %all-gather.9.cloned.1.call-done = bf16[64,16,1024]{2,1,0:T(8,128)(2,1)} async-done(((bf16[8,16,1024]{2,1,0:T(8,128)(2,1)}), bf16[64,16,1024]{2,1,0:T(8,128)(2,1)}) %all-gather.9.cloned.1.call-update) | async-done | bytes 2097168 | tf_op jit(solution)/shard_map/all_gather | solution.py:21
  92.7 0.1 all-gather.11.cloned.1.call-update
  92.7 0.1 all-gather.7.cloned.1.call-start
  92.8 0.7 convert_element_type.78
  93.5 0.1 fusion.21
  93.6 0.1 copy.72
  93.7 0.1 broadcast_in_dim.36
  93.9 1.5 mul.32
  95.4 0.1 all-gather.7.cloned.1.call-update
  95.4 0.7 convert_element_type.82
  96.1 0.1 copy.73
  96.2 0.1 fusion.25
  96.4 0.1 broadcast_in_dim.37
  96.4 0.8 mul.34
  97.2 1.6 broadcast_in_dim.38
  98.8 11.5 %all-to-all-start.3 = ((bf16[64,2,8,1024]{3,2,1,0:T(8,128)(2,1)}), bf16[64,2,8,1024]{3,2,1,0:T(8,128)(2,1)S(1)}, u32[]{:S(2)}, u32[]{:S(2)}) async-start(bf16[64,2,8,1024]{3,2,1,0:T(8,128)(2,1)} %broadcast_in_dim.38), calls=%async_computation.3 | async-start | bytes 4194304 | tf_op jit(solution)/shard_map/all_to_all | solution.py:34
  110.3 0.8 copy.69
  111.2 42.6 %all-to-all-done.3 = bf16[64,2,8,1024]{3,2,1,0:T(8,128)(2,1)S(1)} async-done(((bf16[64,2,8,1024]{3,2,1,0:T(8,128)(2,1)}), bf16[64,2,8,1024]{3,2,1,0:T(8,128)(2,1)S(1)}, u32[]{:S(2)}, u32[]{:S(2)}) %all-to-all-start.3) | async-done | bytes 2097184 | tf_op jit(solution)/shard_map/all_to_all | solution.py:34
  153.8 1.3 copy-done.4
  155.1 19.3 %all-to-all-start = ((bf16[16,128,8]{0,2,1:T(8,128)(2,1)}), bf16[16,128,8]{0,2,1:T(8,128)(2,1)S(1)}, u32[]{:S(2)}, u32[]{:S(2)}) async-start(bf16[16,128,8]{0,2,1:T(8,128)(2,1)} %bitcast.6), calls=%async_computation | async-start | bytes 524288 | tf_op jit(solution)/shard_map/all_to_all | solution.py:85
  174.4 1.8 copy.74
  176.2 0.0 all-gather.11.cloned.1.call-done
  176.2 2.6 copy.68
  178.8 0.0 copy-done
  178.9 0.7 convolution_convert_fusion
  179.5 0.2 copy.77
  179.7 8.8 %all-to-all-done = bf16[16,128,8]{0,2,1:T(8,128)(2,1)S(1)} async-done(((bf16[16,128,8]{0,2,1:T(8,128)(2,1)}), bf16[16,128,8]{0,2,1:T(8,128)(2,1)S(1)}, u32[]{:S(2)}, u32[]{:S(2)}) %all-to-all-start) | async-done | bytes 32800 | tf_op jit(solution)/shard_map/all_to_all | solution.py:85
  188.5 0.5 broadcast_in_dim.39
  189.0 8.9 %all_to_all.68 = bf16[2,64,2,8,1024]{4,3,1,2,0:T(8,128)(2,1)} all-to-all(bf16[2,64,2,8,1024]{4,3,1,2,0:T(8,128)(2,1)S(1)} %broadcast_in_dim.39), channel_id=1, replica_groups=mesh['parts'=2,'row_0'=8,'row_1'=8,'row_2'=2] {'row_2'}, dimensions={0} | all-to-all | bytes 8388608 | tf_op jit(solution)/shard_map/all_to_all | solution.py:34
  197.9 24.1 %all_to_all.69 = bf16[16,128,8]{0,2,1:T(8,128)(2,1)S(1)} all-to-all(bf16[16,128,8]{0,2,1:T(8,128)(2,1)S(1)} %bitcast.86), channel_id=1, replica_groups=mesh['parts'=2,'row_0'=8,'row_1'=8,'row_2'=2] {'row_0','row_1','row_2'}, dimensions={1} | all-to-all | bytes 65536 | tf_op jit(solution)/shard_map/all_to_all | solution.py:94
  222.0 1.6 broadcast_in_dim.34
  223.6 6.6 %all-to-all-start.1 = ((bf16[64,16,1024]{2,1,0:T(8,128)(2,1)}), bf16[64,16,1024]{2,1,0:T(8,128)(2,1)S(1)}, u32[]{:S(2)}, u32[]{:S(2)}) async-start(bf16[64,16,1024]{2,1,0:T(8,128)(2,1)} %broadcast_in_dim.34), calls=%async_computation.1 | async-start | bytes 4194304 | tf_op jit(solution)/shard_map/all_to_all | solution.py:34
  230.2 0.3 all_to_all.49
  230.5 2.6 copy.75
  233.1 0.0 copy-start.2
  233.1 1.9 copy-done.2
  235.1 0.7 fusion.2
  235.8 0.3 reshape.77
  236.1 44.0 %all-to-all-done.1 = bf16[64,16,1024]{2,1,0:T(8,128)(2,1)S(1)} async-done(((bf16[64,16,1024]{2,1,0:T(8,128)(2,1)}), bf16[64,16,1024]{2,1,0:T(8,128)(2,1)S(1)}, u32[]{:S(2)}, u32[]{:S(2)}) %all-to-all-start.1) | async-done | bytes 2097184 | tf_op jit(solution)/shard_map/all_to_all | solution.py:34
  280.1 0.5 broadcast_in_dim.35
  280.7 9.4 %all_to_all.70 = bf16[2,64,16,1024]{3,2,1,0:T(8,128)(2,1)S(1)} all-to-all(bf16[2,64,16,1024]{3,2,1,0:T(8,128)(2,1)S(1)} %broadcast_in_dim.35), channel_id=1, replica_groups=mesh['parts'=2,'row_0'=8,'row_1'=8,'row_2'=2] {'row_2'}, dimensions={0} | all-to-all | bytes 8388608 | tf_op jit(solution)/shard_map/all_to_all | solution.py:34
  290.1 0.8 copy.71
  290.9 0.7 fusion.17
  291.6 0.0 copy-start.3
  291.6 0.0 copy-start.1
  291.6 4.7 %fusion.27 = f32[2,1024,8]{1,2,0:T(8,128)S(1)} fusion(bf16[2,2048,1024]{2,1,0:T(8,128)(2,1)} %all-gather.7.cloned.1.call-done, bf16[2048,8,1]{0,1,2:T(8,128)(2,1)S(1)} %reshape.77), kind=kOutput, calls=%fused_computation.39 | convolution fusion | flops 67108864 | bytes 8486912 | tf_op jit(solution)/shard_map/rc,kcw->krw/dot_general | solution.py:98
  296.3 1.3 multiply_reduce_fusion.1
  297.6 1.0 copy-done.1
  298.6 0.0 copy-done.5
  298.7 1.8 multiply_reduce_fusion
  300.5 3.8 %all_to_all.71 = f32[2,2,1024]{2,1,0:T(2,128)S(1)} all-to-all(f32[2,2,1024]{2,1,0:T(2,128)S(1)} %broadcast_in_dim.40), channel_id=1, replica_groups=mesh['parts'=2,'row_0'=8,'row_1'=8,'row_2'=2] {'row_2'}, dimensions={0} | all-to-all | bytes 32768 | tf_op jit(solution)/shard_map/all_to_all | solution.py:34
  304.3 0.1 broadcast_in_dim.41
  304.5 27.9 %all_to_all.72 = f32[64,2,1024]{2,1,0:T(2,128)S(1)} all-to-all(f32[64,2,1024]{2,1,0:T(2,128)S(1)} %broadcast_in_dim.41), channel_id=1, replica_groups=mesh['parts'=2,'row_0'=8,'row_1'=8,'row_2'=2] {'row_0','row_1'}, dimensions={0} | all-to-all | bytes 1048576 | tf_op jit(solution)/shard_map/all_to_all | solution.py:34
  332.4 0.2 reduce_sum.39
  332.6 0.6 add.65
  (23 shorter events, 0.2 us)
Async XLA Ops:
  7.2 171.7 %copy-start = (bf16[16,2048]{1,0:T(8,128)(2,1)S(1)}, bf16[16,2048]{1,0:T(8,128)(2,1)}, u32[]{:S(2)}) copy-start(bf16[16,2048]{1,0:T(8,128)(2,1)} %param.9) | copy-start | bytes 196612
  7.2 85.5 %all-gather.9.cloned.1.call-start = ((), (), s32[]{:S(2)}) async-start(), calls=%async_computation.9 | async-start | bytes 2359296 | tf_op jit(solution)/shard_map/all_gather | solution.py:21
  39.4 136.8 %all-gather.11.cloned.1.call-start = ((), (), s32[]{:S(2)}) async-start(), calls=%async_computation.10 | async-start | bytes 6291456 | tf_op jit(solution)/shard_map/all_gather | solution.py:21
  92.7 198.8 %all-gather.7.cloned.1.call-start = ((), (), s32[]{:S(2)}) async-start(), calls=%async_computation.8 | async-start | bytes 8454144 | tf_op jit(solution)/shard_map/all_gather | solution.py:96
  98.8 55.0 %all-to-all-start.3 = ((bf16[64,2,8,1024]{3,2,1,0:T(8,128)(2,1)}), bf16[64,2,8,1024]{3,2,1,0:T(8,128)(2,1)S(1)}, u32[]{:S(2)}, u32[]{:S(2)}) async-start(bf16[64,2,8,1024]{3,2,1,0:T(8,128)(2,1)} %broadcast_in_dim.38), calls=%async_computation.3 | async-start | bytes 4194304 | tf_op jit(solution)/shard_map/all_to_all | solution.py:34
  153.8 1.3 copy-start.4
  155.1 33.4 %all-to-all-start = ((bf16[16,128,8]{0,2,1:T(8,128)(2,1)}), bf16[16,128,8]{0,2,1:T(8,128)(2,1)S(1)}, u32[]{:S(2)}, u32[]{:S(2)}) async-start(bf16[16,128,8]{0,2,1:T(8,128)(2,1)} %bitcast.6), calls=%async_computation | async-start | bytes 524288 | tf_op jit(solution)/shard_map/all_to_all | solution.py:85
  179.5 53.6 %copy-start.6 = (bf16[1024,16]{0,1:T(8,128)(2,1)}, bf16[1024,16]{0,1:T(8,128)(2,1)S(1)}, u32[]{:S(2)}) copy-start(bf16[1024,16]{0,1:T(8,128)(2,1)S(1)} %convolution_convert_fusion) | copy-start | bytes 98308
  223.6 56.6 %all-to-all-start.1 = ((bf16[64,16,1024]{2,1,0:T(8,128)(2,1)}), bf16[64,16,1024]{2,1,0:T(8,128)(2,1)S(1)}, u32[]{:S(2)}, u32[]{:S(2)}) async-start(bf16[64,16,1024]{2,1,0:T(8,128)(2,1)} %broadcast_in_dim.34), calls=%async_computation.1 | async-start | bytes 4194304 | tf_op jit(solution)/shard_map/all_to_all | solution.py:34
  233.1 2.0 copy-start.2
  290.1 0.8 copy-start.7
  291.6 4.7 %copy-start.8 = (bf16[8,1024]{1,0:T(8,128)(2,1)}, bf16[8,1024]{1,0:T(8,128)(2,1)S(1)}, u32[]{:S(2)}) copy-start(bf16[8,1024]{1,0:T(8,128)(2,1)S(1)} %fusion.17) | copy-start | bytes 49156
  291.6 4.7 %copy-start.3 = (bf16[2,64,2,8,1024]{4,3,2,0,1:T(8,128)(2,1)S(1)}, bf16[2,64,2,8,1024]{4,3,2,0,1:T(8,128)(2,1)}, u32[]{:S(2)}) copy-start(bf16[2,64,2,8,1024]{4,3,2,0,1:T(8,128)(2,1)} %copy-done.2) | copy-start | bytes 12582916
  291.6 7.1 %copy-start.1 = (bf16[2,2048,1024]{2,1,0:T(8,128)(2,1)S(1)}, bf16[2,2048,1024]{2,1,0:T(8,128)(2,1)}, u32[]{:S(2)}) copy-start(bf16[2,2048,1024]{2,1,0:T(8,128)(2,1)} %all-gather.7.cloned.1.call-done) | copy-start | bytes 25165828
  296.3 2.4 copy-start.5
  298.7 33.9 %copy-start.9 = (f32[2,1024]{1,0:T(2,128)S(1)}, f32[2,1024]{1,0:T(2,128)}, u32[]{:S(2)}) copy-start(f32[2,1024]{1,0:T(2,128)} %param.14) | copy-start | bytes 24580
Sparse Core Ops, SparseCore 0:
  39.5 53.1 all-gather.8
  94.5 24.7 all-gather.10
  122.5 108.7 all-gather.6
where the time goes:
time: 342 us; the launch traced here: 340 us
  waiting for transfers between devices  149 us (44%)
  blocking collectives  104 us (30%)
  starting transfers between devices  37.6 us (11%)
  local copies, waits for them, and re-layouts  18.9 us (6%)
  between operations  14 us (4%)
  matrix products  10.9 us (3%)
  other arithmetic  5.28 us (2%)
    all_to_all x2, waiting for transfers between devices, sent_to_all(): return lax.all_to_all(copies, axis, split_axis=0, concat_axis=0, tiled=True)  86.7 us
    all_gather x2, waiting for transfers between devices, stacked_from(): tiles = lax.all_gather(tiles, axes[k])  53.2 us
    all_to_all x4, blocking collectives, sent_to_all(): return lax.all_to_all(copies, axis, split_axis=0, concat_axis=0, tiled=True)  49.9 us
    all_gather x1, blocking collectives, stacked_from(): tiles = lax.all_gather(tiles, axes[k])  30.3 us
    all_to_all x1, blocking collectives, shards(): lax.all_to_all(cross_par, ROW, split_axis=1, concat_axis=0, tiled=True)  24.1 us
    all_to_all x1, starting transfers between devices, shards(): lax.all_to_all(par_masked, ROW, split_axis=1, concat_axis=0, tiled=True)  19.3 us
    all_to_all x2, starting transfers between devices, sent_to_all(): return lax.all_to_all(copies, axis, split_axis=0, concat_axis=0, tiled=True)  18.1 us
    all_to_all x1, waiting for transfers between devices, shards(): lax.all_to_all(par_masked, ROW, split_axis=1, concat_axis=0, tiled=True)  8.82 us
  transfers between devices with their start and end apart: 6, of which 4 were waited for; matrix products, arithmetic and copies ran while one was open for 6% of the time, Pallas kernels for 0%

commit v1 on v0

v1 whole, which is shorter than its diff:
```python
import jax
import jax.numpy as jnp
from jax import lax
from jax.sharding import Mesh
from jax.sharding import PartitionSpec as P

BLK = 256
LANES = 128
ROW = ("y", "x", "c")
PARTS_ROW = ("parts", "y", "x", "c")
XC = ("x", "c")
F32 = jnp.float32
BF16 = jnp.bfloat16


def exchanged(x, axes):
    return lax.all_to_all(x, axes, split_axis=0, concat_axis=0, tiled=True)


def sent_to_all(x, axes):
    return exchanged(jnp.broadcast_to(x, (lax.axis_size(axes), *x.shape)), axes)


def row_mask(mask, rows, first):
    picked = lax.dynamic_index_in_dim(mask, first // BLK, axis=mask.ndim - 2, keepdims=True)
    assert BLK % rows == 0
    return jnp.repeat(picked, BLK, axis=-1).astype(BF16)


def dot(a, b):
    return jnp.dot(a, b, preferred_element_type=F32)


def dot_t(a, b):
    return lax.dot_general(a, b, (((0,), (0,)), ((), ())), preferred_element_type=F32)


def split3(v):
    parts = []
    for _ in range(3):
        top = lax.reduce_precision(v, 8, 7)
        parts.append(top.astype(BF16))
        v = v - top
    return jnp.stack(parts + [jnp.zeros_like(parts[0])])


def column_slots(x):
    rows = x.shape[-2]
    x = x.reshape(-1, rows, x.shape[-1] // LANES, LANES)
    return x.transpose(0, 2, 1, 3).reshape(-1, rows, LANES)


def from_column_slots(x, kids):
    rows = x.shape[1]
    x = x.reshape(kids, -1, rows, LANES).transpose(0, 2, 1, 3)
    return x.reshape(kids, rows, -1)


def halves_beside(x):
    n, rows, width = x.shape
    x = x.reshape(n, 2, rows // 2, width).transpose(0, 2, 1, 3)
    return x.reshape(n, rows // 2, 2 * width)


def halves_below(x):
    n, rows, width = x.shape
    x = x.reshape(n, rows, 2, width // 2).transpose(0, 2, 1, 3)
    return x.reshape(n, 2 * rows, width // 2)


def shards(
    sigma_top,
    panel_par,
    dinv_par,
    panel_kid_top,
    panel_kid_par,
    dvar_kid,
    mask_par,
    mask_kid_top,
    mask_kid_par,
):
    rt, wt = sigma_top.shape
    rp, w1 = dinv_par.shape
    kids, _, w2 = panel_kid_top.shape
    ny = lax.axis_size("y")
    nx = lax.axis_size("x")
    nj = lax.axis_size(XC)
    half = w1 // nj
    assert kids * w2 == nj * LANES and 2 * half == LANES and wt == 2 * w1
    position = lax.axis_index(ROW)
    first_core = lax.axis_index("c") == 0

    def in_order(own, other, rows):
        own = own.reshape(nx, rows, -1)
        other = other.reshape(nx, rows, -1)
        low = jnp.where(first_core, own, other)
        high = jnp.where(first_core, other, own)
        return jnp.stack([low, high], axis=1).reshape(nj, rows, -1)

    par = panel_par * row_mask(mask_par, rt, position * rt)
    kid_top = panel_kid_top * row_mask(mask_kid_top, rt, position * rt)
    kid_par = panel_kid_par * row_mask(mask_kid_par, rp, position * rp)

    par_slots = halves_beside(par.reshape(rt, nj, half).transpose(1, 0, 2))
    cols = jnp.concatenate([column_slots(kid_par), par_slots, column_slots(kid_top)], axis=1)
    cols = exchanged(cols, XC)
    rows = jnp.concatenate([par, sigma_top[:, :w1], sigma_top[:, w1:], dinv_par.astype(BF16)])
    rows = sent_to_all(rows, "x")
    others = lax.ppermute(rows, "c", [(0, 1), (1, 0)])

    def pieces(r):
        cut = [0, rt, 2 * rt, 3 * rt, 3 * rt + rp]
        return [r[:, a:b].reshape(-1, w1) for a, b in zip(cut[:-1], cut[1:])]

    par_own, s0_own, s1_own, d_own = pieces(rows)
    par_oth, s0_oth, s1_oth, d_oth = pieces(others)

    tall = sent_to_all(cols[:, : 2 * rp], "y")
    kid_par_j = tall[:, :, :rp].reshape(w1, LANES)
    par_j = halves_below(tall[:, :, rp:].reshape(ny * nj, rp, LANES)).reshape(wt, half)

    kid_par_tile = cols[:, :rp].astype(F32)
    kid_top_tile = cols[:, 2 * rp :].astype(F32)
    step = kid_top_tile + in_order(dot(par_own, kid_par_j), dot(par_oth, kid_par_j), rt)
    step_j = sent_to_all(step.astype(BF16), "y").reshape(wt, LANES)

    both_j = jnp.concatenate([step_j, par_j], axis=1)
    x_own = (dot(s0_own, both_j[:w1]) + dot(s1_own, both_j[w1:])).astype(BF16)
    x_oth = (dot(s0_oth, both_j[:w1]) + dot(s1_oth, both_j[w1:])).astype(BF16)
    x_tile = in_order(x_own, x_oth, rt)
    kt_tile = x_tile[:, :, :LANES]
    c_tile = x_tile[:, :, LANES:]

    db_tile = in_order(dot(d_own, kid_par_j), dot(d_oth, kid_par_j), rp)
    var_part = jnp.sum(step * kt_tile.astype(F32), axis=(0, 1))
    var_part = var_part + jnp.sum(kid_par_tile * db_tile, axis=(0, 1))

    y_part = dot_t(par_own, x_own) + dot_t(par_oth, x_oth)
    kp_part = y_part[:, :LANES].astype(BF16).reshape(ny, nj * rp, LANES)
    q_part = halves_beside(y_part[:, LANES:].astype(BF16).reshape(ny * nj, rp, half))
    q_part = q_part.reshape(ny, nj * rp // 2, LANES)
    var_rows = jnp.broadcast_to(split3(var_part), (ny, 4, LANES))
    summed = exchanged(jnp.concatenate([kp_part, q_part, var_rows], axis=1), "y")
    summed = jnp.sum(summed.astype(F32), axis=0)
    n1 = nj * rp
    kp_tile = summed[:n1].reshape(nj, rp, LANES) + db_tile
    q_tile = summed[n1 : n1 + n1 // 2].reshape(nj, rp // 2, LANES)
    var_j = jnp.sum(summed[n1 + n1 // 2 :], axis=0)

    out = jnp.concatenate(
        [
            kt_tile,
            kp_tile.astype(BF16),
            halves_beside(c_tile),
            q_tile.astype(BF16),
            jnp.broadcast_to(split3(var_j), (nj, 4, LANES)),
        ],
        axis=1,
    )
    out = exchanged(out, XC)
    cut = [rt, rt + rp, rt + 2 * rp, rt + 2 * rp + rp // 2]
    kt, kp, cr, q, var = jnp.split(out, cut, axis=1)
    cross_kid_top = from_column_slots(kt, kids)
    cross_kid_par = from_column_slots(kp, kids)
    cross_par = halves_below(cr).transpose(1, 0, 2).reshape(rt, w1)
    q = halves_below(q).transpose(1, 0, 2).reshape(rp, w1)
    sigma_par = (dinv_par + q.astype(F32)).astype(BF16)
    variance_kid = dvar_kid + jnp.sum(var.astype(F32), axis=1).reshape(kids, w2)
    return (cross_par, sigma_par, cross_kid_top, cross_kid_par, variance_kid)


def solution(mesh):
    finer = Mesh(mesh.devices.reshape(mesh.shape["parts"], 8, 8, 2), PARTS_ROW)
    return jax.shard_map(
        shards,
        mesh=finer,
        in_specs=(
            P(PARTS_ROW, None),
            P(PARTS_ROW, None),
            P(PARTS_ROW, None),
            P("parts", ROW, None),
            P("parts", ROW, None),
            P("parts", None),
            P("parts", None),
            P("parts", None, None),
            P("parts", None, None),
        ),
        out_specs=(
            P(PARTS_ROW, None),
            P(PARTS_ROW, None),
            P("parts", ROW, None),
            P("parts", ROW, None),
            P("parts", None),
        ),
        check_vma=False,
    )
```

time: 342 us -> 158 us (0.46)
  blocking collectives: 104 us -> 16 us
  waiting for transfers between devices: 149 us -> 75.9 us
  between operations: 14 us -> 1.23 us
  matrix products: 10.9 us -> 2.6 us
    all_to_all x5 -> x1, blocking collectives: 74 us -> 16 us  [exchanged(): return lax.all_to_all(x, axes, split_axis=0, concat_axis=0, tiled=True)]
    all_gather x3 -> x0, waiting for transfers between devices: 53.2 us -> none  [the longest x2 53.2 us: stacked_from(): tiles = lax.all_gather(tiles, axes[k])]
    all_gather x1 -> x0, blocking collectives: 30.3 us -> none  [stacked_from(): tiles = lax.all_gather(tiles, axes[k])]
    all_to_all x3 -> x5, waiting for transfers between devices: 95.5 us -> 75.9 us  [exchanged(): return lax.all_to_all(x, axes, split_axis=0, concat_axis=0, tiled=True)]
    dot_general x7 -> x10, matrix products: 10.6 us -> 2.6 us  [the longest x8 2.09 us: dot(): return jnp.dot(a, b, preferred_element_type=F32)]
    all_to_all x7 -> x0, local copies, waits for them, and re-layouts: 5.96 us -> none  [the longest x3 5.26 us: sent_to_all(): return lax.all_to_all(copies, axis, split_axis=0, concat_axis=0, tiled=True)]
    slice x0 -> x12, local copies, waits for them, and re-layouts: none -> 3.66 us  [the longest x2 1.63 us: pieces(): return [r[:, a:b].reshape(-1, w1) for a, b in zip(cut[:-1], cut[1:])]]
    all_to_all x3 -> x5, starting transfers between devices: 37.4 us -> 38.7 us  [exchanged(): return lax.all_to_all(x, axes, split_axis=0, concat_axis=0, tiled=True)]
  transfers between devices with their start and end apart: 6 -> 6, of which waited for: 4 -> 5; matrix products, arithmetic and copies ran while one was open for 6% -> 2% of each run, Pallas kernels for 0% -> 0%
where the time goes in v1:
time: 158 us; the launch traced here: 157 us
  waiting for transfers between devices  75.9 us (48%)
  starting transfers between devices  39.3 us (25%)
  local copies, waits for them, and re-layouts  17.2 us (11%)
  blocking collectives  16 us (10%)
  other arithmetic  4.4 us (3%)
  matrix products  2.6 us (2%)
    all_to_all x5, waiting for transfers between devices, exchanged(): return lax.all_to_all(x, axes, split_axis=0, concat_axis=0, tiled=True)  75.9 us
    all_to_all x5, starting transfers between devices, exchanged(): return lax.all_to_all(x, axes, split_axis=0, concat_axis=0, tiled=True)  38.7 us
    all_to_all x1, blocking collectives, exchanged(): return lax.all_to_all(x, axes, split_axis=0, concat_axis=0, tiled=True)  16 us
    unnamed x43, local copies, waits for them, and re-layouts  6.65 us
  transfers between devices with their start and end apart: 6, of which 5 were waited for; matrix products, arithmetic and copies ran while one was open for 2% of the time, Pallas kernels for 0%

profile of v1, /device:TPU:513, one launch (start us, length us, event | category | flops | bytes accessed | tf_op | source)
XLA Modules:
  0.0 156.6 jit_solution(7386782039488088731)
XLA Ops:
  0.7 0.7 copy-done.16
  1.4 0.2 fusion.13
  1.5 0.2 fusion.12
  1.7 0.7 dynamic-slice_convert_fusion.2
  2.8 0.8 copy-done.10
  3.6 0.1 reshape.298
  3.8 0.1 reshape.300
  3.9 0.6 copy-done.13
  4.5 0.7 pad_maximum_fusion.2
  5.2 23.9 %all-to-all-start.1 = ((bf16[16,32,128]{2,1,0:T(8,128)(2,1)}), bf16[16,32,128]{2,1,0:T(8,128)(2,1)S(1)}, u32[]{:S(2)}, u32[]{:S(2)}) async-start(bf16[16,32,128]{2,1,0:T(8,128)(2,1)} %pad_maximum_fusion.2), calls=%async_computation.1 | async-start | bytes 262144 | tf_op jit(solution)/shard_map/all_to_all | solution.py:17
  29.1 9.2 %all-to-all-done.1 = bf16[16,32,128]{2,1,0:T(8,128)(2,1)S(1)} async-done(((bf16[16,32,128]{2,1,0:T(8,128)(2,1)}), bf16[16,32,128]{2,1,0:T(8,128)(2,1)S(1)}, u32[]{:S(2)}, u32[]{:S(2)}) %all-to-all-start.1) | async-done | bytes 131104 | tf_op jit(solution)/shard_map/all_to_all | solution.py:17
  38.3 1.1 broadcast_in_dim.25
  39.4 3.8 %all-to-all-start = ((bf16[8,56,1024]{2,1,0:T(8,128)(2,1)}), bf16[8,56,1024]{2,1,0:T(8,128)(2,1)S(1)}, u32[]{:S(2)}, u32[]{:S(2)}) async-start(bf16[8,56,1024]{2,1,0:T(8,128)(2,1)} %broadcast_in_dim.25), calls=%async_computation | async-start | bytes 1835008 | tf_op jit(solution)/shard_map/all_to_all | solution.py:17
  43.1 26.2 %all-to-all-done = bf16[8,56,1024]{2,1,0:T(8,128)(2,1)S(1)} async-done(((bf16[8,56,1024]{2,1,0:T(8,128)(2,1)}), bf16[8,56,1024]{2,1,0:T(8,128)(2,1)S(1)}, u32[]{:S(2)}, u32[]{:S(2)}) %all-to-all-start) | async-done | bytes 917536 | tf_op jit(solution)/shard_map/all_to_all | solution.py:17
  69.3 0.9 broadcast_in_dim.28
  70.2 3.7 %all-to-all-start.2 = ((bf16[8,16,16,128]{3,2,1,0:T(8,128)(2,1)}), bf16[8,16,16,128]{3,2,1,0:T(8,128)(2,1)S(1)}, u32[]{:S(2)}, u32[]{:S(2)}) async-start(bf16[8,16,16,128]{3,2,1,0:T(8,128)(2,1)} %broadcast_in_dim.28), calls=%async_computation.2 | async-start | bytes 1048576 | tf_op jit(solution)/shard_map/all_to_all | solution.py:17
  73.9 0.7 collective-permute-start
  74.7 15.7 %all-to-all-done.2 = bf16[8,16,16,128]{3,2,1,0:T(8,128)(2,1)S(1)} async-done(((bf16[8,16,16,128]{3,2,1,0:T(8,128)(2,1)}), bf16[8,16,16,128]{3,2,1,0:T(8,128)(2,1)S(1)}, u32[]{:S(2)}, u32[]{:S(2)}) %all-to-all-start.2) | async-done | bytes 524320 | tf_op jit(solution)/shard_map/all_to_all | solution.py:17
  90.4 0.1 fusion.29
  90.5 0.2 reshape_reshape.12
  90.9 0.2 fusion.22
  91.1 0.2 select_bitcast_fusion.1
  91.4 0.9 broadcast_in_dim.29
  92.3 3.7 %all-to-all-start.3 = ((bf16[8,16,16,128]{3,2,1,0:T(8,128)(2,1)}), bf16[8,16,16,128]{3,2,1,0:T(8,128)(2,1)S(1)}, u32[]{:S(2)}, u32[]{:S(2)}) async-start(bf16[8,16,16,128]{3,2,1,0:T(8,128)(2,1)} %broadcast_in_dim.29), calls=%async_computation.3 | async-start | bytes 1048576 | tf_op jit(solution)/shard_map/all_to_all | solution.py:17
  96.0 0.2 fusion.6
  96.2 0.9 fusion.28
  97.0 0.2 select_bitcast_fusion.3
  97.3 0.9 copy-done.3
  98.2 0.8 fusion.27
  98.9 12.8 %all-to-all-done.3 = bf16[8,16,16,128]{3,2,1,0:T(8,128)(2,1)S(1)} async-done(((bf16[8,16,16,128]{3,2,1,0:T(8,128)(2,1)}), bf16[8,16,16,128]{3,2,1,0:T(8,128)(2,1)S(1)}, u32[]{:S(2)}, u32[]{:S(2)}) %all-to-all-start.3) | async-done | bytes 524320 | tf_op jit(solution)/shard_map/all_to_all | solution.py:17
  111.8 0.3 fusion.9
  112.1 0.6 copy-done.6
  112.7 0.3 fusion.25
  113.0 0.6 copy-done.7
  113.7 0.3 fusion.2
  114.0 0.6 copy-done.1
  114.6 0.3 broadcast_select_fusion.1
  115.0 0.3 fusion.36
  115.2 0.3 fusion
  115.5 0.7 copy-done
  116.2 0.1 copy.108
  116.3 0.1 copy.109
  116.5 0.9 slice-done.1
  117.4 0.2 copy.125
  117.6 0.7 slice-done
  118.3 0.2 copy.111
  118.5 0.2 copy.112
  118.7 0.1 reshape_reshape.15
  119.0 0.8 pad_maximum_fusion.1
  119.8 3.7 %all-to-all-start.4 = ((bf16[8,196,128]{2,1,0:T(8,128)(2,1)}), bf16[8,196,128]{2,1,0:T(8,128)(2,1)S(1)}, u32[]{:S(2)}, u32[]{:S(2)}) async-start(bf16[8,196,128]{2,1,0:T(8,128)(2,1)} %pad_maximum_fusion.1), calls=%async_computation.4 | async-start | bytes 819200 | tf_op jit(solution)/shard_map/all_to_all | solution.py:17
  123.5 0.1 reshape.316
  123.7 11.9 %all-to-all-done.4 = bf16[8,196,128]{2,1,0:T(8,128)(2,1)S(1)} async-done(((bf16[8,196,128]{2,1,0:T(8,128)(2,1)}), bf16[8,196,128]{2,1,0:T(8,128)(2,1)S(1)}, u32[]{:S(2)}, u32[]{:S(2)}) %all-to-all-start.4) | async-done | bytes 401440 | tf_op jit(solution)/shard_map/all_to_all | solution.py:17
  135.6 0.3 convert_reduce_fusion
  135.9 0.1 copy.130
  136.0 0.1 copy.119
  136.2 0.1 concatenate.19
  136.3 16.0 %all_to_all.30 = bf16[16,40,128]{2,1,0:T(8,128)(2,1)S(1)} all-to-all(bf16[16,40,128]{2,1,0:T(8,128)(2,1)S(1)} %concatenate.19), channel_id=1, replica_groups=mesh['parts'=2,'y'=8,'x'=8,'c'=2] {'x','c'}, dimensions={0} | all-to-all | bytes 327680 | tf_op jit(solution)/shard_map/all_to_all | solution.py:17
  152.4 0.1 reshape.328
  152.6 0.7 copy-done.9
  153.3 0.6 add_convert_fusion
  153.9 0.6 copy.143
  154.5 0.6 fusion.30
  155.3 0.7 reshape.319
  156.0 0.6 add.72
  (77 shorter events, 1.4 us)
Async XLA Ops:
  0.6 2.0 %copy-start.11 = (bf16[2,16,1024]{2,1,0:T(8,128)(2,1)S(1)}, bf16[2,16,1024]{2,1,0:T(8,128)(2,1)}, u32[]{:S(2)}) copy-start(bf16[2,16,1024]{2,1,0:T(8,128)(2,1)} %param.12) | copy-start | bytes 196612
  0.7 0.7 copy-start.16
  0.7 0.9 copy-start.15
  2.7 0.8 copy-start.10
  2.7 0.8 copy-start.12
  3.8 0.8 copy-start.13
  5.2 23.9 %copy-start.8 = (f32[8,1024]{1,0:T(8,128)S(1)}, f32[8,1024]{1,0:T(8,128)}, u32[]{:S(2)}) copy-start(f32[8,1024]{1,0:T(8,128)} %param.11) | copy-start | bytes 98308
  5.2 33.1 %all-to-all-start.1 = ((bf16[16,32,128]{2,1,0:T(8,128)(2,1)}), bf16[16,32,128]{2,1,0:T(8,128)(2,1)S(1)}, u32[]{:S(2)}, u32[]{:S(2)}) async-start(bf16[16,32,128]{2,1,0:T(8,128)(2,1)} %pad_maximum_fusion.2), calls=%async_computation.1 | async-start | bytes 262144 | tf_op jit(solution)/shard_map/all_to_all | solution.py:17
  38.3 53.1 %copy-start.2 = (bf16[16,32,128]{2,1,0:T(8,128)(2,1)}, bf16[16,32,128]{2,1,0:T(8,128)(2,1)S(1)}, u32[]{:S(2)}) copy-start(bf16[16,32,128]{2,1,0:T(8,128)(2,1)S(1)} %all-to-all-done.1) | copy-start | bytes 393220
  39.4 30.0 %all-to-all-start = ((bf16[8,56,1024]{2,1,0:T(8,128)(2,1)}), bf16[8,56,1024]{2,1,0:T(8,128)(2,1)S(1)}, u32[]{:S(2)}, u32[]{:S(2)}) async-start(bf16[8,56,1024]{2,1,0:T(8,128)(2,1)} %broadcast_in_dim.25), calls=%async_computation | async-start | bytes 1835008 | tf_op jit(solution)/shard_map/all_to_all | solution.py:17
  70.2 20.2 %all-to-all-start.2 = ((bf16[8,16,16,128]{3,2,1,0:T(8,128)(2,1)}), bf16[8,16,16,128]{3,2,1,0:T(8,128)(2,1)S(1)}, u32[]{:S(2)}, u32[]{:S(2)}) async-start(bf16[8,16,16,128]{3,2,1,0:T(8,128)(2,1)} %broadcast_in_dim.28), calls=%async_computation.2 | async-start | bytes 1048576 | tf_op jit(solution)/shard_map/all_to_all | solution.py:17
  73.9 17.2 %collective-permute-start = (bf16[8,56,1024]{2,1,0:T(8,128)(2,1)S(1)}, bf16[8,56,1024]{2,1,0:T(8,128)(2,1)S(1)}, u32[]{:S(2)}, u32[]{:S(2)}) collective-permute-start(bf16[8,56,1024]{2,1,0:T(8,128)(2,1)S(1)} %all-to-all-done), channel_id=1, source_target_pairs={{0,1},{1,0},{2,3},{3,2},{4,5},{5,4},{6,7},{7,6},{8,9},{9,8},{10,11... | collective-permute-start | bytes 2752520 | tf_op jit(solution)/shard_map/ppermute | solution.py:109
  92.3 19.5 %all-to-all-start.3 = ((bf16[8,16,16,128]{3,2,1,0:T(8,128)(2,1)}), bf16[8,16,16,128]{3,2,1,0:T(8,128)(2,1)S(1)}, u32[]{:S(2)}, u32[]{:S(2)}) async-start(bf16[8,16,16,128]{3,2,1,0:T(8,128)(2,1)} %broadcast_in_dim.29), calls=%async_computation.3 | async-start | bytes 1048576 | tf_op jit(solution)/shard_map/all_to_all | solution.py:17
  97.2 0.9 copy-start.3
  98.1 0.8 copy-start.4
  111.8 1.0 copy-start.6
  112.7 0.9 copy-start.7
  113.7 0.9 copy-start.1
  115.5 0.8 copy-start
  116.4 1.0 slice-start.1
  117.4 0.9 slice-start
  119.8 15.8 %all-to-all-start.4 = ((bf16[8,196,128]{2,1,0:T(8,128)(2,1)}), bf16[8,196,128]{2,1,0:T(8,128)(2,1)S(1)}, u32[]{:S(2)}, u32[]{:S(2)}) async-start(bf16[8,196,128]{2,1,0:T(8,128)(2,1)} %pad_maximum_fusion.1), calls=%async_computation.4 | async-start | bytes 819200 | tf_op jit(solution)/shard_map/all_to_all | solution.py:17
  123.6 12.2 %copy-start.5 = (f32[8,2,8,128]{3,2,1,0:T(8,128)S(1)}, f32[8,2,8,128]{3,2,1,0:T(8,128)}, u32[]{:S(2)}) copy-start(f32[8,2,8,128]{3,2,1,0:T(8,128)} %copy-done.4) | copy-start | bytes 196612
  152.5 0.8 copy-start.9
  155.3 0.7 copy-start.14

commit v2 on v1

v2 whole, which is shorter than its diff:
```python
import jax
import jax.numpy as jnp
from jax import lax
from jax.experimental import pallas as pl
from jax.experimental.pallas import tpu as pltpu
from jax.sharding import Mesh
from jax.sharding import PartitionSpec as P

BLK = 256
LANES = 128
HALF = LANES // 2
ROW = ("y", "x", "c")
PARTS_ROW = ("parts", "y", "x", "c")
XC = ("x", "c")
F32 = jnp.float32
BF16 = jnp.bfloat16
VMEM = pl.BlockSpec(memory_space=pltpu.VMEM)
SMEM = pl.BlockSpec(memory_space=pltpu.SMEM)


def exchanged(x, axes):
    return lax.all_to_all(x, axes, split_axis=0, concat_axis=0, tiled=True)


def sent_to_all(x, axes):
    return exchanged(jnp.broadcast_to(x, (lax.axis_size(axes), *x.shape)), axes)


def swapped(x, axis, bit):
    return lax.ppermute(x, axis, [(i, i ^ bit) for i in range(lax.axis_size(axis))])


def dot(a, b):
    return jnp.dot(a, b, preferred_element_type=F32)


def dot_t(a, b):
    return lax.dot_general(a, b, (((0,), (0,)), ((), ())), preferred_element_type=F32)


def turned(x):
    return pltpu.roll(x, HALF, x.ndim - 1)


def low_high(low, high):
    lane = lax.broadcasted_iota(jnp.int32, low.shape, low.ndim - 1)
    return jnp.where(lane < HALF, low, high)


def split3(v):
    parts = []
    for _ in range(3):
        top = v.astype(BF16).astype(F32)
        parts.append(top)
        v = v - top
    return parts


def call(kernel, outs, args, specs=None, scratch=()):
    return pl.pallas_call(
        kernel,
        out_shape=tuple(jax.ShapeDtypeStruct(s, d) for s, d in outs),
        in_specs=specs or [VMEM] * len(args),
        out_specs=tuple(VMEM for _ in outs),
        scratch_shapes=scratch,
        compiler_params=pltpu.CompilerParams(vmem_limit_bytes=48 * 2**20),
    )(*args)


def pack_kernel(
    sigma, par, dinv, kid_top, kid_par, mask_par, mask_kid_top, mask_kid_par, slots, own
):
    rt, w1 = par.shape
    rp = dinv.shape[0]
    kids = kid_top.shape[0]
    nj = slots.shape[0]
    position = lax.axis_index(ROW)
    block_top = lax.div(position * rt, BLK)
    block_par = lax.div(position * rp, BLK)
    own[0:rt, :] = sigma[:, 0:w1]
    own[rt : 2 * rt, :] = sigma[:, w1 : 2 * w1]
    own[2 * rt : 2 * rt + rp, :] = dinv[...].astype(BF16)

    packed = []
    for m in range(w1 // LANES):
        at = slice(m * LANES, (m + 1) * LANES)
        keep = mask_par[block_top, m * LANES // BLK].astype(F32)
        piece = par[:, at].astype(F32) * keep
        top, low = piece[:rp], piece[rp:]
        packed.append(low_high(top, turned(low)))
        packed.append(low_high(turned(top), low))
        piece = piece.astype(BF16)
        for j in range(nj):
            slots[j, 2 * rt + m * rt : 2 * rt + (m + 1) * rt, :] = piece
    per_kid = nj // kids
    for j in range(nj):
        k, m = divmod(j, per_kid)
        at = slice(m * LANES, (m + 1) * LANES)
        keep = mask_kid_par[k, block_par, m * LANES // BLK].astype(F32)
        piece = kid_par[k, :, at].astype(F32) * keep
        slots[j, 0 : 2 * rp, :] = jnp.concatenate([piece, packed[j]], axis=0).astype(BF16)
        keep = mask_kid_top[k, block_top, m * LANES // BLK].astype(F32)
        slots[j, rt : 2 * rt, :] = (kid_top[k, :, at].astype(F32) * keep).astype(BF16)


def kid_par_columns(tall):
    ny, nj, rows, _ = tall.shape
    rp = rows // 2
    return tall[:, :, 0:rp, :].astype(F32).reshape(ny * nj * rp, LANES).astype(BF16)


def par_block(cols, m, rt):
    nj = cols.shape[0]
    return cols[:, 2 * rt + m * rt : 2 * rt + (m + 1) * rt, :].reshape(nj * rt, LANES)


def step_kernel(rt, cols, tall, send, step):
    nj = cols.shape[0]
    kid_par_j = kid_par_columns(tall)
    total = cols[:, rt : 2 * rt, :].astype(F32).reshape(nj * rt, LANES)
    for m in range(kid_par_j.shape[0] // LANES):
        total = total + dot(par_block(cols, m, rt), kid_par_j[m * LANES : (m + 1) * LANES])
    total = total.reshape(nj, rt, LANES)
    step[...] = total
    rounded = total.astype(BF16)
    for y in range(send.shape[0]):
        send[y] = rounded


def main_kernel(rt, rp, near, far, tall, step_j, cols, step, slots, part, db, xs):
    w1 = near.shape[-1]
    ny, nj = tall.shape[:2]
    x_me, c_me = lax.axis_index("x"), lax.axis_index("c")
    kid_par_j = kid_par_columns(tall)
    par_j = tall[:, :, rp : 2 * rp, :].astype(F32).reshape(ny * nj, 1, rp, LANES)
    par_j = jnp.concatenate([par_j, turned(par_j)], axis=1)
    par_j = par_j.reshape(ny * nj * 2 * rp, LANES).astype(BF16)
    both = jnp.concatenate([step_j[...].reshape(ny * nj * rt, LANES), par_j], axis=1)

    for b1, chunks in enumerate((near, far)):
        chunk_count = chunks.shape[0]
        s0 = chunks[:, 0:rt, :].reshape(chunk_count * rt, w1)
        s1 = chunks[:, rt : 2 * rt, :].reshape(chunk_count * rt, w1)
        d = chunks[:, 2 * rt : 2 * rt + rp, :].astype(F32).reshape(chunk_count * rp, w1)
        x = dot(s0, both[:w1]) + dot(s1, both[w1:])
        db_own = dot(d.astype(BF16), kid_par_j)
        for k in range(chunk_count):
            bc, b2, b4 = k // 4, (k // 2) % 2, k % 2
            chip = jnp.bitwise_xor(x_me, b1 + 2 * b2 + 4 * b4)
            at = 2 * chip + jnp.bitwise_xor(c_me, bc)
            piece = x[k * rt : (k + 1) * rt]
            xs[at] = piece.astype(BF16)
            part[at, 0:rt, :] = piece[:, :LANES].astype(BF16)
            c = piece[:, LANES:]
            part[at, rt : rt + rp, :] = low_high(c[:rp], turned(c[rp:])).astype(BF16)
            db[at] = db_own[k * rp : (k + 1) * rp]

    x = xs[...].reshape(nj * rt, 2 * LANES)
    for y in range(ny):
        partial = dot_t(par_block(cols, y, rt), x)
        rows = partial.shape[0]
        slots[y, 0:rows, :] = partial[:, :LANES].astype(BF16)
        q = partial[:, LANES:]
        q = low_high(q[: rows // 2], turned(q[rows // 2 :]))
        slots[y, rows : rows + rows // 2, :] = q.astype(BF16)
    kt = x[:, :LANES].astype(F32)
    var = jnp.sum(step[...].reshape(nj * rt, LANES) * kt, axis=0, keepdims=True)
    kid_par_tile = cols[:, 0:rp, :].astype(F32)
    var = var + jnp.sum((kid_par_tile * db[...]).reshape(nj * rp, LANES), axis=0, keepdims=True)
    var_rows = jnp.concatenate(split3(var) + [jnp.zeros((5, LANES), F32)], axis=0).astype(BF16)
    for y in range(ny):
        slots[y, rows + rows // 2 : rows + rows // 2 + 8, :] = var_rows


def sum_kernel(rt, rp, received, db, part, out):
    ny = received.shape[0]
    nj = out.shape[0]
    rows = nj * rp
    total = received[0].astype(F32)
    for y in range(1, ny):
        total = total + received[y].astype(F32)
    q = total[rows : rows + rows // 2]
    q = jnp.concatenate([q, turned(q)], axis=0)
    first = rows + rows // 2
    var = total[first : first + 1] + total[first + 1 : first + 2] + total[first + 2 : first + 3]
    var_rows = []
    for top in split3(var):
        var_rows += [turned(top), top]
    var_rows = jnp.concatenate(var_rows + [jnp.zeros((2, LANES), F32)], axis=0)
    for j in range(nj):
        at = slice(j * rp, (j + 1) * rp)
        out[j, 0 : rt + rp, :] = part[j]
        kp = total[at] + db[j]
        out[j, rt + rp : rt + 3 * rp, :] = jnp.concatenate(
            [kp, low_high(q[at], var_rows)], axis=0
        ).astype(BF16)


def final_kernel(rt, rp, got, dinv, dvar, cross_par, sigma_par, kid_top, kid_par, variance):
    nj = got.shape[0]
    kids = dvar.shape[0]
    per_kid = nj // kids
    for j in range(nj):
        k, m = divmod(j, per_kid)
        at = slice(m * LANES, (m + 1) * LANES)
        kid_top[k, :, at] = got[j, 0:rt, :]
        kid_par[k, :, at] = got[j, rt + rp : rt + 2 * rp, :]
        v = got[j, rt + 2 * rp : rt + 3 * rp, :].astype(F32)
        low = v[0:1] + v[2:3] + v[4:5]
        high = v[1:2] + v[3:4] + v[5:6]
        variance[k : k + 1, at] = dvar[k : k + 1, at] + low_high(turned(low), high)
    for m in range(nj // 2):
        at = slice(m * LANES, (m + 1) * LANES)
        a = got[2 * m, rt : rt + rp, :].astype(F32)
        b = got[2 * m + 1, rt : rt + rp, :].astype(F32)
        cross_par[:, at] = jnp.concatenate(
            [low_high(a, turned(b)), low_high(turned(a), b)], axis=0
        ).astype(BF16)
        a = got[2 * m, rt + 2 * rp : rt + 3 * rp, :].astype(F32)
        b = got[2 * m + 1, rt + 2 * rp : rt + 3 * rp, :].astype(F32)
        sigma_par[:, at] = (dinv[:, at] + low_high(a, turned(b))).astype(BF16)


def device_part(
    sigma_top,
    panel_par,
    dinv_par,
    panel_kid_top,
    panel_kid_par,
    dvar_kid,
    mask_par,
    mask_kid_top,
    mask_kid_par,
):
    rt, wt = sigma_top.shape
    rp, w1 = dinv_par.shape
    kids, _, w2 = panel_kid_top.shape
    ny = lax.axis_size("y")
    nx = lax.axis_size("x")
    nj = lax.axis_size(XC)
    assert kids * w2 == nj * LANES and w1 == nj * HALF and wt == 2 * w1
    assert nx == 8 and rt == 2 * rp and nj * rp == LANES and ny * LANES == w1

    slots, own = call(
        pack_kernel,
        [((nj, 2 * rt + w1 // LANES * rt, LANES), BF16), ((2 * rt + rp, w1), BF16)],
        (
            sigma_top,
            panel_par,
            dinv_par,
            panel_kid_top,
            panel_kid_par,
            mask_par,
            mask_kid_top,
            mask_kid_par,
        ),
        [VMEM] * 5 + [SMEM] * 3,
    )
    cols = exchanged(slots, XC)
    two = jnp.stack([own, swapped(own, "x", 4)])
    tall = sent_to_all(cols[:, : 2 * rp], "y")
    four = jnp.concatenate([two, swapped(two, "x", 2)])
    near = jnp.concatenate([four, swapped(four, "c", 1)])
    far = swapped(near, "x", 1)

    def sized(kernel):
        return lambda *refs: kernel(rt, rp, *refs)

    send, step = call(
        lambda *refs: step_kernel(rt, *refs),
        [((ny, nj, rt, LANES), BF16), ((nj, rt, LANES), F32)],
        (cols, tall),
    )
    step_j = exchanged(send, "y")
    rows4 = nj * rp + nj * rp // 2 + 8
    slots4, part, db = call(
        sized(main_kernel),
        [((ny, rows4, LANES), BF16), ((nj, rt + rp, LANES), BF16), ((nj, rp, LANES), F32)],
        (near, far, tall, step_j, cols, step),
        scratch=[pltpu.VMEM((nj, rt, 2 * LANES), BF16)],
    )
    received = exchanged(slots4, "y")
    (out,) = call(
        sized(sum_kernel), [((nj, rt + 3 * rp, LANES), BF16)], (received, db, part)
    )
    got = exchanged(out, XC)
    return call(
        sized(final_kernel),
        [
            ((rt, w1), BF16),
            ((rp, w1), BF16),
            ((kids, rt, w2), BF16),
            ((kids, rp, w2), BF16),
            ((kids, w2), F32),
        ],
        (got, dinv_par, dvar_kid),
    )


def solution(mesh):
    finer = Mesh(mesh.devices.reshape(mesh.shape["parts"], 8, 8, 2), PARTS_ROW)
    return jax.shard_map(
        device_part,
        mesh=finer,
        in_specs=(
            P(PARTS_ROW, None),
            P(PARTS_ROW, None),
            P(PARTS_ROW, None),
            P("parts", ROW, None),
            P("parts", ROW, None),
            P("parts", None),
            P("parts", None),
            P("parts", None, None),
            P("parts", None, None),
        ),
        out_specs=(
            P(PARTS_ROW, None),
            P(PARTS_ROW, None),
            P("parts", ROW, None),
            P("parts", ROW, None),
            P("parts", None),
        ),
        check_vma=False,
    )
```

time: 158 us -> 136 us (0.86)
  blocking collectives: 16 us -> 76.1 us
  waiting for transfers between devices: 75.9 us -> 36.3 us
  starting transfers between devices: 39.3 us -> 12 us
  local copies, waits for them, and re-layouts: 17.2 us -> 6.29 us
  other arithmetic: 4.4 us -> 0.12 us
  Pallas kernels: 0 us -> 3.77 us
  matrix products: 2.6 us -> 0 us
    all_to_all x5 -> x2, waiting for transfers between devices: 75.9 us -> 1.85 us  [exchanged(): return lax.all_to_all(x, axes, split_axis=0, concat_axis=0, tiled=True)]
    all_to_all x1 -> x3, blocking collectives: 16 us -> 76.1 us  [exchanged(): return lax.all_to_all(x, axes, split_axis=0, concat_axis=0, tiled=True)]
    ppermute x1 -> x4, waiting for transfers between devices: 0.01 us -> 34.4 us  [swapped(): lax.ppermute(x, axis, [(i, i ^ bit) for i in range(lax.axis_size(axis))])]
    all_to_all x5 -> x2, starting transfers between devices: 38.7 us -> 10.1 us  [exchanged(): return lax.all_to_all(x, axes, split_axis=0, concat_axis=0, tiled=True)]
    pallas_call x0 -> x5, Pallas kernels: none -> 3.77 us  [call(): pl.pallas_call(kernel, out_shape=tuple((jax.ShapeDtypeStruct(s, d) for s,...]
    slice x12 -> x1, local copies, waits for them, and re-layouts: 3.66 us -> 0.01 us  [device_part(): tall = sent_to_all(cols[:, :2 * rp], 'y')]
    dot_general x10 -> x0, matrix products: 2.6 us -> none  [the longest x8 2.09 us: dot(): return jnp.dot(a, b, preferred_element_type=F32)]
    reshape x10 -> x0, local copies, waits for them, and re-layouts: 2.01 us -> none  [the longest x1 0.73 us: shards(): cross_par = halves_below(cr).transpose(1, 0, 2).reshape(rt, w1)]
  transfers between devices with their start and end apart: 6 -> 6, of which waited for: 5 -> 4; matrix products, arithmetic and copies ran while one was open for 2% -> 0% of each run, Pallas kernels for 0% -> 1%
where the time goes in v2:
time: 136 us; the launch traced here: 135 us
  blocking collectives  76.1 us (56%)
  waiting for transfers between devices  36.3 us (27%)
  starting transfers between devices  12 us (9%)
  local copies, waits for them, and re-layouts  6.29 us (5%)
  Pallas kernels  3.77 us (3%)
    all_to_all x3, blocking collectives, exchanged(): return lax.all_to_all(x, axes, split_axis=0, concat_axis=0, tiled=True)  76.1 us
    ppermute x4, waiting for transfers between devices, swapped(): lax.ppermute(x, axis, [(i, i ^ bit) for i in range(lax.axis_size(axis))])  34.4 us
    all_to_all x2, starting transfers between devices, exchanged(): return lax.all_to_all(x, axes, split_axis=0, concat_axis=0, tiled=True)  10.1 us
    unnamed x20, local copies, waits for them, and re-layouts  5.42 us
    pallas_call x5, Pallas kernels, call(): pl.pallas_call(kernel, out_shape=tuple((jax.ShapeDtypeStruct(s, d) for s,...  3.77 us
  transfers between devices with their start and end apart: 6, of which 4 were waited for; matrix products, arithmetic and copies ran while one was open for 0% of the time, Pallas kernels for 1%

profile of v2, /device:TPU:513, one launch (start us, length us, event | category | flops | bytes accessed | tf_op | source)
XLA Modules:
  0.0 135.2 jit_solution(8717220757306923000)
XLA Ops:
  0.6 0.0 copy-start.8
  0.6 0.8 copy.14.mask_par
  1.4 0.0 copy-done.8
  1.4 0.0 copy-start.7
  1.4 0.1 copy.15.mask_kid_top
  1.5 0.6 copy-done.7
  2.1 0.0 copy-start
  2.1 0.8 copy-done
  2.9 0.0 copy-start.2
  2.9 0.8 copy-done.2
  3.7 0.0 copy-start.3
  3.7 0.8 copy-done.3
  4.5 0.0 copy-start.4
  4.5 0.8 copy-done.4
  5.3 0.0 copy-start.5
  5.3 0.8 copy-done.5
  6.0 0.9 shard_map.128
  7.0 43.4 %all_to_all.25.refs_0_.refs_4_ = bf16[16,160,128]{2,1,0:T(8,128)(2,1)S(1)} all-to-all(bf16[16,160,128]{2,1,0:T(8,128)(2,1)S(1)} %get-tuple-element.13), channel_id=1, replica_groups=mesh['parts'=2,'y'=8,'x'=8,'c'=2] {'x','c'}, dimensions={0} | all-to-all | bytes 1310720 | tf_op jit(solution)/shard_map/all_to_all | solution.py:22
  50.3 0.9 broadcast_in_dim.3
  51.2 3.7 %all-to-all-start.1 = ((bf16[8,16,16,128]{3,2,1,0:T(8,128)(2,1)}), bf16[8,16,16,128]{3,2,1,0:T(8,128)(2,1)S(1)}, u32[]{:S(2)}, u32[]{:S(2)}) async-start(bf16[8,16,16,128]{3,2,1,0:T(8,128)(2,1)} %broadcast_in_dim.3), calls=%async_computation.1 | async-start | bytes 1048576 | tf_op jit(solution)/shard_map/all_to_all | solution.py:22
  54.9 0.7 collective-permute-start
  55.6 8.2 %collective-permute-done = bf16[40,1024]{1,0:T(8,128)(2,1)S(1)} collective-permute-done((bf16[40,1024]{1,0:T(8,128)(2,1)S(1)}, bf16[40,1024]{1,0:T(8,128)(2,1)S(1)}, u32[]{:S(2)}, u32[]{:S(2)}) %collective-permute-start) | collective-permute-done | bytes 81952 | tf_op jit(solution)/shard_map/ppermute | solution.py:30
  63.8 0.1 collective-permute-start.1
  64.0 10.3 %collective-permute-done.1 = bf16[2,40,1024]{2,1,0:T(8,128)(2,1)S(1)} collective-permute-done((bf16[2,40,1024]{2,1,0:T(8,128)(2,1)S(1)}, bf16[2,40,1024]{2,1,0:T(8,128)(2,1)S(1)}, u32[]{:S(2)}, u32[]{:S(2)}) %collective-permute-start.1) | collective-permute-done | bytes 163872 | tf_op jit(solution)/shard_map/ppermute | solution.py:30
  74.3 0.8 collective-permute-start.2
  75.1 0.0 all-to-all-done.1.refs_1_.refs_2_
  75.1 1.1 shard_map.129
  76.2 6.4 %all-to-all-start.2 = ((bf16[8,16,16,128]{3,2,1,0:T(8,128)(2,1)}), bf16[8,16,16,128]{3,2,1,0:T(8,128)(2,1)S(1)}, u32[]{:S(2)}, u32[]{:S(2)}) async-start(bf16[8,16,16,128]{3,2,1,0:T(8,128)(2,1)} %get-tuple-element.14), calls=%async_computation.2 | async-start | bytes 1048576 | tf_op jit(solution)/shard_map/all_to_all | solution.py:22
  82.7 0.0 collective-permute-done.2
  82.7 0.1 pad_maximum_fusion.refs_0_
  82.7 0.1 collective-permute-start.3
  82.9 15.9 %collective-permute-done.3.refs_1_ = bf16[8,40,1024]{2,1,0:T(8,128)(2,1)S(1)} collective-permute-done((bf16[8,40,1024]{2,1,0:T(8,128)(2,1)S(1)}, bf16[8,40,1024]{2,1,0:T(8,128)(2,1)S(1)}, u32[]{:S(2)}, u32[]{:S(2)}) %collective-permute-start.3) | collective-permute-done | bytes 655392 | tf_op jit(solution)/shard_map/ppermute | solution.py:30
  98.8 1.8 %all-to-all-done.2.refs_3_ = bf16[8,16,16,128]{3,2,1,0:T(8,128)(2,1)S(1)} async-done(((bf16[8,16,16,128]{3,2,1,0:T(8,128)(2,1)}), bf16[8,16,16,128]{3,2,1,0:T(8,128)(2,1)S(1)}, u32[]{:S(2)}, u32[]{:S(2)}) %all-to-all-start.2) | async-done | bytes 524320 | tf_op jit(solution)/shard_map/all_to_all | solution.py:22
  100.7 0.9 shard_map.130
  101.6 17.3 %all_to_all.26.refs_0_ = bf16[8,200,128]{2,1,0:T(8,128)(2,1)S(1)} all-to-all(bf16[8,200,128]{2,1,0:T(8,128)(2,1)S(1)} %get-tuple-element.16), channel_id=1, replica_groups=mesh['parts'=2,'y'=8,'x'=8,'c'=2] {'y'}, dimensions={0} | all-to-all | bytes 819200 | tf_op jit(solution)/shard_map/all_to_all | solution.py:22
  118.9 0.1 shard_map.131
  119.0 0.0 copy-start.1
  119.0 0.0 copy-start.6
  119.0 15.5 %all_to_all.27.refs_0_ = bf16[16,40,128]{2,1,0:T(8,128)(2,1)S(1)} all-to-all(bf16[16,40,128]{2,1,0:T(8,128)(2,1)S(1)} %shard_map.131), channel_id=1, replica_groups=mesh['parts'=2,'y'=8,'x'=8,'c'=2] {'x','c'}, dimensions={0} | all-to-all | bytes 327680 | tf_op jit(solution)/shard_map/all_to_all | solution.py:22
  134.5 0.0 copy-done.1
  134.5 0.0 copy-done.6
  134.5 0.7 shard_map.132
  (3 shorter events, 0.1 us)
Async XLA Ops:
  0.6 0.8 copy-start.8
  1.4 0.7 copy-start.7
  2.1 0.8 copy-start
  2.9 0.8 copy-start.2
  3.7 0.8 copy-start.3
  4.5 0.8 copy-start.4
  5.3 0.8 copy-start.5
  51.2 23.9 %all-to-all-start.1 = ((bf16[8,16,16,128]{3,2,1,0:T(8,128)(2,1)}), bf16[8,16,16,128]{3,2,1,0:T(8,128)(2,1)S(1)}, u32[]{:S(2)}, u32[]{:S(2)}) async-start(bf16[8,16,16,128]{3,2,1,0:T(8,128)(2,1)} %broadcast_in_dim.3), calls=%async_computation.1 | async-start | bytes 1048576 | tf_op jit(solution)/shard_map/all_to_all | solution.py:22
  54.9 8.9 %collective-permute-start = (bf16[40,1024]{1,0:T(8,128)(2,1)S(1)}, bf16[40,1024]{1,0:T(8,128)(2,1)S(1)}, u32[]{:S(2)}, u32[]{:S(2)}) collective-permute-start(bf16[40,1024]{1,0:T(8,128)(2,1)S(1)} %get-tuple-element.12), channel_id=1, source_target_pairs={{0,8},{2,10},{4,12},{6,14},{8,0},{10,2},{12,4},{14,6},{1,9},{3,11}... | collective-permute-start | bytes 245768 | tf_op jit(solution)/shard_map/ppermute | solution.py:30
  63.8 10.4 %collective-permute-start.1 = (bf16[2,40,1024]{2,1,0:T(8,128)(2,1)S(1)}, bf16[2,40,1024]{2,1,0:T(8,128)(2,1)S(1)}, u32[]{:S(2)}, u32[]{:S(2)}) collective-permute-start(bf16[2,40,1024]{2,1,0:T(8,128)(2,1)S(1)} %pad_maximum_fusion.2), channel_id=1, source_target_pairs={{0,4},{2,6},{4,0},{6,2},{8,12},{10,14},{12,8},{14,10},{1,5},{3,7},... | collective-permute-start | bytes 491528 | tf_op jit(solution)/shard_map/ppermute | solution.py:30
  74.3 8.4 %collective-permute-start.2 = (bf16[4,40,1024]{2,1,0:T(8,128)(2,1)S(1)}, bf16[4,40,1024]{2,1,0:T(8,128)(2,1)S(1)}, u32[]{:S(2)}, u32[]{:S(2)}) collective-permute-start(bf16[4,40,1024]{2,1,0:T(8,128)(2,1)S(1)} %pad_maximum_fusion.1), channel_id=1, source_target_pairs={{0,1},{1,0},{2,3},{3,2},{4,5},{5,4},{6,7},{7,6},{8,9},{9,8},{10,11... | collective-permute-start | bytes 983048 | tf_op jit(solution)/shard_map/ppermute | solution.py:30
  76.2 24.5 %all-to-all-start.2 = ((bf16[8,16,16,128]{3,2,1,0:T(8,128)(2,1)}), bf16[8,16,16,128]{3,2,1,0:T(8,128)(2,1)S(1)}, u32[]{:S(2)}, u32[]{:S(2)}) async-start(bf16[8,16,16,128]{3,2,1,0:T(8,128)(2,1)} %get-tuple-element.14), calls=%async_computation.2 | async-start | bytes 1048576 | tf_op jit(solution)/shard_map/all_to_all | solution.py:22
  82.7 16.1 %collective-permute-start.3 = (bf16[8,40,1024]{2,1,0:T(8,128)(2,1)S(1)}, bf16[8,40,1024]{2,1,0:T(8,128)(2,1)S(1)}, u32[]{:S(2)}, u32[]{:S(2)}) collective-permute-start(bf16[8,40,1024]{2,1,0:T(8,128)(2,1)S(1)} %pad_maximum_fusion.refs_0_), channel_id=1, source_target_pairs={{0,2},{2,0},{4,6},{6,4},{8,10},{10,8},{12,14},{14,12},{1,3},{3,1},... | collective-permute-start | bytes 1966088 | tf_op jit(solution)/shard_map/ppermute | solution.py:30
  119.0 15.5 %copy-start.1 = (f32[8,1024]{1,0:T(8,128)S(1)}, f32[8,1024]{1,0:T(8,128)}, u32[]{:S(2)}) copy-start(f32[8,1024]{1,0:T(8,128)} %refs_1_.1) | copy-start | bytes 98308
  119.0 15.5 %copy-start.6 = (f32[2,1024]{1,0:T(2,128)S(1)}, f32[2,1024]{1,0:T(2,128)}, u32[]{:S(2)}) copy-start(f32[2,1024]{1,0:T(2,128)} %refs_2_.1) | copy-start | bytes 24580

commit v3 on v2

--- a/solution.py
+++ b/solution.py
@@ -67,9 +67,15 @@
     )(*args)
 
 
-def pack_kernel(
-    sigma, par, dinv, kid_top, kid_par, mask_par, mask_kid_top, mask_kid_par, slots, own
-):
+def pack_kernel(*refs):
+    sources, (slots, own), scratch, done = refs[:8], refs[8:10], refs[10:18], refs[18]
+    pairs = enumerate(zip(sources, scratch))
+    copies = [pltpu.make_async_copy(a, b, done.at[i]) for i, (a, b) in pairs]
+    for copy in copies:
+        copy.start()
+    for copy in copies:
+        copy.wait()
+    sigma, par, dinv, kid_top, kid_par, mask_par, mask_kid_top, mask_kid_par = scratch
     rt, w1 = par.shape
     rp = dinv.shape[0]
     kids = kid_top.shape[0]
@@ -77,30 +83,36 @@
     position = lax.axis_index(ROW)
     block_top = lax.div(position * rt, BLK)
     block_par = lax.div(position * rp, BLK)
-    own[0:rt, :] = sigma[:, 0:w1]
-    own[rt : 2 * rt, :] = sigma[:, w1 : 2 * w1]
-    own[2 * rt : 2 * rt + rp, :] = dinv[...].astype(BF16)
-
+    own[rt : 2 * rt, :] = sigma[:, 0:w1]
+    own[2 * rt : 3 * rt, :] = sigma[:, w1 : 2 * w1]
+    own[3 * rt : 3 * rt + rp, :] = dinv[...].astype(BF16)
+
+    def top_row(mask):
+        lane = lax.broadcasted_iota(jnp.int32, mask.shape, 1)
+        return jnp.sum(jnp.where(lane == block_top, mask, 0).astype(F32), axis=1, keepdims=True)
+
+    keep = top_row(mask_par[...])
     packed = []
     for m in range(w1 // LANES):
         at = slice(m * LANES, (m + 1) * LANES)
-        keep = mask_par[block_top, m * LANES // BLK].astype(F32)
-        piece = par[:, at].astype(F32) * keep
+        block = m * LANES // BLK
+        piece = par[:, at].astype(F32) * keep[block : block + 1]
         top, low = piece[:rp], piece[rp:]
         packed.append(low_high(top, turned(low)))
         packed.append(low_high(turned(top), low))
-        piece = piece.astype(BF16)
-        for j in range(nj):
-            slots[j, 2 * rt + m * rt : 2 * rt + (m + 1) * rt, :] = piece
+        own[0:rt, at] = piece.astype(BF16)
     per_kid = nj // kids
-    for j in range(nj):
-        k, m = divmod(j, per_kid)
-        at = slice(m * LANES, (m + 1) * LANES)
-        keep = mask_kid_par[k, block_par, m * LANES // BLK].astype(F32)
-        piece = kid_par[k, :, at].astype(F32) * keep
-        slots[j, 0 : 2 * rp, :] = jnp.concatenate([piece, packed[j]], axis=0).astype(BF16)
-        keep = mask_kid_top[k, block_top, m * LANES // BLK].astype(F32)
-        slots[j, rt : 2 * rt, :] = (kid_top[k, :, at].astype(F32) * keep).astype(BF16)
+    for k in range(kids):
+        keep_top = top_row(mask_kid_top[k])
+        keep_par = mask_kid_par[k, pl.ds(block_par, 1), :].astype(F32)
+        for m in range(per_kid):
+            j = k * per_kid + m
+            at = slice(m * LANES, (m + 1) * LANES)
+            block = m * LANES // BLK
+            piece = kid_par[k, :, at].astype(F32) * keep_par[:, block : block + 1]
+            slots[j, 0 : 2 * rp, :] = jnp.concatenate([piece, packed[j]], axis=0).astype(BF16)
+            piece = kid_top[k, :, at].astype(F32) * keep_top[block : block + 1]
+            slots[j, 2 * rp : 2 * rp + rt, :] = piece.astype(BF16)
 
 
 def kid_par_columns(tall):
@@ -109,25 +121,29 @@
     return tall[:, :, 0:rp, :].astype(F32).reshape(ny * nj * rp, LANES).astype(BF16)
 
 
-def par_block(cols, m, rt):
-    nj = cols.shape[0]
-    return cols[:, 2 * rt + m * rt : 2 * rt + (m + 1) * rt, :].reshape(nj * rt, LANES)
-
-
-def step_kernel(rt, cols, tall, send, step):
-    nj = cols.shape[0]
+def chunk_place(x_me, c_me, bits):
+    b1, b2, b4, bc = bits
+    return 2 * jnp.bitwise_xor(x_me, b1 + 2 * b2 + 4 * b4) + jnp.bitwise_xor(c_me, bc)
+
+
+def step_kernel(rt, rp, cols, tall, par_own, par_other, send, step):
+    x_me, c_me = lax.axis_index("x"), lax.axis_index("c")
     kid_par_j = kid_par_columns(tall)
-    total = cols[:, rt : 2 * rt, :].astype(F32).reshape(nj * rt, LANES)
-    for m in range(kid_par_j.shape[0] // LANES):
-        total = total + dot(par_block(cols, m, rt), kid_par_j[m * LANES : (m + 1) * LANES])
-    total = total.reshape(nj, rt, LANES)
-    step[...] = total
-    rounded = total.astype(BF16)
-    for y in range(send.shape[0]):
-        send[y] = rounded
-
-
-def main_kernel(rt, rp, near, far, tall, step_j, cols, step, slots, part, db, xs):
+    for bc, par in enumerate((par_own, par_other)):
+        count, _, w1 = par.shape
+        product = dot(par[...].reshape(count * rt, w1), kid_par_j)
+        for k in range(count):
+            at = chunk_place(x_me, c_me, (k // 4, (k // 2) % 2, k % 2, bc))
+            total = cols[at, 2 * rp : 2 * rp + rt, :].astype(F32) + product[k * rt : (k + 1) * rt]
+            step[at] = total
+            rounded = total.astype(BF16)
+            for y in range(send.shape[0]):
+                send[y, at] = rounded
+
+
+def main_kernel(
+    rt, rp, near, far, par_own, par_other, tall, step_j, cols, step, slots, part, db
+):
     w1 = near.shape[-1]
     ny, nj = tall.shape[:2]
     x_me, c_me = lax.axis_index("x"), lax.axis_index("c")
@@ -137,36 +153,39 @@
     par_j = par_j.reshape(ny * nj * 2 * rp, LANES).astype(BF16)
     both = jnp.concatenate([step_j[...].reshape(ny * nj * rt, LANES), par_j], axis=1)
 
+    var = jnp.zeros((1, LANES), F32)
+    xs, ps = [], []
     for b1, chunks in enumerate((near, far)):
-        chunk_count = chunks.shape[0]
-        s0 = chunks[:, 0:rt, :].reshape(chunk_count * rt, w1)
-        s1 = chunks[:, rt : 2 * rt, :].reshape(chunk_count * rt, w1)
-        d = chunks[:, 2 * rt : 2 * rt + rp, :].astype(F32).reshape(chunk_count * rp, w1)
+        count = chunks.shape[0]
+        s0 = chunks[:, 0:rt, :].reshape(count * rt, w1)
+        s1 = chunks[:, rt : 2 * rt, :].reshape(count * rt, w1)
+        d = chunks[:, 2 * rt : 2 * rt + rp, :].astype(F32).reshape(count * rp, w1)
         x = dot(s0, both[:w1]) + dot(s1, both[w1:])
         db_own = dot(d.astype(BF16), kid_par_j)
-        for k in range(chunk_count):
-            bc, b2, b4 = k // 4, (k // 2) % 2, k % 2
-            chip = jnp.bitwise_xor(x_me, b1 + 2 * b2 + 4 * b4)
-            at = 2 * chip + jnp.bitwise_xor(c_me, bc)
+        for k in range(count):
+            at = chunk_place(x_me, c_me, (b1, (k // 2) % 2, k % 2, k // 4))
             piece = x[k * rt : (k + 1) * rt]
-            xs[at] = piece.astype(BF16)
-            part[at, 0:rt, :] = piece[:, :LANES].astype(BF16)
+            kt = piece[:, :LANES].astype(BF16)
+            part[at, 0:rt, :] = kt
             c = piece[:, LANES:]
             part[at, rt : rt + rp, :] = low_high(c[:rp], turned(c[rp:])).astype(BF16)
-            db[at] = db_own[k * rp : (k + 1) * rp]
-
-    x = xs[...].reshape(nj * rt, 2 * LANES)
+            db_k = db_own[k * rp : (k + 1) * rp]
+            db[at] = db_k
+            var = var + jnp.sum(step[at] * kt.astype(F32), axis=0, keepdims=True)
+            var = var + jnp.sum(cols[at, 0:rp, :].astype(F32) * db_k, axis=0, keepdims=True)
+        xs.append(x.astype(BF16))
+        for par in (par_own, par_other):
+            ps.append(par[4 * b1 : 4 * b1 + 4].reshape(4 * rt, w1))
+
+    x = jnp.concatenate(xs, axis=0)
+    p = jnp.concatenate(ps, axis=0)
     for y in range(ny):
-        partial = dot_t(par_block(cols, y, rt), x)
+        partial = dot_t(p[:, y * LANES : (y + 1) * LANES], x)
         rows = partial.shape[0]
         slots[y, 0:rows, :] = partial[:, :LANES].astype(BF16)
         q = partial[:, LANES:]
         q = low_high(q[: rows // 2], turned(q[rows // 2 :]))
         slots[y, rows : rows + rows // 2, :] = q.astype(BF16)
-    kt = x[:, :LANES].astype(F32)
-    var = jnp.sum(step[...].reshape(nj * rt, LANES) * kt, axis=0, keepdims=True)
-    kid_par_tile = cols[:, 0:rp, :].astype(F32)
-    var = var + jnp.sum((kid_par_tile * db[...]).reshape(nj * rp, LANES), axis=0, keepdims=True)
     var_rows = jnp.concatenate(split3(var) + [jnp.zeros((5, LANES), F32)], axis=0).astype(BF16)
     for y in range(ny):
         slots[y, rows + rows // 2 : rows + rows // 2 + 8, :] = var_rows
@@ -241,25 +260,33 @@
     assert kids * w2 == nj * LANES and w1 == nj * HALF and wt == 2 * w1
     assert nx == 8 and rt == 2 * rp and nj * rp == LANES and ny * LANES == w1
 
+    arrays = (
+        sigma_top,
+        panel_par,
+        dinv_par,
+        panel_kid_top,
+        panel_kid_par,
+        mask_par.T,
+        mask_kid_top.transpose(0, 2, 1),
+        mask_kid_par,
+    )
     slots, own = call(
         pack_kernel,
-        [((nj, 2 * rt + w1 // LANES * rt, LANES), BF16), ((2 * rt + rp, w1), BF16)],
-        (
-            sigma_top,
-            panel_par,
-            dinv_par,
-            panel_kid_top,
-            panel_kid_par,
-            mask_par,
-            mask_kid_top,
-            mask_kid_par,
-        ),
-        [VMEM] * 5 + [SMEM] * 3,
-    )
+        [((nj, 2 * rp + rt, LANES), BF16), ((3 * rt + rp, w1), BF16)],
+        tuple(pltpu.with_memory_space_constraint(a, pltpu.HBM) for a in arrays),
+        [pl.BlockSpec(memory_space=pltpu.HBM)] * len(arrays),
+        [pltpu.VMEM(a.shape, a.dtype) for a in arrays]
+        + [pltpu.SemaphoreType.DMA((len(arrays),))],
+    )
+    own_4 = swapped(own, "x", 4)
     cols = exchanged(slots, XC)
-    two = jnp.stack([own, swapped(own, "x", 4)])
+    two = jnp.stack([own, own_4])
     tall = sent_to_all(cols[:, : 2 * rp], "y")
-    four = jnp.concatenate([two, swapped(two, "x", 2)])
+    two_2 = swapped(two, "x", 2)
+    par_four = jnp.concatenate([two[:, :rt], two_2[:, :rt]])
+    four = jnp.concatenate([two[:, rt:], two_2[:, rt:]])
+    par_own = jnp.concatenate([par_four, swapped(par_four, "x", 1)])
+    par_other = swapped(par_own, "c", 1)
     near = jnp.concatenate([four, swapped(four, "c", 1)])
     far = swapped(near, "x", 1)
 
@@ -267,17 +294,16 @@
         return lambda *refs: kernel(rt, rp, *refs)
 
     send, step = call(
-        lambda *refs: step_kernel(rt, *refs),
+        sized(step_kernel),
         [((ny, nj, rt, LANES), BF16), ((nj, rt, LANES), F32)],
-        (cols, tall),
+        (cols, tall, par_own, par_other),
     )
     step_j = exchanged(send, "y")
     rows4 = nj * rp + nj * rp // 2 + 8
     slots4, part, db = call(
         sized(main_kernel),
         [((ny, rows4, LANES), BF16), ((nj, rt + rp, LANES), BF16), ((nj, rp, LANES), F32)],
-        (near, far, tall, step_j, cols, step),
-        scratch=[pltpu.VMEM((nj, rt, 2 * LANES), BF16)],
+        (near, far, par_own, par_other, tall, step_j, cols, step),
     )
     received = exchanged(slots4, "y")
     (out,) = call(

time: 136 us -> 121 us (0.89)
  blocking collectives: 76.1 us -> 32.4 us
  starting transfers between devices: 12 us -> 42.3 us
  local copies, waits for them, and re-layouts: 6.29 us -> 0.9 us
  waiting for transfers between devices: 36.3 us -> 39.5 us
    all_to_all x3 -> x2, blocking collectives: 76.1 us -> 32.4 us  [exchanged(): return lax.all_to_all(x, axes, split_axis=0, concat_axis=0, tiled=True)]
    all_to_all x2 -> x3, starting transfers between devices: 10.1 us -> 34.1 us  [exchanged(): return lax.all_to_all(x, axes, split_axis=0, concat_axis=0, tiled=True)]
    ppermute x4 -> x6, starting transfers between devices: 1.83 us -> 8.28 us  [swapped(): lax.ppermute(x, axis, [(i, i ^ bit) for i in range(lax.axis_size(axis))])]
    unnamed x20 -> x4, local copies, waits for them, and re-layouts: 5.42 us -> 0.01 us
    all_to_all x2 -> x3, waiting for transfers between devices: 1.85 us -> 6.18 us  [exchanged(): return lax.all_to_all(x, axes, split_axis=0, concat_axis=0, tiled=True)]
    ppermute x4 -> x6, waiting for transfers between devices: 34.4 us -> 33.3 us  [swapped(): lax.ppermute(x, axis, [(i, i ^ bit) for i in range(lax.axis_size(axis))])]
  transfers between devices with their start and end apart: 6 -> 9, of which waited for: 4 -> 7; matrix products, arithmetic and copies ran while one was open for 0% -> 1% of each run, Pallas kernels for 1% -> 1%
where the time goes in v3:
time: 121 us
  starting transfers between devices  42.3 us (35%)
  waiting for transfers between devices  39.5 us (33%)
  blocking collectives  32.4 us (27%)
  Pallas kernels  4.65 us (4%)
    all_to_all x3, starting transfers between devices, exchanged(): return lax.all_to_all(x, axes, split_axis=0, concat_axis=0, tiled=True)  34.1 us
    ppermute x6, waiting for transfers between devices, swapped(): lax.ppermute(x, axis, [(i, i ^ bit) for i in range(lax.axis_size(axis))])  33.3 us
    all_to_all x2, blocking collectives, exchanged(): return lax.all_to_all(x, axes, split_axis=0, concat_axis=0, tiled=True)  32.4 us
    ppermute x6, starting transfers between devices, swapped(): lax.ppermute(x, axis, [(i, i ^ bit) for i in range(lax.axis_size(axis))])  8.28 us
    all_to_all x3, waiting for transfers between devices, exchanged(): return lax.all_to_all(x, axes, split_axis=0, concat_axis=0, tiled=True)  6.18 us
    pallas_call x5, Pallas kernels, call(): pl.pallas_call(kernel, out_shape=tuple((jax.ShapeDtypeStruct(s, d) for s,...  4.65 us
  transfers between devices with their start and end apart: 9, of which 7 were waited for; matrix products, arithmetic and copies ran while one was open for 1% of the time, Pallas kernels for 1%

profile of v3, /device:TPU:513, one launch (start us, length us, event | category | flops | bytes accessed | tf_op | source)
XLA Modules:
  0.0 120.7 jit_solution(8013612409419567177)
XLA Ops:
  0.6 1.8 %shard_map.128 = (bf16[16,32,128]{2,1,0:T(8,128)(2,1)}, bf16[56,1024]{1,0:T(8,128)(2,1)S(1)}) custom-call(bf16[16,2048]{1,0:T(8,128)(2,1)} %refs_0_.1, bf16[16,1024]{1,0:T(8,128)(2,1)} %refs_1_.2, f32[8,1024]{1,0:T(8,128)} %refs_1_.3, bf16[2,16,1024]{2,1,0:T(8,128)(2,1)} %refs_3_.1, bf16[2,8,1024]{2,1,0:T(8,128)(2,1)} %refs_4_.1, s32[4,8]{1,0:T(4,128)} %bitcast.11, ...), custom_call_target="tpu_custom_call" | custom-call | tf_op jit(solution)/shard_map/pallas_call | solution.py:60
  2.5 23.7 %all-to-all-start = ((bf16[16,32,128]{2,1,0:T(8,128)(2,1)}), bf16[16,32,128]{2,1,0:T(8,128)(2,1)S(1)}, u32[]{:S(2)}, u32[]{:S(2)}) async-start(bf16[16,32,128]{2,1,0:T(8,128)(2,1)} %get-tuple-element.13), calls=%async_computation | async-start | bytes 262144 | tf_op jit(solution)/shard_map/all_to_all | solution.py:22
  26.2 5.4 %collective-permute-start = (bf16[56,1024]{1,0:T(8,128)(2,1)S(1)}, bf16[56,1024]{1,0:T(8,128)(2,1)S(1)}, u32[]{:S(2)}, u32[]{:S(2)}) collective-permute-start(bf16[56,1024]{1,0:T(8,128)(2,1)S(1)} %get-tuple-element.12), channel_id=1, source_target_pairs={{0,8},{2,10},{4,12},{6,14},{8,0},{10,2},{12,4},{14,6},{1,9},{3,11}... | collective-permute-start | bytes 344072 | tf_op jit(solution)/shard_map/ppermute | solution.py:30
  31.6 4.1 %all-to-all-done.refs_0_.refs_6_ = bf16[16,32,128]{2,1,0:T(8,128)(2,1)S(1)} async-done(((bf16[16,32,128]{2,1,0:T(8,128)(2,1)}), bf16[16,32,128]{2,1,0:T(8,128)(2,1)S(1)}, u32[]{:S(2)}, u32[]{:S(2)}) %all-to-all-start) | async-done | bytes 131104 | tf_op jit(solution)/shard_map/all_to_all | solution.py:22
  35.7 0.9 broadcast_in_dim.3
  36.5 3.7 %all-to-all-start.1 = ((bf16[8,16,16,128]{3,2,1,0:T(8,128)(2,1)}), bf16[8,16,16,128]{3,2,1,0:T(8,128)(2,1)S(1)}, u32[]{:S(2)}, u32[]{:S(2)}) async-start(bf16[8,16,16,128]{3,2,1,0:T(8,128)(2,1)} %broadcast_in_dim.3), calls=%async_computation.1 | async-start | bytes 1048576 | tf_op jit(solution)/shard_map/all_to_all | solution.py:22
  40.2 0.2 collective-permute-done
  40.5 0.4 collective-permute-start.1
  40.8 12.5 %collective-permute-done.1 = bf16[2,56,1024]{2,1,0:T(8,128)(2,1)S(1)} collective-permute-done((bf16[2,56,1024]{2,1,0:T(8,128)(2,1)S(1)}, bf16[2,56,1024]{2,1,0:T(8,128)(2,1)S(1)}, u32[]{:S(2)}, u32[]{:S(2)}) %collective-permute-start.1) | collective-permute-done | bytes 229408 | tf_op jit(solution)/shard_map/ppermute | solution.py:30
  53.3 0.1 collective-permute-start.4
  53.5 4.0 %collective-permute-done.4 = bf16[4,16,1024]{2,1,0:T(8,128)(2,1)S(1)} collective-permute-done((bf16[4,16,1024]{2,1,0:T(8,128)(2,1)S(1)}, bf16[4,16,1024]{2,1,0:T(8,128)(2,1)S(1)}, u32[]{:S(2)}, u32[]{:S(2)}) %collective-permute-start.4) | collective-permute-done | bytes 131104 | tf_op jit(solution)/shard_map/ppermute | solution.py:30
  57.6 2.1 %collective-permute-start.5 = (bf16[8,16,1024]{2,1,0:T(8,128)(2,1)S(1)}, bf16[8,16,1024]{2,1,0:T(8,128)(2,1)S(1)}, u32[]{:S(2)}, u32[]{:S(2)}) collective-permute-start(bf16[8,16,1024]{2,1,0:T(8,128)(2,1)S(1)} %pad_maximum_fusion.3.refs_2_), channel_id=1, source_target_pairs={{0,1},{1,0},{2,3},{3,2},{4,5},{5,4},{6,7},{7,6},{8,9},{9,8},{10,11... | collective-permute-start | bytes 786440 | tf_op jit(solution)/shard_map/ppermute | solution.py:30
  59.7 0.2 collective-permute-start.2
  59.9 1.0 collective-permute-done.5.refs_3_
  60.8 0.0 all-to-all-done.1.refs_1_.refs_4_
  60.8 1.1 shard_map.129
  61.9 6.6 %all-to-all-start.2 = ((bf16[8,16,16,128]{3,2,1,0:T(8,128)(2,1)}), bf16[8,16,16,128]{3,2,1,0:T(8,128)(2,1)S(1)}, u32[]{:S(2)}, u32[]{:S(2)}) async-start(bf16[8,16,16,128]{3,2,1,0:T(8,128)(2,1)} %get-tuple-element.14), calls=%async_computation.2 | async-start | bytes 1048576 | tf_op jit(solution)/shard_map/all_to_all | solution.py:22
  68.6 0.0 collective-permute-done.2
  68.6 0.1 pad_maximum_fusion.refs_0_
  68.6 0.1 collective-permute-start.3
  68.8 15.6 %collective-permute-done.3.refs_1_ = bf16[8,40,1024]{2,1,0:T(8,128)(2,1)S(1)} collective-permute-done((bf16[8,40,1024]{2,1,0:T(8,128)(2,1)S(1)}, bf16[8,40,1024]{2,1,0:T(8,128)(2,1)S(1)}, u32[]{:S(2)}, u32[]{:S(2)}) %collective-permute-start.3) | collective-permute-done | bytes 655392 | tf_op jit(solution)/shard_map/ppermute | solution.py:30
  84.4 2.1 %all-to-all-done.2.refs_5_ = bf16[8,16,16,128]{3,2,1,0:T(8,128)(2,1)S(1)} async-done(((bf16[8,16,16,128]{3,2,1,0:T(8,128)(2,1)}), bf16[8,16,16,128]{3,2,1,0:T(8,128)(2,1)S(1)}, u32[]{:S(2)}, u32[]{:S(2)}) %all-to-all-start.2) | async-done | bytes 524320 | tf_op jit(solution)/shard_map/all_to_all | solution.py:22
  86.5 0.9 shard_map.130
  87.4 16.5 %all_to_all.25.refs_0_ = bf16[8,200,128]{2,1,0:T(8,128)(2,1)S(1)} all-to-all(bf16[8,200,128]{2,1,0:T(8,128)(2,1)S(1)} %get-tuple-element.16), channel_id=1, replica_groups=mesh['parts'=2,'y'=8,'x'=8,'c'=2] {'y'}, dimensions={0} | all-to-all | bytes 819200 | tf_op jit(solution)/shard_map/all_to_all | solution.py:22
  103.9 0.1 shard_map.131
  104.0 0.0 copy-start
  104.0 0.0 copy-start.1
  104.0 16.0 %all_to_all.26.refs_0_ = bf16[16,40,128]{2,1,0:T(8,128)(2,1)S(1)} all-to-all(bf16[16,40,128]{2,1,0:T(8,128)(2,1)S(1)} %shard_map.131), channel_id=1, replica_groups=mesh['parts'=2,'y'=8,'x'=8,'c'=2] {'x','c'}, dimensions={0} | all-to-all | bytes 327680 | tf_op jit(solution)/shard_map/all_to_all | solution.py:22
  120.0 0.0 copy-done
  120.0 0.0 copy-done.1
  120.0 0.7 shard_map.132
  (9 shorter events, 0.1 us)
Async XLA Ops:
  2.5 33.2 %all-to-all-start = ((bf16[16,32,128]{2,1,0:T(8,128)(2,1)}), bf16[16,32,128]{2,1,0:T(8,128)(2,1)S(1)}, u32[]{:S(2)}, u32[]{:S(2)}) async-start(bf16[16,32,128]{2,1,0:T(8,128)(2,1)} %get-tuple-element.13), calls=%async_computation | async-start | bytes 262144 | tf_op jit(solution)/shard_map/all_to_all | solution.py:22
  26.2 14.2 %collective-permute-start = (bf16[56,1024]{1,0:T(8,128)(2,1)S(1)}, bf16[56,1024]{1,0:T(8,128)(2,1)S(1)}, u32[]{:S(2)}, u32[]{:S(2)}) collective-permute-start(bf16[56,1024]{1,0:T(8,128)(2,1)S(1)} %get-tuple-element.12), channel_id=1, source_target_pairs={{0,8},{2,10},{4,12},{6,14},{8,0},{10,2},{12,4},{14,6},{1,9},{3,11}... | collective-permute-start | bytes 344072 | tf_op jit(solution)/shard_map/ppermute | solution.py:30
  36.5 24.3 %all-to-all-start.1 = ((bf16[8,16,16,128]{3,2,1,0:T(8,128)(2,1)}), bf16[8,16,16,128]{3,2,1,0:T(8,128)(2,1)S(1)}, u32[]{:S(2)}, u32[]{:S(2)}) async-start(bf16[8,16,16,128]{3,2,1,0:T(8,128)(2,1)} %broadcast_in_dim.3), calls=%async_computation.1 | async-start | bytes 1048576 | tf_op jit(solution)/shard_map/all_to_all | solution.py:22
  40.5 12.9 %collective-permute-start.1 = (bf16[2,56,1024]{2,1,0:T(8,128)(2,1)S(1)}, bf16[2,56,1024]{2,1,0:T(8,128)(2,1)S(1)}, u32[]{:S(2)}, u32[]{:S(2)}) collective-permute-start(bf16[2,56,1024]{2,1,0:T(8,128)(2,1)S(1)} %pad_maximum_fusion.2), channel_id=1, source_target_pairs={{0,4},{2,6},{4,0},{6,2},{8,12},{10,14},{12,8},{14,10},{1,5},{3,7},... | collective-permute-start | bytes 688136 | tf_op jit(solution)/shard_map/ppermute | solution.py:30
  53.3 4.2 %collective-permute-start.4 = (bf16[4,16,1024]{2,1,0:T(8,128)(2,1)S(1)}, bf16[4,16,1024]{2,1,0:T(8,128)(2,1)S(1)}, u32[]{:S(2)}, u32[]{:S(2)}) collective-permute-start(bf16[4,16,1024]{2,1,0:T(8,128)(2,1)S(1)} %pad_maximum_fusion.4), channel_id=1, source_target_pairs={{0,2},{2,0},{4,6},{6,4},{8,10},{10,8},{12,14},{14,12},{1,3},{3,1},... | collective-permute-start | bytes 393224 | tf_op jit(solution)/shard_map/ppermute | solution.py:30
  57.6 3.2 %collective-permute-start.5 = (bf16[8,16,1024]{2,1,0:T(8,128)(2,1)S(1)}, bf16[8,16,1024]{2,1,0:T(8,128)(2,1)S(1)}, u32[]{:S(2)}, u32[]{:S(2)}) collective-permute-start(bf16[8,16,1024]{2,1,0:T(8,128)(2,1)S(1)} %pad_maximum_fusion.3.refs_2_), channel_id=1, source_target_pairs={{0,1},{1,0},{2,3},{3,2},{4,5},{5,4},{6,7},{7,6},{8,9},{9,8},{10,11... | collective-permute-start | bytes 786440 | tf_op jit(solution)/shard_map/ppermute | solution.py:30
  59.7 8.9 %collective-permute-start.2 = (bf16[4,40,1024]{2,1,0:T(8,128)(2,1)S(1)}, bf16[4,40,1024]{2,1,0:T(8,128)(2,1)S(1)}, u32[]{:S(2)}, u32[]{:S(2)}) collective-permute-start(bf16[4,40,1024]{2,1,0:T(8,128)(2,1)S(1)} %pad_maximum_fusion.1), channel_id=1, source_target_pairs={{0,1},{1,0},{2,3},{3,2},{4,5},{5,4},{6,7},{7,6},{8,9},{9,8},{10,11... | collective-permute-start | bytes 983048 | tf_op jit(solution)/shard_map/ppermute | solution.py:30
  61.9 24.6 %all-to-all-start.2 = ((bf16[8,16,16,128]{3,2,1,0:T(8,128)(2,1)}), bf16[8,16,16,128]{3,2,1,0:T(8,128)(2,1)S(1)}, u32[]{:S(2)}, u32[]{:S(2)}) async-start(bf16[8,16,16,128]{3,2,1,0:T(8,128)(2,1)} %get-tuple-element.14), calls=%async_computation.2 | async-start | bytes 1048576 | tf_op jit(solution)/shard_map/all_to_all | solution.py:22
  68.6 15.8 %collective-permute-start.3 = (bf16[8,40,1024]{2,1,0:T(8,128)(2,1)S(1)}, bf16[8,40,1024]{2,1,0:T(8,128)(2,1)S(1)}, u32[]{:S(2)}, u32[]{:S(2)}) collective-permute-start(bf16[8,40,1024]{2,1,0:T(8,128)(2,1)S(1)} %pad_maximum_fusion.refs_0_), channel_id=1, source_target_pairs={{0,2},{2,0},{4,6},{6,4},{8,10},{10,8},{12,14},{14,12},{1,3},{3,1},... | collective-permute-start | bytes 1966088 | tf_op jit(solution)/shard_map/ppermute | solution.py:30
  104.0 16.0 %copy-start = (f32[8,1024]{1,0:T(8,128)S(1)}, f32[8,1024]{1,0:T(8,128)}, u32[]{:S(2)}) copy-start(f32[8,1024]{1,0:T(8,128)} %refs_1_.3) | copy-start | bytes 98308
  104.0 16.0 %copy-start.1 = (f32[2,1024]{1,0:T(2,128)S(1)}, f32[2,1024]{1,0:T(2,128)}, u32[]{:S(2)}) copy-start(f32[2,1024]{1,0:T(2,128)} %refs_2_.3) | copy-start | bytes 24580

commit v4 on v3

--- a/solution.py
+++ b/solution.py
@@ -67,31 +67,31 @@
     )(*args)
 
 
-def pack_kernel(*refs):
-    sources, (slots, own), scratch, done = refs[:8], refs[8:10], refs[10:18], refs[18]
+def fetched(sources, scratch, done):
     pairs = enumerate(zip(sources, scratch))
     copies = [pltpu.make_async_copy(a, b, done.at[i]) for i, (a, b) in pairs]
     for copy in copies:
         copy.start()
     for copy in copies:
         copy.wait()
-    sigma, par, dinv, kid_top, kid_par, mask_par, mask_kid_top, mask_kid_par = scratch
+
+
+def lane_of(mask, at):
+    lane = lax.broadcasted_iota(jnp.int32, mask.shape, 1)
+    return jnp.sum(jnp.where(lane == at, mask, 0).astype(F32), axis=1, keepdims=True)
+
+
+def slots_kernel(*refs):
+    sources, slots, scratch, done = refs[:6], refs[6], refs[7:13], refs[13]
+    fetched(sources, scratch, done)
+    par, kid_top, kid_par, mask_par, mask_kid_top, mask_kid_par = scratch
     rt, w1 = par.shape
-    rp = dinv.shape[0]
-    kids = kid_top.shape[0]
+    kids, rp = kid_par.shape[:2]
     nj = slots.shape[0]
     position = lax.axis_index(ROW)
     block_top = lax.div(position * rt, BLK)
     block_par = lax.div(position * rp, BLK)
-    own[rt : 2 * rt, :] = sigma[:, 0:w1]
-    own[2 * rt : 3 * rt, :] = sigma[:, w1 : 2 * w1]
-    own[3 * rt : 3 * rt + rp, :] = dinv[...].astype(BF16)
-
-    def top_row(mask):
-        lane = lax.broadcasted_iota(jnp.int32, mask.shape, 1)
-        return jnp.sum(jnp.where(lane == block_top, mask, 0).astype(F32), axis=1, keepdims=True)
-
-    keep = top_row(mask_par[...])
+    keep = lane_of(mask_par[...], block_top)
     packed = []
     for m in range(w1 // LANES):
         at = slice(m * LANES, (m + 1) * LANES)
@@ -100,10 +100,9 @@
         top, low = piece[:rp], piece[rp:]
         packed.append(low_high(top, turned(low)))
         packed.append(low_high(turned(top), low))
-        own[0:rt, at] = piece.astype(BF16)
     per_kid = nj // kids
     for k in range(kids):
-        keep_top = top_row(mask_kid_top[k])
+        keep_top = lane_of(mask_kid_top[k], block_top)
         keep_par = mask_kid_par[k, pl.ds(block_par, 1), :].astype(F32)
         for m in range(per_kid):
             j = k * per_kid + m
@@ -113,6 +112,29 @@
             slots[j, 0 : 2 * rp, :] = jnp.concatenate([piece, packed[j]], axis=0).astype(BF16)
             piece = kid_top[k, :, at].astype(F32) * keep_top[block : block + 1]
             slots[j, 2 * rp : 2 * rp + rt, :] = piece.astype(BF16)
+
+
+def masked_kernel(par_hbm, mask_hbm, masked, par, mask_par, done):
+    fetched((par_hbm, mask_hbm), (par, mask_par), done)
+    rt, w1 = par.shape
+    keep = lane_of(mask_par[...], lax.div(lax.axis_index(ROW) * rt, BLK))
+    for b in range(w1 // BLK):
+        at = slice(b * BLK, (b + 1) * BLK)
+        masked[:, at] = (par[:, at].astype(F32) * keep[b : b + 1]).astype(BF16)
+
+
+def rows_kernel(sigma_hbm, dinv_hbm, rows, sigma, dinv, done):
+    fetched((sigma_hbm, dinv_hbm), (sigma, dinv), done)
+    rt = sigma.shape[0]
+    rp, w1 = dinv.shape
+    rows[0:rt, :] = sigma[:, 0:w1]
+    rows[rt : 2 * rt, :] = sigma[:, w1 : 2 * w1]
+    rows[2 * rt : 2 * rt + rp, :] = dinv[...].astype(BF16)
+
+
+def copy_kernel(source_hbm, result, scratch, done):
+    fetched((source_hbm,), (scratch,), done)
+    result[...] = scratch[...]
 
 
 def kid_par_columns(tall):
@@ -154,8 +176,8 @@
     both = jnp.concatenate([step_j[...].reshape(ny * nj * rt, LANES), par_j], axis=1)
 
     var = jnp.zeros((1, LANES), F32)
-    xs, ps = [], []
-    for b1, chunks in enumerate((near, far)):
+    xs = []
+    for bc, chunks in enumerate((near, far)):
         count = chunks.shape[0]
         s0 = chunks[:, 0:rt, :].reshape(count * rt, w1)
         s1 = chunks[:, rt : 2 * rt, :].reshape(count * rt, w1)
@@ -163,7 +185,7 @@
         x = dot(s0, both[:w1]) + dot(s1, both[w1:])
         db_own = dot(d.astype(BF16), kid_par_j)
         for k in range(count):
-            at = chunk_place(x_me, c_me, (b1, (k // 2) % 2, k % 2, k // 4))
+            at = chunk_place(x_me, c_me, (k // 4, (k // 2) % 2, k % 2, bc))
             piece = x[k * rt : (k + 1) * rt]
             kt = piece[:, :LANES].astype(BF16)
             part[at, 0:rt, :] = kt
@@ -174,11 +196,9 @@
             var = var + jnp.sum(step[at] * kt.astype(F32), axis=0, keepdims=True)
             var = var + jnp.sum(cols[at, 0:rp, :].astype(F32) * db_k, axis=0, keepdims=True)
         xs.append(x.astype(BF16))
-        for par in (par_own, par_other):
-            ps.append(par[4 * b1 : 4 * b1 + 4].reshape(4 * rt, w1))
 
     x = jnp.concatenate(xs, axis=0)
-    p = jnp.concatenate(ps, axis=0)
+    p = jnp.concatenate([p[...].reshape(nj // 2 * rt, w1) for p in (par_own, par_other)], axis=0)
     for y in range(ny):
         partial = dot_t(p[:, y * LANES : (y + 1) * LANES], x)
         rows = partial.shape[0]
@@ -260,35 +280,35 @@
     assert kids * w2 == nj * LANES and w1 == nj * HALF and wt == 2 * w1
     assert nx == 8 and rt == 2 * rp and nj * rp == LANES and ny * LANES == w1
 
-    arrays = (
-        sigma_top,
-        panel_par,
-        dinv_par,
-        panel_kid_top,
-        panel_kid_par,
-        mask_par.T,
-        mask_kid_top.transpose(0, 2, 1),
-        mask_kid_par,
-    )
-    slots, own = call(
-        pack_kernel,
-        [((nj, 2 * rp + rt, LANES), BF16), ((3 * rt + rp, w1), BF16)],
-        tuple(pltpu.with_memory_space_constraint(a, pltpu.HBM) for a in arrays),
-        [pl.BlockSpec(memory_space=pltpu.HBM)] * len(arrays),
-        [pltpu.VMEM(a.shape, a.dtype) for a in arrays]
-        + [pltpu.SemaphoreType.DMA((len(arrays),))],
-    )
-    own_4 = swapped(own, "x", 4)
+    def fetching(kernel, outs, arrays):
+        return call(
+            kernel,
+            outs,
+            tuple(pltpu.with_memory_space_constraint(a, pltpu.HBM) for a in arrays),
+            [pl.BlockSpec(memory_space=pltpu.HBM)] * len(arrays),
+            [pltpu.VMEM(a.shape, a.dtype) for a in arrays]
+            + [pltpu.SemaphoreType.DMA((len(arrays),))],
+        )
+
+    masks = (mask_par.T, mask_kid_top.transpose(0, 2, 1), mask_kid_par)
+    (slots,) = fetching(
+        slots_kernel,
+        [((nj, 2 * rp + rt, LANES), BF16)],
+        (panel_par, panel_kid_top, panel_kid_par, *masks),
+    )
     cols = exchanged(slots, XC)
-    two = jnp.stack([own, own_4])
+    (par_rows,) = fetching(masked_kernel, [((rt, w1), BF16)], (panel_par, masks[0]))
+    par_rows = jnp.stack([par_rows, swapped(par_rows, "x", 4)])
+    (rows,) = fetching(rows_kernel, [((2 * rt + rp, w1), BF16)], (sigma_top, dinv_par))
+    rows = jnp.stack([rows, swapped(rows, "x", 4)])
+    (dvar_kid,) = fetching(copy_kernel, [(dvar_kid.shape, F32)], (dvar_kid,))
     tall = sent_to_all(cols[:, : 2 * rp], "y")
-    two_2 = swapped(two, "x", 2)
-    par_four = jnp.concatenate([two[:, :rt], two_2[:, :rt]])
-    four = jnp.concatenate([two[:, rt:], two_2[:, rt:]])
-    par_own = jnp.concatenate([par_four, swapped(par_four, "x", 1)])
+    par_rows = jnp.concatenate([par_rows, swapped(par_rows, "x", 2)])
+    par_own = jnp.concatenate([par_rows, swapped(par_rows, "x", 1)])
     par_other = swapped(par_own, "c", 1)
-    near = jnp.concatenate([four, swapped(four, "c", 1)])
-    far = swapped(near, "x", 1)
+    rows = jnp.concatenate([rows, swapped(rows, "x", 2)])
+    near = jnp.concatenate([rows, swapped(rows, "x", 1)])
+    far = swapped(near, "c", 1)
 
     def sized(kernel):
         return lambda *refs: kernel(rt, rp, *refs)

time: 121 us -> 119 us (0.983)
  blocking collectives: 32.4 us -> 13.4 us
  starting transfers between devices: 42.3 us -> 60.4 us
  waiting for transfers between devices: 39.5 us -> 34.7 us
  Pallas kernels: 4.65 us -> 7.7 us
    all_to_all x2 -> x1, blocking collectives: 32.4 us -> 13.4 us  [exchanged(): return lax.all_to_all(x, axes, split_axis=0, concat_axis=0, tiled=True)]
    ppermute x6 -> x8, waiting for transfers between devices: 33.3 us -> 15.1 us  [swapped(): lax.ppermute(x, axis, [(i, i ^ bit) for i in range(lax.axis_size(axis))])]
    all_to_all x3 -> x4, waiting for transfers between devices: 6.18 us -> 19.6 us  [exchanged(): return lax.all_to_all(x, axes, split_axis=0, concat_axis=0, tiled=True)]
    all_to_all x3 -> x4, starting transfers between devices: 34.1 us -> 45.4 us  [exchanged(): return lax.all_to_all(x, axes, split_axis=0, concat_axis=0, tiled=True)]
    ppermute x6 -> x8, starting transfers between devices: 8.28 us -> 15 us  [swapped(): lax.ppermute(x, axis, [(i, i ^ bit) for i in range(lax.axis_size(axis))])]
    pallas_call x5 -> x8, Pallas kernels: 4.65 us -> 7.7 us  [call(): pl.pallas_call(kernel, out_shape=tuple((jax.ShapeDtypeStruct(s, d) for s,...]
  transfers between devices with their start and end apart: 9 -> 12, of which waited for: 7 -> 8; matrix products, arithmetic and copies ran while one was open for 1% -> 1% of each run, Pallas kernels for 1% -> 3%
where the time goes in v4:
time: 119 us; the launch traced here: 118 us
  starting transfers between devices  60.4 us (51%)
  waiting for transfers between devices  34.7 us (29%)
  blocking collectives  13.4 us (11%)
  Pallas kernels  7.7 us (6%)
    all_to_all x4, starting transfers between devices, exchanged(): return lax.all_to_all(x, axes, split_axis=0, concat_axis=0, tiled=True)  45.4 us
    all_to_all x4, waiting for transfers between devices, exchanged(): return lax.all_to_all(x, axes, split_axis=0, concat_axis=0, tiled=True)  19.6 us
    ppermute x8, waiting for transfers between devices, swapped(): lax.ppermute(x, axis, [(i, i ^ bit) for i in range(lax.axis_size(axis))])  15.1 us
    ppermute x8, starting transfers between devices, swapped(): lax.ppermute(x, axis, [(i, i ^ bit) for i in range(lax.axis_size(axis))])  15 us
    all_to_all x1, blocking collectives, exchanged(): return lax.all_to_all(x, axes, split_axis=0, concat_axis=0, tiled=True)  13.4 us
    pallas_call x8, Pallas kernels, call(): pl.pallas_call(kernel, out_shape=tuple((jax.ShapeDtypeStruct(s, d) for s,...  7.7 us
  transfers between devices with their start and end apart: 12, of which 8 were waited for; matrix products, arithmetic and copies ran while one was open for 1% of the time, Pallas kernels for 3%

profile of v4, /device:TPU:513, one launch (start us, length us, event | category | flops | bytes accessed | tf_op | source)
XLA Modules:
  0.0 118.1 jit_solution(14344272880743000849)
XLA Ops:
  0.6 1.8 %shard_map.130 = bf16[16,32,128]{2,1,0:T(8,128)(2,1)} custom-call(bf16[16,1024]{1,0:T(8,128)(2,1)} %refs_0_.1, bf16[2,16,1024]{2,1,0:T(8,128)(2,1)} %refs_1_.2, bf16[2,8,1024]{2,1,0:T(8,128)(2,1)} %refs_2_.1, s32[4,8]{1,0:T(4,128)} %bitcast.18, s32[2,4,8]{2,1,0:T(4,128)} %bitcast.20, s32[2,4,4]{2,1,0:T(4,128)} %refs_5_.1), custom_call_target="tpu_custom_call" | custom-call | tf_op jit(solution)/shard_map/pallas_call | solution.py:60
  2.4 23.7 %all-to-all-start = ((bf16[16,32,128]{2,1,0:T(8,128)(2,1)}), bf16[16,32,128]{2,1,0:T(8,128)(2,1)S(1)}, u32[]{:S(2)}, u32[]{:S(2)}) async-start(bf16[16,32,128]{2,1,0:T(8,128)(2,1)} %shard_map.130), calls=%async_computation | async-start | bytes 262144 | tf_op jit(solution)/shard_map/all_to_all | solution.py:22
  26.1 0.9 shard_map.129
  27.0 5.5 %collective-permute-start.4 = (bf16[16,1024]{1,0:T(8,128)(2,1)S(1)}, bf16[16,1024]{1,0:T(8,128)(2,1)S(1)}, u32[]{:S(2)}, u32[]{:S(2)}) collective-permute-start(bf16[16,1024]{1,0:T(8,128)(2,1)S(1)} %shard_map.129), channel_id=1, source_target_pairs={{0,8},{2,10},{4,12},{6,14},{8,0},{10,2},{12,4},{14,6},{1,9},{3,11}... | collective-permute-start | bytes 98312 | tf_op jit(solution)/shard_map/ppermute | solution.py:30
  32.5 3.1 %all-to-all-done.refs_0_.refs_6_ = bf16[16,32,128]{2,1,0:T(8,128)(2,1)S(1)} async-done(((bf16[16,32,128]{2,1,0:T(8,128)(2,1)}), bf16[16,32,128]{2,1,0:T(8,128)(2,1)S(1)}, u32[]{:S(2)}, u32[]{:S(2)}) %all-to-all-start) | async-done | bytes 131104 | tf_op jit(solution)/shard_map/all_to_all | solution.py:22
  35.6 0.9 broadcast_in_dim.3
  36.5 3.7 %all-to-all-start.1 = ((bf16[8,16,16,128]{3,2,1,0:T(8,128)(2,1)}), bf16[8,16,16,128]{3,2,1,0:T(8,128)(2,1)S(1)}, u32[]{:S(2)}, u32[]{:S(2)}) async-start(bf16[8,16,16,128]{3,2,1,0:T(8,128)(2,1)} %broadcast_in_dim.3), calls=%async_computation.1 | async-start | bytes 1048576 | tf_op jit(solution)/shard_map/all_to_all | solution.py:22
  40.2 0.0 collective-permute-done.4
  40.2 0.2 collective-permute-start.5
  40.5 0.9 shard_map.128
  41.3 2.1 %collective-permute-start = (bf16[40,1024]{1,0:T(8,128)(2,1)S(1)}, bf16[40,1024]{1,0:T(8,128)(2,1)S(1)}, u32[]{:S(2)}, u32[]{:S(2)}) collective-permute-start(bf16[40,1024]{1,0:T(8,128)(2,1)S(1)} %shard_map.128), channel_id=1, source_target_pairs={{0,8},{2,10},{4,12},{6,14},{8,0},{10,2},{12,4},{14,6},{1,9},{3,11}... | collective-permute-start | bytes 245768 | tf_op jit(solution)/shard_map/ppermute | solution.py:30
  43.4 3.8 %collective-permute-done.5 = bf16[2,16,1024]{2,1,0:T(8,128)(2,1)S(1)} collective-permute-done((bf16[2,16,1024]{2,1,0:T(8,128)(2,1)S(1)}, bf16[2,16,1024]{2,1,0:T(8,128)(2,1)S(1)}, u32[]{:S(2)}, u32[]{:S(2)}) %collective-permute-start.5) | collective-permute-done | bytes 65568 | tf_op jit(solution)/shard_map/ppermute | solution.py:30
  47.2 0.1 collective-permute-start.6
  47.3 2.7 %collective-permute-done = bf16[40,1024]{1,0:T(8,128)(2,1)S(1)} collective-permute-done((bf16[40,1024]{1,0:T(8,128)(2,1)S(1)}, bf16[40,1024]{1,0:T(8,128)(2,1)S(1)}, u32[]{:S(2)}, u32[]{:S(2)}) %collective-permute-start) | collective-permute-done | bytes 81952 | tf_op jit(solution)/shard_map/ppermute | solution.py:30
  50.1 3.7 %collective-permute-start.1 = (bf16[2,40,1024]{2,1,0:T(8,128)(2,1)S(1)}, bf16[2,40,1024]{2,1,0:T(8,128)(2,1)S(1)}, u32[]{:S(2)}, u32[]{:S(2)}) collective-permute-start(bf16[2,40,1024]{2,1,0:T(8,128)(2,1)S(1)} %pad_maximum_fusion.3), channel_id=1, source_target_pairs={{0,4},{2,6},{4,0},{6,2},{8,12},{10,14},{12,8},{14,10},{1,5},{3,7},... | collective-permute-start | bytes 491528 | tf_op jit(solution)/shard_map/ppermute | solution.py:30
  53.8 0.0 collective-permute-done.6
  53.8 0.8 collective-permute-start.7
  54.7 4.7 %collective-permute-done.1 = bf16[2,40,1024]{2,1,0:T(8,128)(2,1)S(1)} collective-permute-done((bf16[2,40,1024]{2,1,0:T(8,128)(2,1)S(1)}, bf16[2,40,1024]{2,1,0:T(8,128)(2,1)S(1)}, u32[]{:S(2)}, u32[]{:S(2)}) %collective-permute-start.1) | collective-permute-done | bytes 163872 | tf_op jit(solution)/shard_map/ppermute | solution.py:30
  59.4 0.1 collective-permute-start.2
  59.5 0.0 collective-permute-done.7.refs_3_
  59.6 0.0 all-to-all-done.1.refs_1_.refs_4_
  59.6 1.1 shard_map.131
  60.7 4.6 %all-to-all-start.2 = ((bf16[8,16,16,128]{3,2,1,0:T(8,128)(2,1)}), bf16[8,16,16,128]{3,2,1,0:T(8,128)(2,1)S(1)}, u32[]{:S(2)}, u32[]{:S(2)}) async-start(bf16[8,16,16,128]{3,2,1,0:T(8,128)(2,1)} %get-tuple-element.10), calls=%async_computation.2 | async-start | bytes 1048576 | tf_op jit(solution)/shard_map/all_to_all | solution.py:22
  65.2 2.2 %collective-permute-done.2 = bf16[4,40,1024]{2,1,0:T(8,128)(2,1)S(1)} collective-permute-done((bf16[4,40,1024]{2,1,0:T(8,128)(2,1)S(1)}, bf16[4,40,1024]{2,1,0:T(8,128)(2,1)S(1)}, u32[]{:S(2)}, u32[]{:S(2)}) %collective-permute-start.2) | collective-permute-done | bytes 327712 | tf_op jit(solution)/shard_map/ppermute | solution.py:30
  67.4 0.1 pad_maximum_fusion.refs_0_
  67.5 2.3 %collective-permute-start.3 = (bf16[8,40,1024]{2,1,0:T(8,128)(2,1)S(1)}, bf16[8,40,1024]{2,1,0:T(8,128)(2,1)S(1)}, u32[]{:S(2)}, u32[]{:S(2)}) collective-permute-start(bf16[8,40,1024]{2,1,0:T(8,128)(2,1)S(1)} %pad_maximum_fusion.refs_0_), channel_id=1, source_target_pairs={{0,1},{1,0},{2,3},{3,2},{4,5},{5,4},{6,7},{7,6},{8,9},{9,8},{10,11... | collective-permute-start | bytes 1966088 | tf_op jit(solution)/shard_map/ppermute | solution.py:30
  69.8 1.7 %collective-permute-done.3.refs_1_ = bf16[8,40,1024]{2,1,0:T(8,128)(2,1)S(1)} collective-permute-done((bf16[8,40,1024]{2,1,0:T(8,128)(2,1)S(1)}, bf16[8,40,1024]{2,1,0:T(8,128)(2,1)S(1)}, u32[]{:S(2)}, u32[]{:S(2)}) %collective-permute-start.3) | collective-permute-done | bytes 655392 | tf_op jit(solution)/shard_map/ppermute | solution.py:30
  71.6 7.7 %all-to-all-done.2.refs_5_ = bf16[8,16,16,128]{3,2,1,0:T(8,128)(2,1)S(1)} async-done(((bf16[8,16,16,128]{3,2,1,0:T(8,128)(2,1)}), bf16[8,16,16,128]{3,2,1,0:T(8,128)(2,1)S(1)}, u32[]{:S(2)}, u32[]{:S(2)}) %all-to-all-start.2) | async-done | bytes 524320 | tf_op jit(solution)/shard_map/all_to_all | solution.py:22
  79.3 0.9 shard_map.132
  80.2 13.4 %all_to_all.25.refs_0_ = bf16[8,200,128]{2,1,0:T(8,128)(2,1)S(1)} all-to-all(bf16[8,200,128]{2,1,0:T(8,128)(2,1)S(1)} %get-tuple-element.12), channel_id=1, replica_groups=mesh['parts'=2,'y'=8,'x'=8,'c'=2] {'y'}, dimensions={0} | all-to-all | bytes 819200 | tf_op jit(solution)/shard_map/all_to_all | solution.py:22
  93.6 0.8 shard_map.133
  94.4 0.0 copy-start
  94.4 13.4 %all-to-all-start.4 = ((bf16[16,40,128]{2,1,0:T(8,128)(2,1)}), bf16[16,40,128]{2,1,0:T(8,128)(2,1)S(1)}, u32[]{:S(2)}, u32[]{:S(2)}) async-start(bf16[16,40,128]{2,1,0:T(8,128)(2,1)} %shard_map.133), calls=%async_computation.4 | async-start | bytes 327680 | tf_op jit(solution)/shard_map/all_to_all | solution.py:22
  107.9 0.7 shard_map.134.refs_2_
  108.6 8.8 %all-to-all-done.4.refs_0_ = bf16[16,40,128]{2,1,0:T(8,128)(2,1)S(1)} async-done(((bf16[16,40,128]{2,1,0:T(8,128)(2,1)}), bf16[16,40,128]{2,1,0:T(8,128)(2,1)S(1)}, u32[]{:S(2)}, u32[]{:S(2)}) %all-to-all-start.4) | async-done | bytes 163872 | tf_op jit(solution)/shard_map/all_to_all | solution.py:22
  117.4 0.0 copy-done
  117.4 0.7 shard_map.135
  (6 shorter events, 0.1 us)
Async XLA Ops:
  2.4 33.2 %all-to-all-start = ((bf16[16,32,128]{2,1,0:T(8,128)(2,1)}), bf16[16,32,128]{2,1,0:T(8,128)(2,1)S(1)}, u32[]{:S(2)}, u32[]{:S(2)}) async-start(bf16[16,32,128]{2,1,0:T(8,128)(2,1)} %shard_map.130), calls=%async_computation | async-start | bytes 262144 | tf_op jit(solution)/shard_map/all_to_all | solution.py:22
  27.0 13.2 %collective-permute-start.4 = (bf16[16,1024]{1,0:T(8,128)(2,1)S(1)}, bf16[16,1024]{1,0:T(8,128)(2,1)S(1)}, u32[]{:S(2)}, u32[]{:S(2)}) collective-permute-start(bf16[16,1024]{1,0:T(8,128)(2,1)S(1)} %shard_map.129), channel_id=1, source_target_pairs={{0,8},{2,10},{4,12},{6,14},{8,0},{10,2},{12,4},{14,6},{1,9},{3,11}... | collective-permute-start | bytes 98312 | tf_op jit(solution)/shard_map/ppermute | solution.py:30
  36.5 23.1 %all-to-all-start.1 = ((bf16[8,16,16,128]{3,2,1,0:T(8,128)(2,1)}), bf16[8,16,16,128]{3,2,1,0:T(8,128)(2,1)S(1)}, u32[]{:S(2)}, u32[]{:S(2)}) async-start(bf16[8,16,16,128]{3,2,1,0:T(8,128)(2,1)} %broadcast_in_dim.3), calls=%async_computation.1 | async-start | bytes 1048576 | tf_op jit(solution)/shard_map/all_to_all | solution.py:22
  40.2 6.9 %collective-permute-start.5 = (bf16[2,16,1024]{2,1,0:T(8,128)(2,1)S(1)}, bf16[2,16,1024]{2,1,0:T(8,128)(2,1)S(1)}, u32[]{:S(2)}, u32[]{:S(2)}) collective-permute-start(bf16[2,16,1024]{2,1,0:T(8,128)(2,1)S(1)} %pad_maximum_fusion.5), channel_id=1, source_target_pairs={{0,4},{2,6},{4,0},{6,2},{8,12},{10,14},{12,8},{14,10},{1,5},{3,7},... | collective-permute-start | bytes 196616 | tf_op jit(solution)/shard_map/ppermute | solution.py:30
  41.3 8.7 %collective-permute-start = (bf16[40,1024]{1,0:T(8,128)(2,1)S(1)}, bf16[40,1024]{1,0:T(8,128)(2,1)S(1)}, u32[]{:S(2)}, u32[]{:S(2)}) collective-permute-start(bf16[40,1024]{1,0:T(8,128)(2,1)S(1)} %shard_map.128), channel_id=1, source_target_pairs={{0,8},{2,10},{4,12},{6,14},{8,0},{10,2},{12,4},{14,6},{1,9},{3,11}... | collective-permute-start | bytes 245768 | tf_op jit(solution)/shard_map/ppermute | solution.py:30
  47.2 6.6 %collective-permute-start.6 = (bf16[4,16,1024]{2,1,0:T(8,128)(2,1)S(1)}, bf16[4,16,1024]{2,1,0:T(8,128)(2,1)S(1)}, u32[]{:S(2)}, u32[]{:S(2)}) collective-permute-start(bf16[4,16,1024]{2,1,0:T(8,128)(2,1)S(1)} %pad_maximum_fusion.4), channel_id=1, source_target_pairs={{0,2},{2,0},{4,6},{6,4},{8,10},{10,8},{12,14},{14,12},{1,3},{3,1},... | collective-permute-start | bytes 393224 | tf_op jit(solution)/shard_map/ppermute | solution.py:30
  50.1 9.3 %collective-permute-start.1 = (bf16[2,40,1024]{2,1,0:T(8,128)(2,1)S(1)}, bf16[2,40,1024]{2,1,0:T(8,128)(2,1)S(1)}, u32[]{:S(2)}, u32[]{:S(2)}) collective-permute-start(bf16[2,40,1024]{2,1,0:T(8,128)(2,1)S(1)} %pad_maximum_fusion.3), channel_id=1, source_target_pairs={{0,4},{2,6},{4,0},{6,2},{8,12},{10,14},{12,8},{14,10},{1,5},{3,7},... | collective-permute-start | bytes 491528 | tf_op jit(solution)/shard_map/ppermute | solution.py:30
  53.8 5.7 %collective-permute-start.7 = (bf16[8,16,1024]{2,1,0:T(8,128)(2,1)S(1)}, bf16[8,16,1024]{2,1,0:T(8,128)(2,1)S(1)}, u32[]{:S(2)}, u32[]{:S(2)}) collective-permute-start(bf16[8,16,1024]{2,1,0:T(8,128)(2,1)S(1)} %pad_maximum_fusion.2.refs_2_), channel_id=1, source_target_pairs={{0,1},{1,0},{2,3},{3,2},{4,5},{5,4},{6,7},{7,6},{8,9},{9,8},{10,11... | collective-permute-start | bytes 786440 | tf_op jit(solution)/shard_map/ppermute | solution.py:30
  59.4 8.0 %collective-permute-start.2 = (bf16[4,40,1024]{2,1,0:T(8,128)(2,1)S(1)}, bf16[4,40,1024]{2,1,0:T(8,128)(2,1)S(1)}, u32[]{:S(2)}, u32[]{:S(2)}) collective-permute-start(bf16[4,40,1024]{2,1,0:T(8,128)(2,1)S(1)} %pad_maximum_fusion.1), channel_id=1, source_target_pairs={{0,2},{2,0},{4,6},{6,4},{8,10},{10,8},{12,14},{14,12},{1,3},{3,1},... | collective-permute-start | bytes 983048 | tf_op jit(solution)/shard_map/ppermute | solution.py:30
  60.7 18.6 %all-to-all-start.2 = ((bf16[8,16,16,128]{3,2,1,0:T(8,128)(2,1)}), bf16[8,16,16,128]{3,2,1,0:T(8,128)(2,1)S(1)}, u32[]{:S(2)}, u32[]{:S(2)}) async-start(bf16[8,16,16,128]{3,2,1,0:T(8,128)(2,1)} %get-tuple-element.10), calls=%async_computation.2 | async-start | bytes 1048576 | tf_op jit(solution)/shard_map/all_to_all | solution.py:22
  67.5 4.1 %collective-permute-start.3 = (bf16[8,40,1024]{2,1,0:T(8,128)(2,1)S(1)}, bf16[8,40,1024]{2,1,0:T(8,128)(2,1)S(1)}, u32[]{:S(2)}, u32[]{:S(2)}) collective-permute-start(bf16[8,40,1024]{2,1,0:T(8,128)(2,1)S(1)} %pad_maximum_fusion.refs_0_), channel_id=1, source_target_pairs={{0,1},{1,0},{2,3},{3,2},{4,5},{5,4},{6,7},{7,6},{8,9},{9,8},{10,11... | collective-permute-start | bytes 1966088 | tf_op jit(solution)/shard_map/ppermute | solution.py:30
  94.4 23.0 %copy-start = (f32[8,1024]{1,0:T(8,128)S(1)}, f32[8,1024]{1,0:T(8,128)}, u32[]{:S(2)}) copy-start(f32[8,1024]{1,0:T(8,128)} %refs_1_.3) | copy-start | bytes 98308
  94.4 23.0 %all-to-all-start.4 = ((bf16[16,40,128]{2,1,0:T(8,128)(2,1)}), bf16[16,40,128]{2,1,0:T(8,128)(2,1)S(1)}, u32[]{:S(2)}, u32[]{:S(2)}) async-start(bf16[16,40,128]{2,1,0:T(8,128)(2,1)} %shard_map.133), calls=%async_computation.4 | async-start | bytes 327680 | tf_op jit(solution)/shard_map/all_to_all | solution.py:22

commit v5 on v4

--- a/solution.py
+++ b/solution.py
@@ -20,10 +20,6 @@
 
 def exchanged(x, axes):
     return lax.all_to_all(x, axes, split_axis=0, concat_axis=0, tiled=True)
-
-
-def sent_to_all(x, axes):
-    return exchanged(jnp.broadcast_to(x, (lax.axis_size(axes), *x.shape)), axes)
 
 
 def swapped(x, axis, bit):
@@ -114,27 +110,43 @@
             slots[j, 2 * rp : 2 * rp + rt, :] = piece.astype(BF16)
 
 
-def masked_kernel(par_hbm, mask_hbm, masked, par, mask_par, done):
-    fetched((par_hbm, mask_hbm), (par, mask_par), done)
+def rows_kernel(*refs):
+    sources, rows, scratch, done = refs[:4], refs[4], refs[5:9], refs[9]
+    fetched(sources, scratch, done)
+    sigma, par, dinv, mask_par = scratch
     rt, w1 = par.shape
+    rp = dinv.shape[0]
     keep = lane_of(mask_par[...], lax.div(lax.axis_index(ROW) * rt, BLK))
     for b in range(w1 // BLK):
         at = slice(b * BLK, (b + 1) * BLK)
-        masked[:, at] = (par[:, at].astype(F32) * keep[b : b + 1]).astype(BF16)
-
-
-def rows_kernel(sigma_hbm, dinv_hbm, rows, sigma, dinv, done):
-    fetched((sigma_hbm, dinv_hbm), (sigma, dinv), done)
-    rt = sigma.shape[0]
-    rp, w1 = dinv.shape
-    rows[0:rt, :] = sigma[:, 0:w1]
-    rows[rt : 2 * rt, :] = sigma[:, w1 : 2 * w1]
-    rows[2 * rt : 2 * rt + rp, :] = dinv[...].astype(BF16)
+        rows[0:rt, at] = (par[:, at].astype(F32) * keep[b : b + 1]).astype(BF16)
+    rows[rt : 2 * rt, :] = sigma[:, 0:w1]
+    rows[2 * rt : 3 * rt, :] = sigma[:, w1 : 2 * w1]
+    rows[3 * rt : 3 * rt + rp, :] = dinv[...].astype(BF16)
 
 
 def copy_kernel(source_hbm, result, scratch, done):
     fetched((source_hbm,), (scratch,), done)
     result[...] = scratch[...]
+
+
+def stack_kernel(own, other, par_rows, rows):
+    rt = par_rows.shape[1]
+    for i, source in enumerate((own, other)):
+        par_rows[i] = source[0:rt, :]
+        rows[i] = source[rt : rt + rows.shape[1], :]
+
+
+def join_kernel(own, other, joined):
+    count = own.shape[0]
+    joined[0:count] = own[...]
+    joined[count : 2 * count] = other[...]
+
+
+def repeat_kernel(cols, send):
+    rows = send.shape[2]
+    for y in range(send.shape[0]):
+        send[y] = cols[:, 0:rows, :]
 
 
 def kid_par_columns(tall):
@@ -297,16 +309,25 @@
         (panel_par, panel_kid_top, panel_kid_par, *masks),
     )
     cols = exchanged(slots, XC)
-    (par_rows,) = fetching(masked_kernel, [((rt, w1), BF16)], (panel_par, masks[0]))
-    par_rows = jnp.stack([par_rows, swapped(par_rows, "x", 4)])
-    (rows,) = fetching(rows_kernel, [((2 * rt + rp, w1), BF16)], (sigma_top, dinv_par))
-    rows = jnp.stack([rows, swapped(rows, "x", 4)])
+    (rows,) = fetching(
+        rows_kernel,
+        [((3 * rt + rp, w1), BF16)],
+        (sigma_top, panel_par, dinv_par, masks[0]),
+    )
+    far_rows = swapped(rows, "x", 4)
     (dvar_kid,) = fetching(copy_kernel, [(dvar_kid.shape, F32)], (dvar_kid,))
-    tall = sent_to_all(cols[:, : 2 * rp], "y")
+    par_rows, rows = call(
+        stack_kernel,
+        [((2, rt, w1), BF16), ((2, 2 * rt + rp, w1), BF16)],
+        (rows, far_rows),
+    )
+    (tall_send,) = call(repeat_kernel, [((ny, nj, 2 * rp, LANES), BF16)], (cols,))
+    tall = exchanged(tall_send, "y")
     par_rows = jnp.concatenate([par_rows, swapped(par_rows, "x", 2)])
     par_own = jnp.concatenate([par_rows, swapped(par_rows, "x", 1)])
     par_other = swapped(par_own, "c", 1)
-    rows = jnp.concatenate([rows, swapped(rows, "x", 2)])
+    rows_2 = swapped(rows, "x", 2)
+    (rows,) = call(join_kernel, [((4, 2 * rt + rp, w1), BF16)], (rows, rows_2))
     near = jnp.concatenate([rows, swapped(rows, "x", 1)])
     far = swapped(near, "c", 1)
 

time: 119 us -> 123 us (1.034)
  starting transfers between devices: 60.4 us -> 26.1 us
  blocking collectives: 13.4 us -> 46.4 us
  waiting for transfers between devices: 34.7 us -> 41.9 us
    all_to_all x1 -> x2, blocking collectives: 13.4 us -> 46.4 us  [exchanged(): return lax.all_to_all(x, axes, split_axis=0, concat_axis=0, tiled=True)]
    all_to_all x4 -> x3, starting transfers between devices: 45.4 us -> 19.3 us  [exchanged(): return lax.all_to_all(x, axes, split_axis=0, concat_axis=0, tiled=True)]
    ppermute x8 -> x7, starting transfers between devices: 15 us -> 6.73 us  [swapped(): lax.ppermute(x, axis, [(i, i ^ bit) for i in range(lax.axis_size(axis))])]
    ppermute x8 -> x7, waiting for transfers between devices: 15.1 us -> 20.3 us  [swapped(): lax.ppermute(x, axis, [(i, i ^ bit) for i in range(lax.axis_size(axis))])]
    all_to_all x4 -> x3, waiting for transfers between devices: 19.6 us -> 21.6 us  [exchanged(): return lax.all_to_all(x, axes, split_axis=0, concat_axis=0, tiled=True)]
    pallas_call x8 -> x10, Pallas kernels: 7.7 us -> 7.18 us  [call(): pl.pallas_call(kernel, out_shape=tuple((jax.ShapeDtypeStruct(s, d) for s,...]
  transfers between devices with their start and end apart: 12 -> 10, of which waited for: 8 -> 7; matrix products, arithmetic and copies ran while one was open for 1% -> 0% of each run, Pallas kernels for 3% -> 2%
where the time goes in v5:
time: 123 us; the launch traced here: 122 us
  blocking collectives  46.4 us (38%)
  waiting for transfers between devices  41.9 us (34%)
  starting transfers between devices  26.1 us (21%)
  Pallas kernels  7.18 us (6%)
    all_to_all x2, blocking collectives, exchanged(): return lax.all_to_all(x, axes, split_axis=0, concat_axis=0, tiled=True)  46.4 us
    all_to_all x3, waiting for transfers between devices, exchanged(): return lax.all_to_all(x, axes, split_axis=0, concat_axis=0, tiled=True)  21.6 us
    ppermute x7, waiting for transfers between devices, swapped(): lax.ppermute(x, axis, [(i, i ^ bit) for i in range(lax.axis_size(axis))])  20.3 us
    all_to_all x3, starting transfers between devices, exchanged(): return lax.all_to_all(x, axes, split_axis=0, concat_axis=0, tiled=True)  19.3 us
    pallas_call x10, Pallas kernels, call(): pl.pallas_call(kernel, out_shape=tuple((jax.ShapeDtypeStruct(s, d) for s,...  7.18 us
    ppermute x7, starting transfers between devices, swapped(): lax.ppermute(x, axis, [(i, i ^ bit) for i in range(lax.axis_size(axis))])  6.73 us
  transfers between devices with their start and end apart: 10, of which 7 were waited for; matrix products, arithmetic and copies ran while one was open for 0% of the time, Pallas kernels for 2%

profile of v5, /device:TPU:513, one launch (start us, length us, event | category | flops | bytes accessed | tf_op | source)
XLA Modules:
  0.0 122.4 jit_solution(9575486793601583258)
XLA Ops:
  0.6 1.1 shard_map.131
  1.7 32.1 %all_to_all.25.cols.refs_0_.refs_6_ = bf16[16,32,128]{2,1,0:T(8,128)(2,1)S(1)} all-to-all(bf16[16,32,128]{2,1,0:T(8,128)(2,1)S(1)} %shard_map.131), channel_id=1, replica_groups=mesh['parts'=2,'y'=8,'x'=8,'c'=2] {'x','c'}, dimensions={0} | all-to-all | bytes 262144 | tf_op jit(solution)/shard_map/all_to_all | solution.py:22
  33.8 0.9 shard_map.132
  34.7 3.7 %all-to-all-start.1 = ((bf16[8,16,16,128]{3,2,1,0:T(8,128)(2,1)}), bf16[8,16,16,128]{3,2,1,0:T(8,128)(2,1)S(1)}, u32[]{:S(2)}, u32[]{:S(2)}) async-start(bf16[8,16,16,128]{3,2,1,0:T(8,128)(2,1)} %shard_map.132), calls=%async_computation.1 | async-start | bytes 1048576 | tf_op jit(solution)/shard_map/all_to_all | solution.py:22
  38.4 1.0 shard_map.128.own
  39.4 0.7 collective-permute-start
  40.1 8.9 %collective-permute-done.other = bf16[56,1024]{1,0:T(8,128)(2,1)S(1)} collective-permute-done((bf16[56,1024]{1,0:T(8,128)(2,1)S(1)}, bf16[56,1024]{1,0:T(8,128)(2,1)S(1)}, u32[]{:S(2)}, u32[]{:S(2)}) %collective-permute-start) | collective-permute-done | bytes 114720 | tf_op jit(solution)/shard_map/ppermute | solution.py:26
  49.0 0.1 collective-permute-start.4
  49.1 4.8 %collective-permute-done.4 = bf16[2,16,1024]{2,1,0:T(8,128)(2,1)S(1)} collective-permute-done((bf16[2,16,1024]{2,1,0:T(8,128)(2,1)S(1)}, bf16[2,16,1024]{2,1,0:T(8,128)(2,1)S(1)}, u32[]{:S(2)}, u32[]{:S(2)}) %collective-permute-start.4) | collective-permute-done | bytes 65568 | tf_op jit(solution)/shard_map/ppermute | solution.py:26
  54.0 0.1 collective-permute-start.5
  54.1 1.3 %collective-permute-start.1 = (bf16[2,40,1024]{2,1,0:T(8,128)(2,1)S(1)}, bf16[2,40,1024]{2,1,0:T(8,128)(2,1)S(1)}, u32[]{:S(2)}, u32[]{:S(2)}) collective-permute-start(bf16[2,40,1024]{2,1,0:T(8,128)(2,1)S(1)} %get-tuple-element.12.own), channel_id=1, source_target_pairs={{0,4},{2,6},{4,0},{6,2},{8,12},{10,14},{12,8},{14,10},{1,5},{3,7},... | collective-permute-start | bytes 491528 | tf_op jit(solution)/shard_map/ppermute | solution.py:26
  55.4 4.1 %collective-permute-done.5 = bf16[4,16,1024]{2,1,0:T(8,128)(2,1)S(1)} collective-permute-done((bf16[4,16,1024]{2,1,0:T(8,128)(2,1)S(1)}, bf16[4,16,1024]{2,1,0:T(8,128)(2,1)S(1)}, u32[]{:S(2)}, u32[]{:S(2)}) %collective-permute-start.5) | collective-permute-done | bytes 131104 | tf_op jit(solution)/shard_map/ppermute | solution.py:26
  59.5 2.2 %collective-permute-start.6 = (bf16[8,16,1024]{2,1,0:T(8,128)(2,1)S(1)}, bf16[8,16,1024]{2,1,0:T(8,128)(2,1)S(1)}, u32[]{:S(2)}, u32[]{:S(2)}) collective-permute-start(bf16[8,16,1024]{2,1,0:T(8,128)(2,1)S(1)} %constant_dynamic-update-slice_fusion.refs_2_), channel_id=1, source_target_pairs={{0,1},{1,0},{2,3},{3,2},{4,5},{5,4},{6,7},{7,6},{8,9},{9,8},{10,11... | collective-permute-start | bytes 786440 | tf_op jit(solution)/shard_map/ppermute | solution.py:26
  61.7 0.0 collective-permute-done.1.other
  61.8 0.3 collective-permute-start.2
  62.1 0.8 collective-permute-done.6.refs_3_
  62.9 0.0 all-to-all-done.1.refs_1_.refs_4_
  62.9 1.1 shard_map.133
  64.0 8.1 %all-to-all-start.2 = ((bf16[8,16,16,128]{3,2,1,0:T(8,128)(2,1)}), bf16[8,16,16,128]{3,2,1,0:T(8,128)(2,1)S(1)}, u32[]{:S(2)}, u32[]{:S(2)}) async-start(bf16[8,16,16,128]{3,2,1,0:T(8,128)(2,1)} %get-tuple-element.14), calls=%async_computation.2 | async-start | bytes 1048576 | tf_op jit(solution)/shard_map/all_to_all | solution.py:22
  72.1 0.0 collective-permute-done.2
  72.1 0.1 pad_maximum_fusion.refs_0_
  72.2 1.9 %collective-permute-start.3 = (bf16[8,40,1024]{2,1,0:T(8,128)(2,1)S(1)}, bf16[8,40,1024]{2,1,0:T(8,128)(2,1)S(1)}, u32[]{:S(2)}, u32[]{:S(2)}) collective-permute-start(bf16[8,40,1024]{2,1,0:T(8,128)(2,1)S(1)} %pad_maximum_fusion.refs_0_), channel_id=1, source_target_pairs={{0,1},{1,0},{2,3},{3,2},{4,5},{5,4},{6,7},{7,6},{8,9},{9,8},{10,11... | collective-permute-start | bytes 1966088 | tf_op jit(solution)/shard_map/ppermute | solution.py:26
  74.0 1.7 %collective-permute-done.3.refs_1_ = bf16[8,40,1024]{2,1,0:T(8,128)(2,1)S(1)} collective-permute-done((bf16[8,40,1024]{2,1,0:T(8,128)(2,1)S(1)}, bf16[8,40,1024]{2,1,0:T(8,128)(2,1)S(1)}, u32[]{:S(2)}, u32[]{:S(2)}) %collective-permute-start.3) | collective-permute-done | bytes 655392 | tf_op jit(solution)/shard_map/ppermute | solution.py:26
  75.8 12.3 %all-to-all-done.2.refs_5_ = bf16[8,16,16,128]{3,2,1,0:T(8,128)(2,1)S(1)} async-done(((bf16[8,16,16,128]{3,2,1,0:T(8,128)(2,1)}), bf16[8,16,16,128]{3,2,1,0:T(8,128)(2,1)S(1)}, u32[]{:S(2)}, u32[]{:S(2)}) %all-to-all-start.2) | async-done | bytes 524320 | tf_op jit(solution)/shard_map/all_to_all | solution.py:22
  88.1 0.9 shard_map.134
  89.0 14.3 %all_to_all.26.refs_0_ = bf16[8,200,128]{2,1,0:T(8,128)(2,1)S(1)} all-to-all(bf16[8,200,128]{2,1,0:T(8,128)(2,1)S(1)} %get-tuple-element.16), channel_id=1, replica_groups=mesh['parts'=2,'y'=8,'x'=8,'c'=2] {'y'}, dimensions={0} | all-to-all | bytes 819200 | tf_op jit(solution)/shard_map/all_to_all | solution.py:22
  103.3 0.8 shard_map.135
  104.1 0.0 copy-start
  104.1 7.5 %all-to-all-start.4 = ((bf16[16,40,128]{2,1,0:T(8,128)(2,1)}), bf16[16,40,128]{2,1,0:T(8,128)(2,1)S(1)}, u32[]{:S(2)}, u32[]{:S(2)}) async-start(bf16[16,40,128]{2,1,0:T(8,128)(2,1)} %shard_map.135), calls=%async_computation.4 | async-start | bytes 327680 | tf_op jit(solution)/shard_map/all_to_all | solution.py:22
  111.7 0.7 shard_map.136.refs_2_
  112.4 9.3 %all-to-all-done.4.refs_0_ = bf16[16,40,128]{2,1,0:T(8,128)(2,1)S(1)} async-done(((bf16[16,40,128]{2,1,0:T(8,128)(2,1)}), bf16[16,40,128]{2,1,0:T(8,128)(2,1)S(1)}, u32[]{:S(2)}, u32[]{:S(2)}) %all-to-all-start.4) | async-done | bytes 163872 | tf_op jit(solution)/shard_map/all_to_all | solution.py:22
  121.6 0.0 copy-done
  121.6 0.7 shard_map.137
  (6 shorter events, 0.1 us)
Async XLA Ops:
  34.7 28.2 %all-to-all-start.1 = ((bf16[8,16,16,128]{3,2,1,0:T(8,128)(2,1)}), bf16[8,16,16,128]{3,2,1,0:T(8,128)(2,1)S(1)}, u32[]{:S(2)}, u32[]{:S(2)}) async-start(bf16[8,16,16,128]{3,2,1,0:T(8,128)(2,1)} %shard_map.132), calls=%async_computation.1 | async-start | bytes 1048576 | tf_op jit(solution)/shard_map/all_to_all | solution.py:22
  39.4 9.6 %collective-permute-start = (bf16[56,1024]{1,0:T(8,128)(2,1)S(1)}, bf16[56,1024]{1,0:T(8,128)(2,1)S(1)}, u32[]{:S(2)}, u32[]{:S(2)}) collective-permute-start(bf16[56,1024]{1,0:T(8,128)(2,1)S(1)} %shard_map.128.own), channel_id=1, source_target_pairs={{0,8},{2,10},{4,12},{6,14},{8,0},{10,2},{12,4},{14,6},{1,9},{3,11}... | collective-permute-start | bytes 344072 | tf_op jit(solution)/shard_map/ppermute | solution.py:26
  49.0 5.0 %collective-permute-start.4 = (bf16[2,16,1024]{2,1,0:T(8,128)(2,1)S(1)}, bf16[2,16,1024]{2,1,0:T(8,128)(2,1)S(1)}, u32[]{:S(2)}, u32[]{:S(2)}) collective-permute-start(bf16[2,16,1024]{2,1,0:T(8,128)(2,1)S(1)} %get-tuple-element.13), channel_id=1, source_target_pairs={{0,4},{2,6},{4,0},{6,2},{8,12},{10,14},{12,8},{14,10},{1,5},{3,7},... | collective-permute-start | bytes 196616 | tf_op jit(solution)/shard_map/ppermute | solution.py:26
  54.0 5.6 %collective-permute-start.5 = (bf16[4,16,1024]{2,1,0:T(8,128)(2,1)S(1)}, bf16[4,16,1024]{2,1,0:T(8,128)(2,1)S(1)}, u32[]{:S(2)}, u32[]{:S(2)}) collective-permute-start(bf16[4,16,1024]{2,1,0:T(8,128)(2,1)S(1)} %pad_maximum_fusion.1), channel_id=1, source_target_pairs={{0,2},{2,0},{4,6},{6,4},{8,10},{10,8},{12,14},{14,12},{1,3},{3,1},... | collective-permute-start | bytes 393224 | tf_op jit(solution)/shard_map/ppermute | solution.py:26
  54.1 7.6 %collective-permute-start.1 = (bf16[2,40,1024]{2,1,0:T(8,128)(2,1)S(1)}, bf16[2,40,1024]{2,1,0:T(8,128)(2,1)S(1)}, u32[]{:S(2)}, u32[]{:S(2)}) collective-permute-start(bf16[2,40,1024]{2,1,0:T(8,128)(2,1)S(1)} %get-tuple-element.12.own), channel_id=1, source_target_pairs={{0,4},{2,6},{4,0},{6,2},{8,12},{10,14},{12,8},{14,10},{1,5},{3,7},... | collective-permute-start | bytes 491528 | tf_op jit(solution)/shard_map/ppermute | solution.py:26
  59.5 3.4 %collective-permute-start.6 = (bf16[8,16,1024]{2,1,0:T(8,128)(2,1)S(1)}, bf16[8,16,1024]{2,1,0:T(8,128)(2,1)S(1)}, u32[]{:S(2)}, u32[]{:S(2)}) collective-permute-start(bf16[8,16,1024]{2,1,0:T(8,128)(2,1)S(1)} %constant_dynamic-update-slice_fusion.refs_2_), channel_id=1, source_target_pairs={{0,1},{1,0},{2,3},{3,2},{4,5},{5,4},{6,7},{7,6},{8,9},{9,8},{10,11... | collective-permute-start | bytes 786440 | tf_op jit(solution)/shard_map/ppermute | solution.py:26
  61.8 10.3 %collective-permute-start.2 = (bf16[4,40,1024]{2,1,0:T(8,128)(2,1)S(1)}, bf16[4,40,1024]{2,1,0:T(8,128)(2,1)S(1)}, u32[]{:S(2)}, u32[]{:S(2)}) collective-permute-start(bf16[4,40,1024]{2,1,0:T(8,128)(2,1)S(1)} %shard_map.130), channel_id=1, source_target_pairs={{0,2},{2,0},{4,6},{6,4},{8,10},{10,8},{12,14},{14,12},{1,3},{3,1},... | collective-permute-start | bytes 983048 | tf_op jit(solution)/shard_map/ppermute | solution.py:26
  64.0 24.1 %all-to-all-start.2 = ((bf16[8,16,16,128]{3,2,1,0:T(8,128)(2,1)}), bf16[8,16,16,128]{3,2,1,0:T(8,128)(2,1)S(1)}, u32[]{:S(2)}, u32[]{:S(2)}) async-start(bf16[8,16,16,128]{3,2,1,0:T(8,128)(2,1)} %get-tuple-element.14), calls=%async_computation.2 | async-start | bytes 1048576 | tf_op jit(solution)/shard_map/all_to_all | solution.py:22
  72.2 3.6 %collective-permute-start.3 = (bf16[8,40,1024]{2,1,0:T(8,128)(2,1)S(1)}, bf16[8,40,1024]{2,1,0:T(8,128)(2,1)S(1)}, u32[]{:S(2)}, u32[]{:S(2)}) collective-permute-start(bf16[8,40,1024]{2,1,0:T(8,128)(2,1)S(1)} %pad_maximum_fusion.refs_0_), channel_id=1, source_target_pairs={{0,1},{1,0},{2,3},{3,2},{4,5},{5,4},{6,7},{7,6},{8,9},{9,8},{10,11... | collective-permute-start | bytes 1966088 | tf_op jit(solution)/shard_map/ppermute | solution.py:26
  104.1 17.5 %copy-start = (f32[8,1024]{1,0:T(8,128)S(1)}, f32[8,1024]{1,0:T(8,128)}, u32[]{:S(2)}) copy-start(f32[8,1024]{1,0:T(8,128)} %refs_1_.5) | copy-start | bytes 98308
  104.1 17.5 %all-to-all-start.4 = ((bf16[16,40,128]{2,1,0:T(8,128)(2,1)}), bf16[16,40,128]{2,1,0:T(8,128)(2,1)S(1)}, u32[]{:S(2)}, u32[]{:S(2)}) async-start(bf16[16,40,128]{2,1,0:T(8,128)(2,1)} %shard_map.135), calls=%async_computation.4 | async-start | bytes 327680 | tf_op jit(solution)/shard_map/all_to_all | solution.py:22

commit v6 on v5

--- a/solution.py
+++ b/solution.py
@@ -176,10 +176,12 @@
 
 
 def main_kernel(
-    rt, rp, near, far, par_own, par_other, tall, step_j, cols, step, slots, part, db
+    near, far, par_own, par_other, tall, step_j, cols, step, slots, part_near, part_far, db
 ):
-    w1 = near.shape[-1]
+    count, _, w1 = near.shape
     ny, nj = tall.shape[:2]
+    rt = par_own.shape[1]
+    rp = rt // 2
     x_me, c_me = lax.axis_index("x"), lax.axis_index("c")
     kid_par_j = kid_par_columns(tall)
     par_j = tall[:, :, rp : 2 * rp, :].astype(F32).reshape(ny * nj, 1, rp, LANES)
@@ -190,19 +192,20 @@
     var = jnp.zeros((1, LANES), F32)
     xs = []
     for bc, chunks in enumerate((near, far)):
-        count = chunks.shape[0]
         s0 = chunks[:, 0:rt, :].reshape(count * rt, w1)
         s1 = chunks[:, rt : 2 * rt, :].reshape(count * rt, w1)
         d = chunks[:, 2 * rt : 2 * rt + rp, :].astype(F32).reshape(count * rp, w1)
         x = dot(s0, both[:w1]) + dot(s1, both[w1:])
         db_own = dot(d.astype(BF16), kid_par_j)
         for k in range(count):
-            at = chunk_place(x_me, c_me, (k // 4, (k // 2) % 2, k % 2, bc))
+            b1, b2, b4 = k // 4, (k // 2) % 2, k % 2
+            at = chunk_place(x_me, c_me, (b1, b2, b4, bc))
+            part, to = (part_near, part_far)[b4], 4 * b2 + 2 * b1 + bc
             piece = x[k * rt : (k + 1) * rt]
             kt = piece[:, :LANES].astype(BF16)
-            part[at, 0:rt, :] = kt
+            part[to, 0:rt, :] = kt
             c = piece[:, LANES:]
-            part[at, rt : rt + rp, :] = low_high(c[:rp], turned(c[rp:])).astype(BF16)
+            part[to, rt : rt + rp, :] = low_high(c[:rp], turned(c[rp:])).astype(BF16)
             db_k = db_own[k * rp : (k + 1) * rp]
             db[at] = db_k
             var = var + jnp.sum(step[at] * kt.astype(F32), axis=0, keepdims=True)
@@ -211,65 +214,85 @@
 
     x = jnp.concatenate(xs, axis=0)
     p = jnp.concatenate([p[...].reshape(nj // 2 * rt, w1) for p in (par_own, par_other)], axis=0)
+    var_rows = jnp.concatenate(split3(var) + [jnp.zeros((rp - 3, LANES), F32)], axis=0)
+    db_here = db[...].reshape(nj * rp, LANES)
+    nx = nj // 2
     for y in range(ny):
         partial = dot_t(p[:, y * LANES : (y + 1) * LANES], x)
-        rows = partial.shape[0]
-        slots[y, 0:rows, :] = partial[:, :LANES].astype(BF16)
-        q = partial[:, LANES:]
-        q = low_high(q[: rows // 2], turned(q[rows // 2 :]))
-        slots[y, rows : rows + rows // 2, :] = q.astype(BF16)
-    var_rows = jnp.concatenate(split3(var) + [jnp.zeros((5, LANES), F32)], axis=0).astype(BF16)
-    for y in range(ny):
-        slots[y, rows + rows // 2 : rows + rows // 2 + 8, :] = var_rows
-
-
-def sum_kernel(rt, rp, received, db, part, out):
-    ny = received.shape[0]
-    nj = out.shape[0]
-    rows = nj * rp
-    total = received[0].astype(F32)
-    for y in range(1, ny):
-        total = total + received[y].astype(F32)
-    q = total[rows : rows + rows // 2]
-    q = jnp.concatenate([q, turned(q)], axis=0)
-    first = rows + rows // 2
-    var = total[first : first + 1] + total[first + 1 : first + 2] + total[first + 2 : first + 3]
-    var_rows = []
-    for top in split3(var):
-        var_rows += [turned(top), top]
-    var_rows = jnp.concatenate(var_rows + [jnp.zeros((2, LANES), F32)], axis=0)
-    for j in range(nj):
-        at = slice(j * rp, (j + 1) * rp)
-        out[j, 0 : rt + rp, :] = part[j]
-        kp = total[at] + db[j]
-        out[j, rt + rp : rt + 3 * rp, :] = jnp.concatenate(
-            [kp, low_high(q[at], var_rows)], axis=0
-        ).astype(BF16)
-
-
-def final_kernel(rt, rp, got, dinv, dvar, cross_par, sigma_par, kid_top, kid_par, variance):
-    nj = got.shape[0]
+        kp = partial[:, :LANES] + jnp.where(lax.axis_index("y") == y, db_here, 0.0)
+        for i in range(nx):
+            slots[y * nx + i, 0:rt, :] = kp[i * rt : (i + 1) * rt].astype(BF16)
+            q = partial[i * rt : (i + 1) * rt, LANES:]
+            q = low_high(q[:rp], turned(q[rp:]))
+            slots[y * nx + i, rt : 2 * rt, :] = jnp.concatenate([q, var_rows], axis=0).astype(BF16)
+
+
+def top_kernel(own, other, kid_top, cross_par):
+    count, rows, _ = own.shape
+    rp = rows // 3
+    rt = 2 * rp
+    kids = kid_top.shape[0]
+    per_kid = 2 * count // kids
+    x_me, c_me = lax.axis_index("x"), lax.axis_index("c")
+    first = c_me == 0
+    for k in range(count):
+        chip = jnp.bitwise_xor(x_me, k // 4 + 2 * ((k // 2) % 2) + 4 * (k % 2))
+        a = jnp.where(first, own[k], other[k])
+        b = jnp.where(first, other[k], own[k])
+        kid = lax.div(2 * chip, per_kid)
+        block = lax.rem(2 * chip, per_kid)
+        for i, slot in enumerate((a, b)):
+            at = pl.ds(pl.multiple_of((block + i) * LANES, LANES), LANES)
+            kid_top[kid, :, at] = slot[0:rt]
+        a, b = a[rt:].astype(F32), b[rt:].astype(F32)
+        at = pl.ds(pl.multiple_of(chip * LANES, LANES), LANES)
+        c = jnp.concatenate([low_high(a, turned(b)), low_high(turned(a), b)], axis=0)
+        cross_par[:, at] = c.astype(BF16)
+
+
+def sum_kernel(received, keep, send):
+    nx = keep.shape[0]
+    rp = keep.shape[1] // 2
+    first = lax.axis_index("c") == 0
+    for i in range(nx):
+        total = received[i].astype(F32)
+        for y in range(1, received.shape[0] // nx):
+            total = total + received[y * nx + i].astype(F32)
+        kp_0, kp_1 = total[:rp], total[rp : 2 * rp]
+        q_0 = total[2 * rp : 3 * rp]
+        q_1 = turned(q_0)
+        var = total[3 * rp : 3 * rp + 1] + total[3 * rp + 1 : 3 * rp + 2]
+        var = var + total[3 * rp + 2 : 3 * rp + 3]
+        var_rows = []
+        for top in split3(var):
+            var_rows += [turned(top), top]
+        var_rows = jnp.concatenate(var_rows + [jnp.zeros((2, LANES), F32)], axis=0)
+        low = jnp.concatenate([kp_0, low_high(q_0, var_rows)], axis=0)
+        high = jnp.concatenate([kp_1, low_high(q_1, var_rows)], axis=0)
+        keep[i] = jnp.where(first, low, high).astype(BF16)
+        send[i] = jnp.where(first, high, low).astype(BF16)
+
+
+def final_kernel(keep, got, dinv, dvar, sigma_par, kid_par, variance):
+    nx = keep.shape[0]
+    rp = dinv.shape[0]
     kids = dvar.shape[0]
-    per_kid = nj // kids
-    for j in range(nj):
-        k, m = divmod(j, per_kid)
-        at = slice(m * LANES, (m + 1) * LANES)
-        kid_top[k, :, at] = got[j, 0:rt, :]
-        kid_par[k, :, at] = got[j, rt + rp : rt + 2 * rp, :]
-        v = got[j, rt + 2 * rp : rt + 3 * rp, :].astype(F32)
-        low = v[0:1] + v[2:3] + v[4:5]
-        high = v[1:2] + v[3:4] + v[5:6]
-        variance[k : k + 1, at] = dvar[k : k + 1, at] + low_high(turned(low), high)
-    for m in range(nj // 2):
-        at = slice(m * LANES, (m + 1) * LANES)
-        a = got[2 * m, rt : rt + rp, :].astype(F32)
-        b = got[2 * m + 1, rt : rt + rp, :].astype(F32)
-        cross_par[:, at] = jnp.concatenate(
-            [low_high(a, turned(b)), low_high(turned(a), b)], axis=0
-        ).astype(BF16)
-        a = got[2 * m, rt + 2 * rp : rt + 3 * rp, :].astype(F32)
-        b = got[2 * m + 1, rt + 2 * rp : rt + 3 * rp, :].astype(F32)
-        sigma_par[:, at] = (dinv[:, at] + low_high(a, turned(b))).astype(BF16)
+    per_kid = 2 * nx // kids
+    first = lax.axis_index("c") == 0
+    for i in range(nx):
+        mine, others = keep[i].astype(F32), got[i].astype(F32)
+        a = jnp.where(first, mine, others)
+        b = jnp.where(first, others, mine)
+        for j, slot in ((2 * i, a), (2 * i + 1, b)):
+            k, m = divmod(j, per_kid)
+            at = slice(m * LANES, (m + 1) * LANES)
+            kid_par[k, :, at] = slot[:rp].astype(BF16)
+            v = slot[rp:]
+            low = v[0:1] + v[2:3] + v[4:5]
+            high = v[1:2] + v[3:4] + v[5:6]
+            variance[k : k + 1, at] = dvar[k : k + 1, at] + low_high(turned(low), high)
+        at = slice(i * LANES, (i + 1) * LANES)
+        sigma_par[:, at] = (dinv[:, at] + low_high(a[rp:], turned(b[rp:]))).astype(BF16)
 
 
 def device_part(
@@ -340,28 +363,35 @@
         (cols, tall, par_own, par_other),
     )
     step_j = exchanged(send, "y")
-    rows4 = nj * rp + nj * rp // 2 + 8
-    slots4, part, db = call(
-        sized(main_kernel),
-        [((ny, rows4, LANES), BF16), ((nj, rt + rp, LANES), BF16), ((nj, rp, LANES), F32)],
+    slot = (rt + rp, LANES)
+    slots, part_near, part_far = call(
+        main_kernel,
+        [((ny * nx, 2 * rt, LANES), BF16), ((nj // 2, *slot), BF16), ((nj // 2, *slot), BF16)],
         (near, far, par_own, par_other, tall, step_j, cols, step),
-    )
-    received = exchanged(slots4, "y")
-    (out,) = call(
-        sized(sum_kernel), [((nj, rt + 3 * rp, LANES), BF16)], (received, db, part)
-    )
-    got = exchanged(out, XC)
-    return call(
-        sized(final_kernel),
-        [
-            ((rt, w1), BF16),
-            ((rp, w1), BF16),
-            ((kids, rt, w2), BF16),
-            ((kids, rp, w2), BF16),
-            ((kids, w2), F32),
-        ],
-        (got, dinv_par, dvar_kid),
-    )
+        scratch=[pltpu.VMEM((nj, rp, LANES), F32)],
+    )
+    received = exchanged(slots, ("y", "x"))
+    got = swapped(part_far, "x", 4)
+    held = jnp.stack([part_near, got]).reshape(2, 2, 4, *slot)
+    got = swapped(held[:, 1], "x", 2)
+    held = jnp.stack([held[:, 0], got]).reshape(2, 2, 2, 2, *slot)
+    got = swapped(held[:, :, 1], "x", 1)
+    held = jnp.stack([held[:, :, 0], got])
+    got = swapped(held[:, :, :, 1], "c", 1)
+    own = held[:, :, :, 0].reshape(nj // 2, *slot)
+    cross_kid_top, cross_par = call(
+        top_kernel,
+        [((kids, rt, w2), BF16), ((rt, w1), BF16)],
+        (own, got.reshape(nj // 2, *slot)),
+    )
+    keep, send = call(sum_kernel, [((nx, rt, LANES), BF16)] * 2, (received,))
+    got = swapped(send, "c", 1)
+    sigma_par, cross_kid_par, variance_kid = call(
+        final_kernel,
+        [((rp, w1), BF16), ((kids, rp, w2), BF16), ((kids, w2), F32)],
+        (keep, got, dinv_par, dvar_kid),
+    )
+    return cross_par, sigma_par, cross_kid_top, cross_kid_par, variance_kid
 
 
 def solution(mesh):

time: 123 us -> 127 us (1.033)
  blocking collectives: 46.4 us -> 32.1 us
  starting transfers between devices: 26.1 us -> 37.4 us
  waiting for transfers between devices: 41.9 us -> 48.2 us
    ppermute x7 -> x12, waiting for transfers between devices: 20.3 us -> 35.8 us  [swapped(): lax.ppermute(x, axis, [(i, i ^ bit) for i in range(lax.axis_size(axis))])]
    all_to_all x2 -> x1, blocking collectives: 46.4 us -> 32.1 us  [exchanged(): return lax.all_to_all(x, axes, split_axis=0, concat_axis=0, tiled=True)]
    ppermute x7 -> x12, starting transfers between devices: 6.73 us -> 19.1 us  [swapped(): lax.ppermute(x, axis, [(i, i ^ bit) for i in range(lax.axis_size(axis))])]
    all_to_all x3, waiting for transfers between devices: 21.6 us -> 12.3 us  [exchanged(): return lax.all_to_all(x, axes, split_axis=0, concat_axis=0, tiled=True)]
    pallas_call x10 -> x11, Pallas kernels: 7.18 us -> 7.24 us  [call(): pl.pallas_call(kernel, out_shape=tuple((jax.ShapeDtypeStruct(s, d) for s,...]
  transfers between devices with their start and end apart: 10 -> 15, of which waited for: 7 -> 9; matrix products, arithmetic and copies ran while one was open for 0% -> 0% of each run, Pallas kernels for 2% -> 3%
where the time goes in v6:
time: 127 us
  waiting for transfers between devices  48.2 us (38%)
  starting transfers between devices  37.4 us (29%)
  blocking collectives  32.1 us (25%)
  Pallas kernels  7.24 us (6%)
    ppermute x12, waiting for transfers between devices, swapped(): lax.ppermute(x, axis, [(i, i ^ bit) for i in range(lax.axis_size(axis))])  35.8 us
    all_to_all x1, blocking collectives, exchanged(): return lax.all_to_all(x, axes, split_axis=0, concat_axis=0, tiled=True)  32.1 us
    ppermute x12, starting transfers between devices, swapped(): lax.ppermute(x, axis, [(i, i ^ bit) for i in range(lax.axis_size(axis))])  19.1 us
    all_to_all x3, starting transfers between devices, exchanged(): return lax.all_to_all(x, axes, split_axis=0, concat_axis=0, tiled=True)  18.3 us
    all_to_all x3, waiting for transfers between devices, exchanged(): return lax.all_to_all(x, axes, split_axis=0, concat_axis=0, tiled=True)  12.3 us
    pallas_call x11, Pallas kernels, call(): pl.pallas_call(kernel, out_shape=tuple((jax.ShapeDtypeStruct(s, d) for s,...  7.24 us
  transfers between devices with their start and end apart: 15, of which 9 were waited for; matrix products, arithmetic and copies ran while one was open for 0% of the time, Pallas kernels for 3%

profile of v6, /device:TPU:513, one launch (start us, length us, event | category | flops | bytes accessed | tf_op | source)
XLA Modules:
  0.0 126.7 jit_solution(10023382591661175382)
XLA Ops:
  0.6 1.1 shard_map.131
  1.7 32.1 %all_to_all.20.cols.refs_0_ = bf16[16,32,128]{2,1,0:T(8,128)(2,1)S(1)} all-to-all(bf16[16,32,128]{2,1,0:T(8,128)(2,1)S(1)} %shard_map.131), channel_id=1, replica_groups=mesh['parts'=2,'y'=8,'x'=8,'c'=2] {'x','c'}, dimensions={0} | all-to-all | bytes 262144 | tf_op jit(solution)/shard_map/all_to_all | solution.py:22
  33.8 0.9 shard_map.132
  34.7 3.7 %all-to-all-start.1 = ((bf16[8,16,16,128]{3,2,1,0:T(8,128)(2,1)}), bf16[8,16,16,128]{3,2,1,0:T(8,128)(2,1)S(1)}, u32[]{:S(2)}, u32[]{:S(2)}) async-start(bf16[8,16,16,128]{3,2,1,0:T(8,128)(2,1)} %shard_map.132), calls=%async_computation.1 | async-start | bytes 1048576 | tf_op jit(solution)/shard_map/all_to_all | solution.py:22
  38.4 1.0 shard_map.128.own
  39.4 0.7 collective-permute-start
  40.1 8.9 %collective-permute-done.other = bf16[56,1024]{1,0:T(8,128)(2,1)S(1)} collective-permute-done((bf16[56,1024]{1,0:T(8,128)(2,1)S(1)}, bf16[56,1024]{1,0:T(8,128)(2,1)S(1)}, u32[]{:S(2)}, u32[]{:S(2)}) %collective-permute-start) | collective-permute-done | bytes 114720 | tf_op jit(solution)/shard_map/ppermute | solution.py:26
  49.0 0.1 collective-permute-start.4
  49.1 4.8 %collective-permute-done.4 = bf16[2,16,1024]{2,1,0:T(8,128)(2,1)S(1)} collective-permute-done((bf16[2,16,1024]{2,1,0:T(8,128)(2,1)S(1)}, bf16[2,16,1024]{2,1,0:T(8,128)(2,1)S(1)}, u32[]{:S(2)}, u32[]{:S(2)}) %collective-permute-start.4) | collective-permute-done | bytes 65568 | tf_op jit(solution)/shard_map/ppermute | solution.py:26
  54.0 0.1 collective-permute-start.5
  54.1 1.3 %collective-permute-start.1 = (bf16[2,40,1024]{2,1,0:T(8,128)(2,1)S(1)}, bf16[2,40,1024]{2,1,0:T(8,128)(2,1)S(1)}, u32[]{:S(2)}, u32[]{:S(2)}) collective-permute-start(bf16[2,40,1024]{2,1,0:T(8,128)(2,1)S(1)} %get-tuple-element.19.own), channel_id=1, source_target_pairs={{0,4},{2,6},{4,0},{6,2},{8,12},{10,14},{12,8},{14,10},{1,5},{3,7},... | collective-permute-start | bytes 491528 | tf_op jit(solution)/shard_map/ppermute | solution.py:26
  55.5 4.1 %collective-permute-done.5 = bf16[4,16,1024]{2,1,0:T(8,128)(2,1)S(1)} collective-permute-done((bf16[4,16,1024]{2,1,0:T(8,128)(2,1)S(1)}, bf16[4,16,1024]{2,1,0:T(8,128)(2,1)S(1)}, u32[]{:S(2)}, u32[]{:S(2)}) %collective-permute-start.5) | collective-permute-done | bytes 131104 | tf_op jit(solution)/shard_map/ppermute | solution.py:26
  59.5 2.2 %collective-permute-start.6 = (bf16[8,16,1024]{2,1,0:T(8,128)(2,1)S(1)}, bf16[8,16,1024]{2,1,0:T(8,128)(2,1)S(1)}, u32[]{:S(2)}, u32[]{:S(2)}) collective-permute-start(bf16[8,16,1024]{2,1,0:T(8,128)(2,1)S(1)} %constant_dynamic-update-slice_fusion.refs_2_.par_own), channel_id=1, source_target_pairs={{0,1},{1,0},{2,3},{3,2},{4,5},{5,4},{6,7},{7,6},{8,9},{9,8},{10,11... | collective-permute-start | bytes 786440 | tf_op jit(solution)/shard_map/ppermute | solution.py:26
  61.8 0.0 collective-permute-done.1.other
  61.8 0.3 collective-permute-start.2
  62.1 0.8 collective-permute-done.6.refs_3_.par_other
  62.9 0.0 all-to-all-done.1.refs_1_.tall
  62.9 1.1 shard_map.133
  64.1 8.1 %all-to-all-start.2 = ((bf16[8,16,16,128]{3,2,1,0:T(8,128)(2,1)}), bf16[8,16,16,128]{3,2,1,0:T(8,128)(2,1)S(1)}, u32[]{:S(2)}, u32[]{:S(2)}) async-start(bf16[8,16,16,128]{3,2,1,0:T(8,128)(2,1)} %get-tuple-element.21), calls=%async_computation.2 | async-start | bytes 1048576 | tf_op jit(solution)/shard_map/all_to_all | solution.py:22
  72.1 0.0 collective-permute-done.2
  72.2 0.1 pad_maximum_fusion.near
  72.2 1.9 %collective-permute-start.3 = (bf16[8,40,1024]{2,1,0:T(8,128)(2,1)S(1)}, bf16[8,40,1024]{2,1,0:T(8,128)(2,1)S(1)}, u32[]{:S(2)}, u32[]{:S(2)}) collective-permute-start(bf16[8,40,1024]{2,1,0:T(8,128)(2,1)S(1)} %pad_maximum_fusion.near), channel_id=1, source_target_pairs={{0,1},{1,0},{2,3},{3,2},{4,5},{5,4},{6,7},{7,6},{8,9},{9,8},{10,11... | collective-permute-start | bytes 1966088 | tf_op jit(solution)/shard_map/ppermute | solution.py:26
  74.1 1.7 %collective-permute-done.3.far = bf16[8,40,1024]{2,1,0:T(8,128)(2,1)S(1)} collective-permute-done((bf16[8,40,1024]{2,1,0:T(8,128)(2,1)S(1)}, bf16[8,40,1024]{2,1,0:T(8,128)(2,1)S(1)}, u32[]{:S(2)}, u32[]{:S(2)}) %collective-permute-start.3) | collective-permute-done | bytes 655392 | tf_op jit(solution)/shard_map/ppermute | solution.py:26
  75.8 12.3 %all-to-all-done.2.step_j = bf16[8,16,16,128]{3,2,1,0:T(8,128)(2,1)S(1)} async-done(((bf16[8,16,16,128]{3,2,1,0:T(8,128)(2,1)}), bf16[8,16,16,128]{3,2,1,0:T(8,128)(2,1)S(1)}, u32[]{:S(2)}, u32[]{:S(2)}) %all-to-all-start.2) | async-done | bytes 524320 | tf_op jit(solution)/shard_map/all_to_all | solution.py:22
  88.1 0.9 shard_map.134
  89.0 0.0 copy-start
  89.0 0.8 copy-done
  89.9 6.5 %all-to-all-start.3 = ((bf16[64,32,128]{2,1,0:T(8,128)(2,1)}), bf16[64,32,128]{2,1,0:T(8,128)(2,1)S(1)}, u32[]{:S(2)}, u32[]{:S(2)}) async-start(bf16[64,32,128]{2,1,0:T(8,128)(2,1)} %copy-done), calls=%async_computation.3 | async-start | bytes 1048576 | tf_op jit(solution)/shard_map/all_to_all | solution.py:22
  96.4 3.9 %collective-permute-start.7 = (bf16[8,24,128]{2,1,0:T(8,128)(2,1)S(1)}, bf16[8,24,128]{2,1,0:T(8,128)(2,1)S(1)}, u32[]{:S(2)}, u32[]{:S(2)}) collective-permute-start(bf16[8,24,128]{2,1,0:T(8,128)(2,1)S(1)} %get-tuple-element.24), channel_id=1, source_target_pairs={{0,8},{2,10},{4,12},{6,14},{8,0},{10,2},{12,4},{14,6},{1,9},{3,11}... | collective-permute-start | bytes 147464 | tf_op jit(solution)/shard_map/ppermute | solution.py:26
  100.3 10.0 %collective-permute-done.7 = bf16[8,24,128]{2,1,0:T(8,128)(2,1)S(1)} collective-permute-done((bf16[8,24,128]{2,1,0:T(8,128)(2,1)S(1)}, bf16[8,24,128]{2,1,0:T(8,128)(2,1)S(1)}, u32[]{:S(2)}, u32[]{:S(2)}) %collective-permute-start.7) | collective-permute-done | bytes 49184 | tf_op jit(solution)/shard_map/ppermute | solution.py:26
  110.2 0.1 collective-permute-start.8
  110.4 4.1 %collective-permute-done.8 = bf16[2,4,24,128]{3,2,1,0:T(8,128)(2,1)S(1)} collective-permute-done((bf16[2,4,24,128]{3,2,1,0:T(8,128)(2,1)S(1)}, bf16[2,4,24,128]{3,2,1,0:T(8,128)(2,1)S(1)}, u32[]{:S(2)}, u32[]{:S(2)}) %collective-permute-start.8) | collective-permute-done | bytes 49184 | tf_op jit(solution)/shard_map/ppermute | solution.py:26
  114.5 1.8 %collective-permute-start.9 = (bf16[2,2,2,24,128]{4,3,1,0,2:T(8,128)(2,1)S(1)}, bf16[2,2,2,24,128]{4,3,1,0,2:T(8,128)(2,1)S(1)}, u32[]{:S(2)}, u32[]{:S(2)}) collective-permute-start(bf16[2,2,2,24,128]{4,3,1,0,2:T(8,128)(2,1)S(1)} %get-tuple-element.35), channel_id=1, source_target_pairs={{0,2},{2,0},{4,6},{6,4},{8,10},{10,8},{12,14},{14,12},{1,3},{3,1},... | collective-permute-start | bytes 147464 | tf_op jit(solution)/shard_map/ppermute | solution.py:26
  116.3 1.5 %collective-permute-done.9 = bf16[2,2,2,24,128]{4,3,1,0,2:T(8,128)(2,1)S(1)} collective-permute-done((bf16[2,2,2,24,128]{4,3,1,0,2:T(8,128)(2,1)S(1)}, bf16[2,2,2,24,128]{4,3,1,0,2:T(8,128)(2,1)S(1)}, u32[]{:S(2)}, u32[]{:S(2)}) %collective-permute-start.9) | collective-permute-done | bytes 49184 | tf_op jit(solution)/shard_map/ppermute | solution.py:26
  117.8 6.4 %collective-permute-start.10 = (bf16[2,2,2,24,128]{4,3,2,1,0:T(8,128)(2,1)S(1)}, bf16[2,2,2,24,128]{4,3,2,1,0:T(8,128)(2,1)S(1)}, u32[]{:S(2)}, u32[]{:S(2)}) collective-permute-start(bf16[2,2,2,24,128]{4,3,2,1,0:T(8,128)(2,1)S(1)} %get-tuple-element.33), channel_id=1, source_target_pairs={{0,1},{1,0},{2,3},{3,2},{4,5},{5,4},{6,7},{7,6},{8,9},{9,8},{10,11... | collective-permute-start | bytes 147464 | tf_op jit(solution)/shard_map/ppermute | solution.py:26
  124.2 0.0 all-to-all-done.3.received
  124.2 0.1 shard_map.136
  124.3 0.2 collective-permute-start.11
  124.5 0.7 shard_map.137.dvar
  125.2 0.0 collective-permute-done.10
  125.2 0.0 copy-start.1
  125.2 0.7 shard_map.135
  125.9 0.0 collective-permute-done.11.got
  125.9 0.0 copy-done.1
  126.0 0.7 shard_map.138
  (11 shorter events, 0.1 us)
Async XLA Ops:
  34.7 28.2 %all-to-all-start.1 = ((bf16[8,16,16,128]{3,2,1,0:T(8,128)(2,1)}), bf16[8,16,16,128]{3,2,1,0:T(8,128)(2,1)S(1)}, u32[]{:S(2)}, u32[]{:S(2)}) async-start(bf16[8,16,16,128]{3,2,1,0:T(8,128)(2,1)} %shard_map.132), calls=%async_computation.1 | async-start | bytes 1048576 | tf_op jit(solution)/shard_map/all_to_all | solution.py:22
  39.4 9.6 %collective-permute-start = (bf16[56,1024]{1,0:T(8,128)(2,1)S(1)}, bf16[56,1024]{1,0:T(8,128)(2,1)S(1)}, u32[]{:S(2)}, u32[]{:S(2)}) collective-permute-start(bf16[56,1024]{1,0:T(8,128)(2,1)S(1)} %shard_map.128.own), channel_id=1, source_target_pairs={{0,8},{2,10},{4,12},{6,14},{8,0},{10,2},{12,4},{14,6},{1,9},{3,11}... | collective-permute-start | bytes 344072 | tf_op jit(solution)/shard_map/ppermute | solution.py:26
  49.0 5.0 %collective-permute-start.4 = (bf16[2,16,1024]{2,1,0:T(8,128)(2,1)S(1)}, bf16[2,16,1024]{2,1,0:T(8,128)(2,1)S(1)}, u32[]{:S(2)}, u32[]{:S(2)}) collective-permute-start(bf16[2,16,1024]{2,1,0:T(8,128)(2,1)S(1)} %get-tuple-element.20), channel_id=1, source_target_pairs={{0,4},{2,6},{4,0},{6,2},{8,12},{10,14},{12,8},{14,10},{1,5},{3,7},... | collective-permute-start | bytes 196616 | tf_op jit(solution)/shard_map/ppermute | solution.py:26
  54.0 5.6 %collective-permute-start.5 = (bf16[4,16,1024]{2,1,0:T(8,128)(2,1)S(1)}, bf16[4,16,1024]{2,1,0:T(8,128)(2,1)S(1)}, u32[]{:S(2)}, u32[]{:S(2)}) collective-permute-start(bf16[4,16,1024]{2,1,0:T(8,128)(2,1)S(1)} %pad_maximum_fusion.1), channel_id=1, source_target_pairs={{0,2},{2,0},{4,6},{6,4},{8,10},{10,8},{12,14},{14,12},{1,3},{3,1},... | collective-permute-start | bytes 393224 | tf_op jit(solution)/shard_map/ppermute | solution.py:26
  54.1 7.6 %collective-permute-start.1 = (bf16[2,40,1024]{2,1,0:T(8,128)(2,1)S(1)}, bf16[2,40,1024]{2,1,0:T(8,128)(2,1)S(1)}, u32[]{:S(2)}, u32[]{:S(2)}) collective-permute-start(bf16[2,40,1024]{2,1,0:T(8,128)(2,1)S(1)} %get-tuple-element.19.own), channel_id=1, source_target_pairs={{0,4},{2,6},{4,0},{6,2},{8,12},{10,14},{12,8},{14,10},{1,5},{3,7},... | collective-permute-start | bytes 491528 | tf_op jit(solution)/shard_map/ppermute | solution.py:26
  59.5 3.4 %collective-permute-start.6 = (bf16[8,16,1024]{2,1,0:T(8,128)(2,1)S(1)}, bf16[8,16,1024]{2,1,0:T(8,128)(2,1)S(1)}, u32[]{:S(2)}, u32[]{:S(2)}) collective-permute-start(bf16[8,16,1024]{2,1,0:T(8,128)(2,1)S(1)} %constant_dynamic-update-slice_fusion.refs_2_.par_own), channel_id=1, source_target_pairs={{0,1},{1,0},{2,3},{3,2},{4,5},{5,4},{6,7},{7,6},{8,9},{9,8},{10,11... | collective-permute-start | bytes 786440 | tf_op jit(solution)/shard_map/ppermute | solution.py:26
  61.8 10.4 %collective-permute-start.2 = (bf16[4,40,1024]{2,1,0:T(8,128)(2,1)S(1)}, bf16[4,40,1024]{2,1,0:T(8,128)(2,1)S(1)}, u32[]{:S(2)}, u32[]{:S(2)}) collective-permute-start(bf16[4,40,1024]{2,1,0:T(8,128)(2,1)S(1)} %shard_map.130), channel_id=1, source_target_pairs={{0,2},{2,0},{4,6},{6,4},{8,10},{10,8},{12,14},{14,12},{1,3},{3,1},... | collective-permute-start | bytes 983048 | tf_op jit(solution)/shard_map/ppermute | solution.py:26
  64.1 24.1 %all-to-all-start.2 = ((bf16[8,16,16,128]{3,2,1,0:T(8,128)(2,1)}), bf16[8,16,16,128]{3,2,1,0:T(8,128)(2,1)S(1)}, u32[]{:S(2)}, u32[]{:S(2)}) async-start(bf16[8,16,16,128]{3,2,1,0:T(8,128)(2,1)} %get-tuple-element.21), calls=%async_computation.2 | async-start | bytes 1048576 | tf_op jit(solution)/shard_map/all_to_all | solution.py:22
  72.2 3.6 %collective-permute-start.3 = (bf16[8,40,1024]{2,1,0:T(8,128)(2,1)S(1)}, bf16[8,40,1024]{2,1,0:T(8,128)(2,1)S(1)}, u32[]{:S(2)}, u32[]{:S(2)}) collective-permute-start(bf16[8,40,1024]{2,1,0:T(8,128)(2,1)S(1)} %pad_maximum_fusion.near), channel_id=1, source_target_pairs={{0,1},{1,0},{2,3},{3,2},{4,5},{5,4},{6,7},{7,6},{8,9},{9,8},{10,11... | collective-permute-start | bytes 1966088 | tf_op jit(solution)/shard_map/ppermute | solution.py:26
  89.0 0.8 copy-start
  89.9 34.3 %all-to-all-start.3 = ((bf16[64,32,128]{2,1,0:T(8,128)(2,1)}), bf16[64,32,128]{2,1,0:T(8,128)(2,1)S(1)}, u32[]{:S(2)}, u32[]{:S(2)}) async-start(bf16[64,32,128]{2,1,0:T(8,128)(2,1)} %copy-done), calls=%async_computation.3 | async-start | bytes 1048576 | tf_op jit(solution)/shard_map/all_to_all | solution.py:22
  96.4 13.9 %collective-permute-start.7 = (bf16[8,24,128]{2,1,0:T(8,128)(2,1)S(1)}, bf16[8,24,128]{2,1,0:T(8,128)(2,1)S(1)}, u32[]{:S(2)}, u32[]{:S(2)}) collective-permute-start(bf16[8,24,128]{2,1,0:T(8,128)(2,1)S(1)} %get-tuple-element.24), channel_id=1, source_target_pairs={{0,8},{2,10},{4,12},{6,14},{8,0},{10,2},{12,4},{14,6},{1,9},{3,11}... | collective-permute-start | bytes 147464 | tf_op jit(solution)/shard_map/ppermute | solution.py:26
  110.2 4.3 %collective-permute-start.8 = (bf16[2,4,24,128]{3,2,1,0:T(8,128)(2,1)S(1)}, bf16[2,4,24,128]{3,2,1,0:T(8,128)(2,1)S(1)}, u32[]{:S(2)}, u32[]{:S(2)}) collective-permute-start(bf16[2,4,24,128]{3,2,1,0:T(8,128)(2,1)S(1)} %get-tuple-element.37), channel_id=1, source_target_pairs={{0,4},{2,6},{4,0},{6,2},{8,12},{10,14},{12,8},{14,10},{1,5},{3,7},... | collective-permute-start | bytes 147464 | tf_op jit(solution)/shard_map/ppermute | solution.py:26
  114.5 3.3 %collective-permute-start.9 = (bf16[2,2,2,24,128]{4,3,1,0,2:T(8,128)(2,1)S(1)}, bf16[2,2,2,24,128]{4,3,1,0,2:T(8,128)(2,1)S(1)}, u32[]{:S(2)}, u32[]{:S(2)}) collective-permute-start(bf16[2,2,2,24,128]{4,3,1,0,2:T(8,128)(2,1)S(1)} %get-tuple-element.35), channel_id=1, source_target_pairs={{0,2},{2,0},{4,6},{6,4},{8,10},{10,8},{12,14},{14,12},{1,3},{3,1},... | collective-permute-start | bytes 147464 | tf_op jit(solution)/shard_map/ppermute | solution.py:26
  117.8 7.4 %collective-permute-start.10 = (bf16[2,2,2,24,128]{4,3,2,1,0:T(8,128)(2,1)S(1)}, bf16[2,2,2,24,128]{4,3,2,1,0:T(8,128)(2,1)S(1)}, u32[]{:S(2)}, u32[]{:S(2)}) collective-permute-start(bf16[2,2,2,24,128]{4,3,2,1,0:T(8,128)(2,1)S(1)} %get-tuple-element.33), channel_id=1, source_target_pairs={{0,1},{1,0},{2,3},{3,2},{4,5},{5,4},{6,7},{7,6},{8,9},{9,8},{10,11... | collective-permute-start | bytes 147464 | tf_op jit(solution)/shard_map/ppermute | solution.py:26
  124.3 1.6 %collective-permute-start.11 = (bf16[8,16,128]{2,1,0:T(8,128)(2,1)S(1)}, bf16[8,16,128]{2,1,0:T(8,128)(2,1)S(1)}, u32[]{:S(2)}, u32[]{:S(2)}) collective-permute-start(bf16[8,16,128]{2,1,0:T(8,128)(2,1)S(1)} %get-tuple-element.28), channel_id=1, source_target_pairs={{0,1},{1,0},{2,3},{3,2},{4,5},{5,4},{6,7},{7,6},{8,9},{9,8},{10,11... | collective-permute-start | bytes 98312 | tf_op jit(solution)/shard_map/ppermute | solution.py:26
  125.2 0.8 copy-start.1

commit v7 on v5

--- a/solution.py
+++ b/solution.py
@@ -160,7 +160,7 @@
     return 2 * jnp.bitwise_xor(x_me, b1 + 2 * b2 + 4 * b4) + jnp.bitwise_xor(c_me, bc)
 
 
-def step_kernel(rt, rp, cols, tall, par_own, par_other, send, step):
+def step_kernel(rt, rp, cols, tall, par_own, par_other, rounded, step):
     x_me, c_me = lax.axis_index("x"), lax.axis_index("c")
     kid_par_j = kid_par_columns(tall)
     for bc, par in enumerate((par_own, par_other)):
@@ -170,14 +170,13 @@
             at = chunk_place(x_me, c_me, (k // 4, (k // 2) % 2, k % 2, bc))
             total = cols[at, 2 * rp : 2 * rp + rt, :].astype(F32) + product[k * rt : (k + 1) * rt]
             step[at] = total
-            rounded = total.astype(BF16)
-            for y in range(send.shape[0]):
-                send[y, at] = rounded
-
-
-def main_kernel(
-    rt, rp, near, far, par_own, par_other, tall, step_j, cols, step, slots, part, db
-):
+            rounded[at] = total.astype(BF16)
+
+
+def main_kernel(rt, rp, near, far, par_own, par_other, tall, cols, step, *refs):
+    steps, (slots, part, db, step_j) = refs[:-4], refs[-4:]
+    for k, rows in enumerate(steps):
+        step_j[jnp.bitwise_xor(lax.axis_index("y"), k)] = rows[...]
     w1 = near.shape[-1]
     ny, nj = tall.shape[:2]
     x_me, c_me = lax.axis_index("x"), lax.axis_index("c")
@@ -334,17 +333,20 @@
     def sized(kernel):
         return lambda *refs: kernel(rt, rp, *refs)
 
-    send, step = call(
+    rounded, step = call(
         sized(step_kernel),
-        [((ny, nj, rt, LANES), BF16), ((nj, rt, LANES), F32)],
+        [((nj, rt, LANES), BF16), ((nj, rt, LANES), F32)],
         (cols, tall, par_own, par_other),
     )
-    step_j = exchanged(send, "y")
+    steps = [rounded]
+    for k in range(1, ny):
+        steps.append(swapped(rounded, "y", k))
     rows4 = nj * rp + nj * rp // 2 + 8
     slots4, part, db = call(
         sized(main_kernel),
         [((ny, rows4, LANES), BF16), ((nj, rt + rp, LANES), BF16), ((nj, rp, LANES), F32)],
-        (near, far, par_own, par_other, tall, step_j, cols, step),
+        (near, far, par_own, par_other, tall, cols, step, *steps),
+        scratch=[pltpu.VMEM((ny, nj, rt, LANES), BF16)],
     )
     received = exchanged(slots4, "y")
     (out,) = call(

time: 123 us -> 124 us (level)
  starting transfers between devices: 26.1 us -> 60.6 us
  blocking collectives: 46.4 us -> 16.1 us
  waiting for transfers between devices: 41.9 us -> 39.1 us
    all_to_all x2 -> x1, blocking collectives: 46.4 us -> 16.1 us  [exchanged(): return lax.all_to_all(x, axes, split_axis=0, concat_axis=0, tiled=True)]
    ppermute x7 -> x14, starting transfers between devices: 6.73 us -> 29.5 us  [swapped(): lax.ppermute(x, axis, [(i, i ^ bit) for i in range(lax.axis_size(axis))])]
    all_to_all x3, starting transfers between devices: 19.3 us -> 31.2 us  [exchanged(): return lax.all_to_all(x, axes, split_axis=0, concat_axis=0, tiled=True)]
    ppermute x7 -> x14, waiting for transfers between devices: 20.3 us -> 17.9 us  [swapped(): lax.ppermute(x, axis, [(i, i ^ bit) for i in range(lax.axis_size(axis))])]
  transfers between devices with their start and end apart: 10 -> 17, of which waited for: 7 -> 11; matrix products, arithmetic and copies ran while one was open for 0% -> 0% of each run, Pallas kernels for 2% -> 3%
where the time goes in v7:
time: 124 us
  starting transfers between devices  60.6 us (49%)
  waiting for transfers between devices  39.1 us (32%)
  blocking collectives  16.1 us (13%)
  Pallas kernels  7 us (6%)
    all_to_all x3, starting transfers between devices, exchanged(): return lax.all_to_all(x, axes, split_axis=0, concat_axis=0, tiled=True)  31.2 us
    ppermute x14, starting transfers between devices, swapped(): lax.ppermute(x, axis, [(i, i ^ bit) for i in range(lax.axis_size(axis))])  29.5 us
    all_to_all x3, waiting for transfers between devices, exchanged(): return lax.all_to_all(x, axes, split_axis=0, concat_axis=0, tiled=True)  21.2 us
    ppermute x14, waiting for transfers between devices, swapped(): lax.ppermute(x, axis, [(i, i ^ bit) for i in range(lax.axis_size(axis))])  17.9 us
    all_to_all x1, blocking collectives, exchanged(): return lax.all_to_all(x, axes, split_axis=0, concat_axis=0, tiled=True)  16.1 us
    pallas_call x10, Pallas kernels, call(): pl.pallas_call(kernel, out_shape=tuple((jax.ShapeDtypeStruct(s, d) for s,...  7 us
  transfers between devices with their start and end apart: 17, of which 11 were waited for; matrix products, arithmetic and copies ran while one was open for 0% of the time, Pallas kernels for 3%

profile of v7, /device:TPU:513, one launch (start us, length us, event | category | flops | bytes accessed | tf_op | source)
XLA Modules:
  0.0 123.7 jit_solution(15778944644289142294)
XLA Ops:
  0.6 1.0 shard_map.128.own
  1.6 6.7 %collective-permute-start = (bf16[56,1024]{1,0:T(8,128)(2,1)S(1)}, bf16[56,1024]{1,0:T(8,128)(2,1)S(1)}, u32[]{:S(2)}, u32[]{:S(2)}) collective-permute-start(bf16[56,1024]{1,0:T(8,128)(2,1)S(1)} %shard_map.128.own), channel_id=1, source_target_pairs={{0,8},{2,10},{4,12},{6,14},{8,0},{10,2},{12,4},{14,6},{1,9},{3,11}... | collective-permute-start | bytes 344072 | tf_op jit(solution)/shard_map/ppermute | solution.py:26
  8.3 2.3 %collective-permute-done.other = bf16[56,1024]{1,0:T(8,128)(2,1)S(1)} collective-permute-done((bf16[56,1024]{1,0:T(8,128)(2,1)S(1)}, bf16[56,1024]{1,0:T(8,128)(2,1)S(1)}, u32[]{:S(2)}, u32[]{:S(2)}) %collective-permute-start) | collective-permute-done | bytes 114720 | tf_op jit(solution)/shard_map/ppermute | solution.py:26
  10.6 4.6 %collective-permute-start.1 = (bf16[2,40,1024]{2,1,0:T(8,128)(2,1)S(1)}, bf16[2,40,1024]{2,1,0:T(8,128)(2,1)S(1)}, u32[]{:S(2)}, u32[]{:S(2)}) collective-permute-start(bf16[2,40,1024]{2,1,0:T(8,128)(2,1)S(1)} %get-tuple-element.12.own), channel_id=1, source_target_pairs={{0,4},{2,6},{4,0},{6,2},{8,12},{10,14},{12,8},{14,10},{1,5},{3,7},... | collective-permute-start | bytes 491528 | tf_op jit(solution)/shard_map/ppermute | solution.py:26
  15.2 1.7 %shard_map.131 = bf16[16,32,128]{2,1,0:T(8,128)(2,1)} custom-call(bf16[16,1024]{1,0:T(8,128)(2,1)} %refs_0_.3, bf16[2,16,1024]{2,1,0:T(8,128)(2,1)} %refs_1_.4, bf16[2,8,1024]{2,1,0:T(8,128)(2,1)} %refs_2_.3, s32[4,8]{1,0:T(4,128)} %bitcast.3, s32[2,4,8]{2,1,0:T(4,128)} %bitcast.4, s32[2,4,4]{2,1,0:T(4,128)} %refs_5_.1), custom_call_target="tpu_custom_call" | custom-call | tf_op jit(solution)/shard_map/pallas_call | solution.py:56
  17.0 20.0 %all-to-all-start = ((bf16[16,32,128]{2,1,0:T(8,128)(2,1)}), bf16[16,32,128]{2,1,0:T(8,128)(2,1)S(1)}, u32[]{:S(2)}, u32[]{:S(2)}) async-start(bf16[16,32,128]{2,1,0:T(8,128)(2,1)} %shard_map.131), calls=%async_computation | async-start | bytes 262144 | tf_op jit(solution)/shard_map/all_to_all | solution.py:22
  37.0 0.0 collective-permute-done.1.other
  37.0 1.5 %collective-permute-start.2 = (bf16[4,40,1024]{2,1,0:T(8,128)(2,1)S(1)}, bf16[4,40,1024]{2,1,0:T(8,128)(2,1)S(1)}, u32[]{:S(2)}, u32[]{:S(2)}) collective-permute-start(bf16[4,40,1024]{2,1,0:T(8,128)(2,1)S(1)} %shard_map.130), channel_id=1, source_target_pairs={{0,2},{2,0},{4,6},{6,4},{8,10},{10,8},{12,14},{14,12},{1,3},{3,1},... | collective-permute-start | bytes 983048 | tf_op jit(solution)/shard_map/ppermute | solution.py:26
  38.5 7.8 %all-to-all-done.cols.refs_0_.refs_5_ = bf16[16,32,128]{2,1,0:T(8,128)(2,1)S(1)} async-done(((bf16[16,32,128]{2,1,0:T(8,128)(2,1)}), bf16[16,32,128]{2,1,0:T(8,128)(2,1)S(1)}, u32[]{:S(2)}, u32[]{:S(2)}) %all-to-all-start) | async-done | bytes 131104 | tf_op jit(solution)/shard_map/all_to_all | solution.py:22
  46.3 0.9 shard_map.132
  47.2 3.7 %all-to-all-start.1 = ((bf16[8,16,16,128]{3,2,1,0:T(8,128)(2,1)}), bf16[8,16,16,128]{3,2,1,0:T(8,128)(2,1)S(1)}, u32[]{:S(2)}, u32[]{:S(2)}) async-start(bf16[8,16,16,128]{3,2,1,0:T(8,128)(2,1)} %shard_map.132), calls=%async_computation.1 | async-start | bytes 1048576 | tf_op jit(solution)/shard_map/all_to_all | solution.py:22
  50.9 0.2 collective-permute-start.4
  51.1 5.9 %collective-permute-done.4 = bf16[2,16,1024]{2,1,0:T(8,128)(2,1)S(1)} collective-permute-done((bf16[2,16,1024]{2,1,0:T(8,128)(2,1)S(1)}, bf16[2,16,1024]{2,1,0:T(8,128)(2,1)S(1)}, u32[]{:S(2)}, u32[]{:S(2)}) %collective-permute-start.4) | collective-permute-done | bytes 65568 | tf_op jit(solution)/shard_map/ppermute | solution.py:26
  57.0 0.1 collective-permute-start.5
  57.1 0.0 collective-permute-done.2
  57.1 0.1 pad_maximum_fusion.refs_0_
  57.2 0.5 collective-permute-start.3
  57.7 4.0 %collective-permute-done.5 = bf16[4,16,1024]{2,1,0:T(8,128)(2,1)S(1)} collective-permute-done((bf16[4,16,1024]{2,1,0:T(8,128)(2,1)S(1)}, bf16[4,16,1024]{2,1,0:T(8,128)(2,1)S(1)}, u32[]{:S(2)}, u32[]{:S(2)}) %collective-permute-start.5) | collective-permute-done | bytes 131104 | tf_op jit(solution)/shard_map/ppermute | solution.py:26
  61.8 1.4 %collective-permute-start.6 = (bf16[8,16,1024]{2,1,0:T(8,128)(2,1)S(1)}, bf16[8,16,1024]{2,1,0:T(8,128)(2,1)S(1)}, u32[]{:S(2)}, u32[]{:S(2)}) collective-permute-start(bf16[8,16,1024]{2,1,0:T(8,128)(2,1)S(1)} %constant_dynamic-update-slice_fusion.refs_2_), channel_id=1, source_target_pairs={{0,1},{1,0},{2,3},{3,2},{4,5},{5,4},{6,7},{7,6},{8,9},{9,8},{10,11... | collective-permute-start | bytes 786440 | tf_op jit(solution)/shard_map/ppermute | solution.py:26
  63.2 1.2 collective-permute-done.6.refs_3_
  64.3 4.1 %all-to-all-done.1.refs_1_.refs_4_ = bf16[8,16,16,128]{3,2,1,0:T(8,128)(2,1)S(1)} async-done(((bf16[8,16,16,128]{3,2,1,0:T(8,128)(2,1)}), bf16[8,16,16,128]{3,2,1,0:T(8,128)(2,1)S(1)}, u32[]{:S(2)}, u32[]{:S(2)}) %all-to-all-start.1) | async-done | bytes 524320 | tf_op jit(solution)/shard_map/all_to_all | solution.py:22
  68.5 0.3 shard_map.133
  68.7 1.0 collective-permute-start.10
  69.7 3.6 %collective-permute-start.11 = (bf16[16,16,128]{2,1,0:T(8,128)(2,1)S(1)}, bf16[16,16,128]{2,1,0:T(8,128)(2,1)S(1)}, u32[]{:S(2)}, u32[]{:S(2)}) collective-permute-start(bf16[16,16,128]{2,1,0:T(8,128)(2,1)S(1)} %get-tuple-element.15.refs_7_), channel_id=1, source_target_pairs={{0,80},{16,64},{32,112},{48,96},{64,16},{80,0},{96,48},{112,32},{1... | collective-permute-start | bytes 196616 | tf_op jit(solution)/shard_map/ppermute | solution.py:26
  73.3 0.0 collective-permute-start.12
  73.3 3.6 %collective-permute-start.13 = (bf16[16,16,128]{2,1,0:T(8,128)(2,1)S(1)}, bf16[16,16,128]{2,1,0:T(8,128)(2,1)S(1)}, u32[]{:S(2)}, u32[]{:S(2)}) collective-permute-start(bf16[16,16,128]{2,1,0:T(8,128)(2,1)S(1)} %get-tuple-element.15.refs_7_), channel_id=1, source_target_pairs={{0,112},{16,96},{32,80},{48,64},{64,48},{80,32},{96,16},{112,0},{1... | collective-permute-start | bytes 196616 | tf_op jit(solution)/shard_map/ppermute | solution.py:26
  76.9 0.1 collective-permute-done.10.refs_11_
  77.0 1.8 %collective-permute-start.7 = (bf16[16,16,128]{2,1,0:T(8,128)(2,1)S(1)}, bf16[16,16,128]{2,1,0:T(8,128)(2,1)S(1)}, u32[]{:S(2)}, u32[]{:S(2)}) collective-permute-start(bf16[16,16,128]{2,1,0:T(8,128)(2,1)S(1)} %get-tuple-element.15.refs_7_), channel_id=1, source_target_pairs={{0,16},{16,0},{32,48},{48,32},{64,80},{80,64},{96,112},{112,96},{1... | collective-permute-start | bytes 196616 | tf_op jit(solution)/shard_map/ppermute | solution.py:26
  78.8 1.7 %collective-permute-done.11.refs_12_ = bf16[16,16,128]{2,1,0:T(8,128)(2,1)S(1)} collective-permute-done((bf16[16,16,128]{2,1,0:T(8,128)(2,1)S(1)}, bf16[16,16,128]{2,1,0:T(8,128)(2,1)S(1)}, u32[]{:S(2)}, u32[]{:S(2)}) %collective-permute-start.11) | collective-permute-done | bytes 65568 | tf_op jit(solution)/shard_map/ppermute | solution.py:26
  80.5 0.0 collective-permute-start.8
  80.5 0.0 collective-permute-done.12.refs_13_
  80.5 4.5 %collective-permute-start.9 = (bf16[16,16,128]{2,1,0:T(8,128)(2,1)S(1)}, bf16[16,16,128]{2,1,0:T(8,128)(2,1)S(1)}, u32[]{:S(2)}, u32[]{:S(2)}) collective-permute-start(bf16[16,16,128]{2,1,0:T(8,128)(2,1)S(1)} %get-tuple-element.15.refs_7_), channel_id=1, source_target_pairs={{0,48},{16,32},{32,16},{48,0},{64,112},{80,96},{96,80},{112,64},{1... | collective-permute-start | bytes 196616 | tf_op jit(solution)/shard_map/ppermute | solution.py:26
  85.0 0.1 collective-permute-done.13.refs_14_
  85.2 0.0 collective-permute-done.7.refs_8_
  85.2 0.0 collective-permute-done.8.refs_9_
  85.2 2.5 %collective-permute-done.9.refs_10_ = bf16[16,16,128]{2,1,0:T(8,128)(2,1)S(1)} collective-permute-done((bf16[16,16,128]{2,1,0:T(8,128)(2,1)S(1)}, bf16[16,16,128]{2,1,0:T(8,128)(2,1)S(1)}, u32[]{:S(2)}, u32[]{:S(2)}) %collective-permute-start.9) | collective-permute-done | bytes 65568 | tf_op jit(solution)/shard_map/ppermute | solution.py:26
  87.7 0.0 collective-permute-done.3.refs_1_
  87.7 0.9 shard_map.134
  88.6 16.1 %all_to_all.20.refs_0_ = bf16[8,200,128]{2,1,0:T(8,128)(2,1)S(1)} all-to-all(bf16[8,200,128]{2,1,0:T(8,128)(2,1)S(1)} %get-tuple-element.16), channel_id=1, replica_groups=mesh['parts'=2,'y'=8,'x'=8,'c'=2] {'y'}, dimensions={0} | all-to-all | bytes 819200 | tf_op jit(solution)/shard_map/all_to_all | solution.py:22
  104.7 0.8 shard_map.135
  105.5 0.0 copy-start
  105.5 7.5 %all-to-all-start.3 = ((bf16[16,40,128]{2,1,0:T(8,128)(2,1)}), bf16[16,40,128]{2,1,0:T(8,128)(2,1)S(1)}, u32[]{:S(2)}, u32[]{:S(2)}) async-start(bf16[16,40,128]{2,1,0:T(8,128)(2,1)} %shard_map.135), calls=%async_computation.3 | async-start | bytes 327680 | tf_op jit(solution)/shard_map/all_to_all | solution.py:22
  113.0 0.7 shard_map.136.refs_2_
  113.7 9.3 %all-to-all-done.3.refs_0_ = bf16[16,40,128]{2,1,0:T(8,128)(2,1)S(1)} async-done(((bf16[16,40,128]{2,1,0:T(8,128)(2,1)}), bf16[16,40,128]{2,1,0:T(8,128)(2,1)S(1)}, u32[]{:S(2)}, u32[]{:S(2)}) %all-to-all-start.3) | async-done | bytes 163872 | tf_op jit(solution)/shard_map/all_to_all | solution.py:22
  122.9 0.0 copy-done
  122.9 0.7 shard_map.137
  (6 shorter events, 0.1 us)
Async XLA Ops:
  1.6 9.0 %collective-permute-start = (bf16[56,1024]{1,0:T(8,128)(2,1)S(1)}, bf16[56,1024]{1,0:T(8,128)(2,1)S(1)}, u32[]{:S(2)}, u32[]{:S(2)}) collective-permute-start(bf16[56,1024]{1,0:T(8,128)(2,1)S(1)} %shard_map.128.own), channel_id=1, source_target_pairs={{0,8},{2,10},{4,12},{6,14},{8,0},{10,2},{12,4},{14,6},{1,9},{3,11}... | collective-permute-start | bytes 344072 | tf_op jit(solution)/shard_map/ppermute | solution.py:26
  10.6 26.4 %collective-permute-start.1 = (bf16[2,40,1024]{2,1,0:T(8,128)(2,1)S(1)}, bf16[2,40,1024]{2,1,0:T(8,128)(2,1)S(1)}, u32[]{:S(2)}, u32[]{:S(2)}) collective-permute-start(bf16[2,40,1024]{2,1,0:T(8,128)(2,1)S(1)} %get-tuple-element.12.own), channel_id=1, source_target_pairs={{0,4},{2,6},{4,0},{6,2},{8,12},{10,14},{12,8},{14,10},{1,5},{3,7},... | collective-permute-start | bytes 491528 | tf_op jit(solution)/shard_map/ppermute | solution.py:26
  17.0 29.3 %all-to-all-start = ((bf16[16,32,128]{2,1,0:T(8,128)(2,1)}), bf16[16,32,128]{2,1,0:T(8,128)(2,1)S(1)}, u32[]{:S(2)}, u32[]{:S(2)}) async-start(bf16[16,32,128]{2,1,0:T(8,128)(2,1)} %shard_map.131), calls=%async_computation | async-start | bytes 262144 | tf_op jit(solution)/shard_map/all_to_all | solution.py:22
  37.0 20.1 %collective-permute-start.2 = (bf16[4,40,1024]{2,1,0:T(8,128)(2,1)S(1)}, bf16[4,40,1024]{2,1,0:T(8,128)(2,1)S(1)}, u32[]{:S(2)}, u32[]{:S(2)}) collective-permute-start(bf16[4,40,1024]{2,1,0:T(8,128)(2,1)S(1)} %shard_map.130), channel_id=1, source_target_pairs={{0,2},{2,0},{4,6},{6,4},{8,10},{10,8},{12,14},{14,12},{1,3},{3,1},... | collective-permute-start | bytes 983048 | tf_op jit(solution)/shard_map/ppermute | solution.py:26
  47.2 21.3 %all-to-all-start.1 = ((bf16[8,16,16,128]{3,2,1,0:T(8,128)(2,1)}), bf16[8,16,16,128]{3,2,1,0:T(8,128)(2,1)S(1)}, u32[]{:S(2)}, u32[]{:S(2)}) async-start(bf16[8,16,16,128]{3,2,1,0:T(8,128)(2,1)} %shard_map.132), calls=%async_computation.1 | async-start | bytes 1048576 | tf_op jit(solution)/shard_map/all_to_all | solution.py:22
  50.9 6.1 %collective-permute-start.4 = (bf16[2,16,1024]{2,1,0:T(8,128)(2,1)S(1)}, bf16[2,16,1024]{2,1,0:T(8,128)(2,1)S(1)}, u32[]{:S(2)}, u32[]{:S(2)}) collective-permute-start(bf16[2,16,1024]{2,1,0:T(8,128)(2,1)S(1)} %get-tuple-element.13), channel_id=1, source_target_pairs={{0,4},{2,6},{4,0},{6,2},{8,12},{10,14},{12,8},{14,10},{1,5},{3,7},... | collective-permute-start | bytes 196616 | tf_op jit(solution)/shard_map/ppermute | solution.py:26
  57.0 4.8 %collective-permute-start.5 = (bf16[4,16,1024]{2,1,0:T(8,128)(2,1)S(1)}, bf16[4,16,1024]{2,1,0:T(8,128)(2,1)S(1)}, u32[]{:S(2)}, u32[]{:S(2)}) collective-permute-start(bf16[4,16,1024]{2,1,0:T(8,128)(2,1)S(1)} %pad_maximum_fusion.1), channel_id=1, source_target_pairs={{0,2},{2,0},{4,6},{6,4},{8,10},{10,8},{12,14},{14,12},{1,3},{3,1},... | collective-permute-start | bytes 393224 | tf_op jit(solution)/shard_map/ppermute | solution.py:26
  57.2 30.5 %collective-permute-start.3 = (bf16[8,40,1024]{2,1,0:T(8,128)(2,1)S(1)}, bf16[8,40,1024]{2,1,0:T(8,128)(2,1)S(1)}, u32[]{:S(2)}, u32[]{:S(2)}) collective-permute-start(bf16[8,40,1024]{2,1,0:T(8,128)(2,1)S(1)} %pad_maximum_fusion.refs_0_), channel_id=1, source_target_pairs={{0,1},{1,0},{2,3},{3,2},{4,5},{5,4},{6,7},{7,6},{8,9},{9,8},{10,11... | collective-permute-start | bytes 1966088 | tf_op jit(solution)/shard_map/ppermute | solution.py:26
  61.8 2.5 %collective-permute-start.6 = (bf16[8,16,1024]{2,1,0:T(8,128)(2,1)S(1)}, bf16[8,16,1024]{2,1,0:T(8,128)(2,1)S(1)}, u32[]{:S(2)}, u32[]{:S(2)}) collective-permute-start(bf16[8,16,1024]{2,1,0:T(8,128)(2,1)S(1)} %constant_dynamic-update-slice_fusion.refs_2_), channel_id=1, source_target_pairs={{0,1},{1,0},{2,3},{3,2},{4,5},{5,4},{6,7},{7,6},{8,9},{9,8},{10,11... | collective-permute-start | bytes 786440 | tf_op jit(solution)/shard_map/ppermute | solution.py:26
  68.7 8.3 %collective-permute-start.10 = (bf16[16,16,128]{2,1,0:T(8,128)(2,1)S(1)}, bf16[16,16,128]{2,1,0:T(8,128)(2,1)S(1)}, u32[]{:S(2)}, u32[]{:S(2)}) collective-permute-start(bf16[16,16,128]{2,1,0:T(8,128)(2,1)S(1)} %get-tuple-element.15.refs_7_), channel_id=1, source_target_pairs={{0,64},{16,80},{32,96},{48,112},{64,0},{80,16},{96,32},{112,48},{1... | collective-permute-start | bytes 196616 | tf_op jit(solution)/shard_map/ppermute | solution.py:26
  69.7 10.8 %collective-permute-start.11 = (bf16[16,16,128]{2,1,0:T(8,128)(2,1)S(1)}, bf16[16,16,128]{2,1,0:T(8,128)(2,1)S(1)}, u32[]{:S(2)}, u32[]{:S(2)}) collective-permute-start(bf16[16,16,128]{2,1,0:T(8,128)(2,1)S(1)} %get-tuple-element.15.refs_7_), channel_id=1, source_target_pairs={{0,80},{16,64},{32,112},{48,96},{64,16},{80,0},{96,48},{112,32},{1... | collective-permute-start | bytes 196616 | tf_op jit(solution)/shard_map/ppermute | solution.py:26
  73.3 7.2 %collective-permute-start.12 = (bf16[16,16,128]{2,1,0:T(8,128)(2,1)S(1)}, bf16[16,16,128]{2,1,0:T(8,128)(2,1)S(1)}, u32[]{:S(2)}, u32[]{:S(2)}) collective-permute-start(bf16[16,16,128]{2,1,0:T(8,128)(2,1)S(1)} %get-tuple-element.15.refs_7_), channel_id=1, source_target_pairs={{0,96},{16,112},{32,64},{48,80},{64,32},{80,48},{96,0},{112,16},{1... | collective-permute-start | bytes 196616 | tf_op jit(solution)/shard_map/ppermute | solution.py:26
  73.3 11.8 %collective-permute-start.13 = (bf16[16,16,128]{2,1,0:T(8,128)(2,1)S(1)}, bf16[16,16,128]{2,1,0:T(8,128)(2,1)S(1)}, u32[]{:S(2)}, u32[]{:S(2)}) collective-permute-start(bf16[16,16,128]{2,1,0:T(8,128)(2,1)S(1)} %get-tuple-element.15.refs_7_), channel_id=1, source_target_pairs={{0,112},{16,96},{32,80},{48,64},{64,48},{80,32},{96,16},{112,0},{1... | collective-permute-start | bytes 196616 | tf_op jit(solution)/shard_map/ppermute | solution.py:26
  77.0 8.2 %collective-permute-start.7 = (bf16[16,16,128]{2,1,0:T(8,128)(2,1)S(1)}, bf16[16,16,128]{2,1,0:T(8,128)(2,1)S(1)}, u32[]{:S(2)}, u32[]{:S(2)}) collective-permute-start(bf16[16,16,128]{2,1,0:T(8,128)(2,1)S(1)} %get-tuple-element.15.refs_7_), channel_id=1, source_target_pairs={{0,16},{16,0},{32,48},{48,32},{64,80},{80,64},{96,112},{112,96},{1... | collective-permute-start | bytes 196616 | tf_op jit(solution)/shard_map/ppermute | solution.py:26
  80.5 4.7 %collective-permute-start.8 = (bf16[16,16,128]{2,1,0:T(8,128)(2,1)S(1)}, bf16[16,16,128]{2,1,0:T(8,128)(2,1)S(1)}, u32[]{:S(2)}, u32[]{:S(2)}) collective-permute-start(bf16[16,16,128]{2,1,0:T(8,128)(2,1)S(1)} %get-tuple-element.15.refs_7_), channel_id=1, source_target_pairs={{0,32},{16,48},{32,0},{48,16},{64,96},{80,112},{96,64},{112,80},{1... | collective-permute-start | bytes 196616 | tf_op jit(solution)/shard_map/ppermute | solution.py:26
  80.5 7.2 %collective-permute-start.9 = (bf16[16,16,128]{2,1,0:T(8,128)(2,1)S(1)}, bf16[16,16,128]{2,1,0:T(8,128)(2,1)S(1)}, u32[]{:S(2)}, u32[]{:S(2)}) collective-permute-start(bf16[16,16,128]{2,1,0:T(8,128)(2,1)S(1)} %get-tuple-element.15.refs_7_), channel_id=1, source_target_pairs={{0,48},{16,32},{32,16},{48,0},{64,112},{80,96},{96,80},{112,64},{1... | collective-permute-start | bytes 196616 | tf_op jit(solution)/shard_map/ppermute | solution.py:26
  105.5 17.5 %copy-start = (f32[8,1024]{1,0:T(8,128)S(1)}, f32[8,1024]{1,0:T(8,128)}, u32[]{:S(2)}) copy-start(f32[8,1024]{1,0:T(8,128)} %refs_1_.5) | copy-start | bytes 98308
  105.5 17.5 %all-to-all-start.3 = ((bf16[16,40,128]{2,1,0:T(8,128)(2,1)}), bf16[16,40,128]{2,1,0:T(8,128)(2,1)S(1)}, u32[]{:S(2)}, u32[]{:S(2)}) async-start(bf16[16,40,128]{2,1,0:T(8,128)(2,1)} %shard_map.135), calls=%async_computation.3 | async-start | bytes 327680 | tf_op jit(solution)/shard_map/all_to_all | solution.py:22

commit v8 on v7

--- a/solution.py
+++ b/solution.py
@@ -77,10 +77,10 @@
     return jnp.sum(jnp.where(lane == at, mask, 0).astype(F32), axis=1, keepdims=True)
 
 
-def slots_kernel(*refs):
-    sources, slots, scratch, done = refs[:6], refs[6], refs[7:13], refs[13]
+def pack_kernel(*refs):
+    sources, (slots, par_rows, rows), scratch, done = refs[:8], refs[8:11], refs[11:19], refs[19]
     fetched(sources, scratch, done)
-    par, kid_top, kid_par, mask_par, mask_kid_top, mask_kid_par = scratch
+    sigma, par, dinv, kid_top, kid_par, mask_par, mask_kid_top, mask_kid_par = scratch
     rt, w1 = par.shape
     kids, rp = kid_par.shape[:2]
     nj = slots.shape[0]
@@ -93,6 +93,7 @@
         at = slice(m * LANES, (m + 1) * LANES)
         block = m * LANES // BLK
         piece = par[:, at].astype(F32) * keep[block : block + 1]
+        par_rows[:, at] = piece.astype(BF16)
         top, low = piece[:rp], piece[rp:]
         packed.append(low_high(top, turned(low)))
         packed.append(low_high(turned(top), low))
@@ -108,33 +109,21 @@
             slots[j, 0 : 2 * rp, :] = jnp.concatenate([piece, packed[j]], axis=0).astype(BF16)
             piece = kid_top[k, :, at].astype(F32) * keep_top[block : block + 1]
             slots[j, 2 * rp : 2 * rp + rt, :] = piece.astype(BF16)
-
-
-def rows_kernel(*refs):
-    sources, rows, scratch, done = refs[:4], refs[4], refs[5:9], refs[9]
+    rows[0:rt, :] = sigma[:, 0:w1]
+    rows[rt : 2 * rt, :] = sigma[:, w1 : 2 * w1]
+    rows[2 * rt : 2 * rt + rp, :] = dinv[...].astype(BF16)
+
+
+def copy_kernel(*refs):
+    sources, results, scratch, done = refs[:2], refs[2:4], refs[4:6], refs[6]
     fetched(sources, scratch, done)
-    sigma, par, dinv, mask_par = scratch
-    rt, w1 = par.shape
-    rp = dinv.shape[0]
-    keep = lane_of(mask_par[...], lax.div(lax.axis_index(ROW) * rt, BLK))
-    for b in range(w1 // BLK):
-        at = slice(b * BLK, (b + 1) * BLK)
-        rows[0:rt, at] = (par[:, at].astype(F32) * keep[b : b + 1]).astype(BF16)
-    rows[rt : 2 * rt, :] = sigma[:, 0:w1]
-    rows[2 * rt : 3 * rt, :] = sigma[:, w1 : 2 * w1]
-    rows[3 * rt : 3 * rt + rp, :] = dinv[...].astype(BF16)
-
-
-def copy_kernel(source_hbm, result, scratch, done):
-    fetched((source_hbm,), (scratch,), done)
-    result[...] = scratch[...]
-
-
-def stack_kernel(own, other, par_rows, rows):
-    rt = par_rows.shape[1]
-    for i, source in enumerate((own, other)):
-        par_rows[i] = source[0:rt, :]
-        rows[i] = source[rt : rt + rows.shape[1], :]
+    for result, value in zip(results, scratch):
+        result[...] = value[...]
+
+
+def stack_kernel(own, other, stacked):
+    stacked[0] = own[...]
+    stacked[1] = other[...]
 
 
 def join_kernel(own, other, joined):
@@ -150,9 +139,8 @@
 
 
 def kid_par_columns(tall):
-    ny, nj, rows, _ = tall.shape
-    rp = rows // 2
-    return tall[:, :, 0:rp, :].astype(F32).reshape(ny * nj * rp, LANES).astype(BF16)
+    ny, nj, rp, _ = tall.shape
+    return tall[...].astype(F32).reshape(ny * nj * rp, LANES).astype(BF16)
 
 
 def chunk_place(x_me, c_me, bits):
@@ -170,18 +158,21 @@
             at = chunk_place(x_me, c_me, (k // 4, (k // 2) % 2, k % 2, bc))
             total = cols[at, 2 * rp : 2 * rp + rt, :].astype(F32) + product[k * rt : (k + 1) * rt]
             step[at] = total
-            rounded[at] = total.astype(BF16)
+            rounded[at, 0:rt, :] = total.astype(BF16)
+            rounded[at, rt : rt + rp, :] = cols[at, rp : 2 * rp, :]
 
 
 def main_kernel(rt, rp, near, far, par_own, par_other, tall, cols, step, *refs):
-    steps, (slots, part, db, step_j) = refs[:-4], refs[-4:]
+    steps, (slots, part, db, step_j, par_j) = refs[:-5], refs[-5:]
     for k, rows in enumerate(steps):
-        step_j[jnp.bitwise_xor(lax.axis_index("y"), k)] = rows[...]
+        y = jnp.bitwise_xor(lax.axis_index("y"), k)
+        step_j[y] = rows[:, 0:rt, :]
+        par_j[y] = rows[:, rt : rt + rp, :].astype(F32)
     w1 = near.shape[-1]
     ny, nj = tall.shape[:2]
     x_me, c_me = lax.axis_index("x"), lax.axis_index("c")
     kid_par_j = kid_par_columns(tall)
-    par_j = tall[:, :, rp : 2 * rp, :].astype(F32).reshape(ny * nj, 1, rp, LANES)
+    par_j = par_j[...].reshape(ny * nj, 1, rp, LANES)
     par_j = jnp.concatenate([par_j, turned(par_j)], axis=1)
     par_j = par_j.reshape(ny * nj * 2 * rp, LANES).astype(BF16)
     both = jnp.concatenate([step_j[...].reshape(ny * nj * rt, LANES), par_j], axis=1)
@@ -302,27 +293,26 @@
         )
 
     masks = (mask_par.T, mask_kid_top.transpose(0, 2, 1), mask_kid_par)
-    (slots,) = fetching(
-        slots_kernel,
-        [((nj, 2 * rp + rt, LANES), BF16)],
-        (panel_par, panel_kid_top, panel_kid_par, *masks),
+    slots, par_rows, rows = fetching(
+        pack_kernel,
+        [
+            ((nj, 2 * rp + rt, LANES), BF16),
+            ((rt, w1), BF16),
+            ((2 * rt + rp, w1), BF16),
+        ],
+        (sigma_top, panel_par, dinv_par, panel_kid_top, panel_kid_par, *masks),
     )
     cols = exchanged(slots, XC)
-    (rows,) = fetching(
-        rows_kernel,
-        [((3 * rt + rp, w1), BF16)],
-        (sigma_top, panel_par, dinv_par, masks[0]),
-    )
+    par_far = swapped(par_rows, "x", 4)
     far_rows = swapped(rows, "x", 4)
-    (dvar_kid,) = fetching(copy_kernel, [(dvar_kid.shape, F32)], (dvar_kid,))
-    par_rows, rows = call(
-        stack_kernel,
-        [((2, rt, w1), BF16), ((2, 2 * rt + rp, w1), BF16)],
-        (rows, far_rows),
-    )
-    (tall_send,) = call(repeat_kernel, [((ny, nj, 2 * rp, LANES), BF16)], (cols,))
+    pair = (dvar_kid, dinv_par)
+    dvar_kid, dinv_par = fetching(copy_kernel, [(a.shape, F32) for a in pair], pair)
+    (tall_send,) = call(repeat_kernel, [((ny, nj, rp, LANES), BF16)], (cols,))
+    par_rows = jnp.stack([par_rows, par_far])
+    par_far = swapped(par_rows, "x", 2)
     tall = exchanged(tall_send, "y")
-    par_rows = jnp.concatenate([par_rows, swapped(par_rows, "x", 2)])
+    (rows,) = call(stack_kernel, [((2, 2 * rt + rp, w1), BF16)], (rows, far_rows))
+    (par_rows,) = call(join_kernel, [((4, rt, w1), BF16)], (par_rows, par_far))
     par_own = jnp.concatenate([par_rows, swapped(par_rows, "x", 1)])
     par_other = swapped(par_own, "c", 1)
     rows_2 = swapped(rows, "x", 2)
@@ -335,7 +325,7 @@
 
     rounded, step = call(
         sized(step_kernel),
-        [((nj, rt, LANES), BF16), ((nj, rt, LANES), F32)],
+        [((nj, rt + rp, LANES), BF16), ((nj, rt, LANES), F32)],
         (cols, tall, par_own, par_other),
     )
     steps = [rounded]
@@ -346,7 +336,10 @@
         sized(main_kernel),
         [((ny, rows4, LANES), BF16), ((nj, rt + rp, LANES), BF16), ((nj, rp, LANES), F32)],
         (near, far, par_own, par_other, tall, cols, step, *steps),
-        scratch=[pltpu.VMEM((ny, nj, rt, LANES), BF16)],
+        scratch=[
+            pltpu.VMEM((ny, nj, rt, LANES), BF16),
+            pltpu.VMEM((ny, nj, rp, LANES), F32),
+        ],
     )
     received = exchanged(slots4, "y")
     (out,) = call(

time: 124 us -> 131 us (1.056)
  waiting for transfers between devices: 39.1 us -> 44.3 us
  starting transfers between devices: 60.6 us -> 64.4 us
  blocking collectives: 16.1 us -> 14.5 us
    ppermute x14 -> x15, waiting for transfers between devices: 17.9 us -> 31.1 us  [swapped(): lax.ppermute(x, axis, [(i, i ^ bit) for i in range(lax.axis_size(axis))])]
    all_to_all x3, waiting for transfers between devices: 21.2 us -> 13.2 us  [exchanged(): return lax.all_to_all(x, axes, split_axis=0, concat_axis=0, tiled=True)]
    all_to_all x3, starting transfers between devices: 31.2 us -> 35.9 us  [exchanged(): return lax.all_to_all(x, axes, split_axis=0, concat_axis=0, tiled=True)]
    all_to_all x1, blocking collectives: 16.1 us -> 14.5 us  [exchanged(): return lax.all_to_all(x, axes, split_axis=0, concat_axis=0, tiled=True)]
    ppermute x14 -> x15, starting transfers between devices: 29.5 us -> 28.5 us  [swapped(): lax.ppermute(x, axis, [(i, i ^ bit) for i in range(lax.axis_size(axis))])]
  transfers between devices with their start and end apart: 17 -> 18, of which waited for: 11 -> 10; matrix products, arithmetic and copies ran while one was open for 0% -> 0% of each run, Pallas kernels for 3% -> 1%
where the time goes in v8:
time: 131 us; the launch traced here: 130 us
  starting transfers between devices  64.4 us (49%)
  waiting for transfers between devices  44.3 us (34%)
  blocking collectives  14.5 us (11%)
  Pallas kernels  6.12 us (5%)
    all_to_all x3, starting transfers between devices, exchanged(): return lax.all_to_all(x, axes, split_axis=0, concat_axis=0, tiled=True)  35.9 us
    ppermute x15, waiting for transfers between devices, swapped(): lax.ppermute(x, axis, [(i, i ^ bit) for i in range(lax.axis_size(axis))])  31.1 us
    ppermute x15, starting transfers between devices, swapped(): lax.ppermute(x, axis, [(i, i ^ bit) for i in range(lax.axis_size(axis))])  28.5 us
    all_to_all x1, blocking collectives, exchanged(): return lax.all_to_all(x, axes, split_axis=0, concat_axis=0, tiled=True)  14.5 us
    all_to_all x3, waiting for transfers between devices, exchanged(): return lax.all_to_all(x, axes, split_axis=0, concat_axis=0, tiled=True)  13.2 us
    pallas_call x10, Pallas kernels, call(): pl.pallas_call(kernel, out_shape=tuple((jax.ShapeDtypeStruct(s, d) for s,...  6.12 us
  transfers between devices with their start and end apart: 18, of which 10 were waited for; matrix products, arithmetic and copies ran while one was open for 0% of the time, Pallas kernels for 1%

profile of v8, /device:TPU:513, one launch (start us, length us, event | category | flops | bytes accessed | tf_op | source)
XLA Modules:
  0.0 130.1 jit_solution(9535999134952465421)
XLA Ops:
  0.6 1.8 %shard_map.128 = (bf16[16,32,128]{2,1,0:T(8,128)(2,1)}, bf16[16,1024]{1,0:T(8,128)(2,1)S(1)}, bf16[40,1024]{1,0:T(8,128)(2,1)S(1)}) custom-call(bf16[16,2048]{1,0:T(8,128)(2,1)} %refs_0_.2, bf16[16,1024]{1,0:T(8,128)(2,1)} %refs_1_.2, f32[8,1024]{1,0:T(8,128)} %refs_1_.3, bf16[2,16,1024]{2,1,0:T(8,128)(2,1)} %refs_3_.1, bf16[2,8,1024]{2,1,0:T(8,128)(2,1)} %refs_4_.1, ...), custom_call_target="tpu_custom_call" | custom-call | tf_op jit(solution)/shard_map/pallas_call | solution.py:56
  2.4 6.7 %collective-permute-start = (bf16[40,1024]{1,0:T(8,128)(2,1)S(1)}, bf16[40,1024]{1,0:T(8,128)(2,1)S(1)}, u32[]{:S(2)}, u32[]{:S(2)}) collective-permute-start(bf16[40,1024]{1,0:T(8,128)(2,1)S(1)} %get-tuple-element.15.own), channel_id=1, source_target_pairs={{0,8},{2,10},{4,12},{6,14},{8,0},{10,2},{12,4},{14,6},{1,9},{3,11}... | collective-permute-start | bytes 245768 | tf_op jit(solution)/shard_map/ppermute | solution.py:26
  9.1 1.9 %collective-permute-done.other = bf16[40,1024]{1,0:T(8,128)(2,1)S(1)} collective-permute-done((bf16[40,1024]{1,0:T(8,128)(2,1)S(1)}, bf16[40,1024]{1,0:T(8,128)(2,1)S(1)}, u32[]{:S(2)}, u32[]{:S(2)}) %collective-permute-start) | collective-permute-done | bytes 81952 | tf_op jit(solution)/shard_map/ppermute | solution.py:26
  11.1 3.9 %collective-permute-start.1 = (bf16[2,40,1024]{2,1,0:T(8,128)(2,1)S(1)}, bf16[2,40,1024]{2,1,0:T(8,128)(2,1)S(1)}, u32[]{:S(2)}, u32[]{:S(2)}) collective-permute-start(bf16[2,40,1024]{2,1,0:T(8,128)(2,1)S(1)} %shard_map.129.own), channel_id=1, source_target_pairs={{0,4},{2,6},{4,0},{6,2},{8,12},{10,14},{12,8},{14,10},{1,5},{3,7},... | collective-permute-start | bytes 491528 | tf_op jit(solution)/shard_map/ppermute | solution.py:26
  15.0 5.5 %collective-permute-done.1.other = bf16[2,40,1024]{2,1,0:T(8,128)(2,1)S(1)} collective-permute-done((bf16[2,40,1024]{2,1,0:T(8,128)(2,1)S(1)}, bf16[2,40,1024]{2,1,0:T(8,128)(2,1)S(1)}, u32[]{:S(2)}, u32[]{:S(2)}) %collective-permute-start.1) | collective-permute-done | bytes 163872 | tf_op jit(solution)/shard_map/ppermute | solution.py:26
  20.5 0.1 collective-permute-start.2
  20.6 21.4 %all-to-all-start = ((bf16[16,32,128]{2,1,0:T(8,128)(2,1)}), bf16[16,32,128]{2,1,0:T(8,128)(2,1)S(1)}, u32[]{:S(2)}, u32[]{:S(2)}) async-start(bf16[16,32,128]{2,1,0:T(8,128)(2,1)} %get-tuple-element.17), calls=%async_computation | async-start | bytes 262144 | tf_op jit(solution)/shard_map/all_to_all | solution.py:22
  42.1 5.4 %collective-permute-start.4 = (bf16[16,1024]{1,0:T(8,128)(2,1)S(1)}, bf16[16,1024]{1,0:T(8,128)(2,1)S(1)}, u32[]{:S(2)}, u32[]{:S(2)}) collective-permute-start(bf16[16,1024]{1,0:T(8,128)(2,1)S(1)} %get-tuple-element.16), channel_id=1, source_target_pairs={{0,8},{2,10},{4,12},{6,14},{8,0},{10,2},{12,4},{14,6},{1,9},{3,11}... | collective-permute-start | bytes 98312 | tf_op jit(solution)/shard_map/ppermute | solution.py:26
  47.5 4.6 %collective-permute-done.4 = bf16[16,1024]{1,0:T(8,128)(2,1)S(1)} collective-permute-done((bf16[16,1024]{1,0:T(8,128)(2,1)S(1)}, bf16[16,1024]{1,0:T(8,128)(2,1)S(1)}, u32[]{:S(2)}, u32[]{:S(2)}) %collective-permute-start.4) | collective-permute-done | bytes 32800 | tf_op jit(solution)/shard_map/ppermute | solution.py:26
  52.1 0.2 collective-permute-start.5
  52.3 4.6 %collective-permute-done.5.other = bf16[2,16,1024]{2,1,0:T(8,128)(2,1)S(1)} collective-permute-done((bf16[2,16,1024]{2,1,0:T(8,128)(2,1)S(1)}, bf16[2,16,1024]{2,1,0:T(8,128)(2,1)S(1)}, u32[]{:S(2)}, u32[]{:S(2)}) %collective-permute-start.5) | collective-permute-done | bytes 65568 | tf_op jit(solution)/shard_map/ppermute | solution.py:26
  56.9 0.3 collective-permute-start.6
  57.3 0.0 all-to-all-done.cols.refs_0_.refs_5_
  57.3 0.7 shard_map.132
  58.0 3.6 %all-to-all-start.1 = ((bf16[8,16,8,128]{3,2,1,0:T(8,128)(2,1)}), bf16[8,16,8,128]{3,2,1,0:T(8,128)(2,1)S(1)}, u32[]{:S(2)}, u32[]{:S(2)}) async-start(bf16[8,16,8,128]{3,2,1,0:T(8,128)(2,1)} %shard_map.132), calls=%async_computation.1 | async-start | bytes 524288 | tf_op jit(solution)/shard_map/all_to_all | solution.py:22
  61.6 0.0 collective-permute-done.2
  61.6 0.1 pad_maximum_fusion.refs_0_
  61.7 2.5 %collective-permute-start.3 = (bf16[8,40,1024]{2,1,0:T(8,128)(2,1)S(1)}, bf16[8,40,1024]{2,1,0:T(8,128)(2,1)S(1)}, u32[]{:S(2)}, u32[]{:S(2)}) collective-permute-start(bf16[8,40,1024]{2,1,0:T(8,128)(2,1)S(1)} %pad_maximum_fusion.refs_0_), channel_id=1, source_target_pairs={{0,1},{1,0},{2,3},{3,2},{4,5},{5,4},{6,7},{7,6},{8,9},{9,8},{10,11... | collective-permute-start | bytes 1966088 | tf_op jit(solution)/shard_map/ppermute | solution.py:26
  64.2 0.0 collective-permute-done.6
  64.3 0.2 collective-permute-start.7
  64.4 1.9 %collective-permute-done.7.refs_3_ = bf16[8,16,1024]{2,1,0:T(8,128)(2,1)S(1)} collective-permute-done((bf16[8,16,1024]{2,1,0:T(8,128)(2,1)S(1)}, bf16[8,16,1024]{2,1,0:T(8,128)(2,1)S(1)}, u32[]{:S(2)}, u32[]{:S(2)}) %collective-permute-start.7) | collective-permute-done | bytes 262176 | tf_op jit(solution)/shard_map/ppermute | solution.py:26
  66.3 4.5 %all-to-all-done.1.refs_1_.refs_4_ = bf16[8,16,8,128]{3,2,1,0:T(8,128)(2,1)S(1)} async-done(((bf16[8,16,8,128]{3,2,1,0:T(8,128)(2,1)}), bf16[8,16,8,128]{3,2,1,0:T(8,128)(2,1)S(1)}, u32[]{:S(2)}, u32[]{:S(2)}) %all-to-all-start.1) | async-done | bytes 262176 | tf_op jit(solution)/shard_map/all_to_all | solution.py:22
  70.8 0.3 shard_map.133
  71.1 0.3 collective-permute-start.10
  71.5 1.6 %collective-permute-start.11 = (bf16[16,24,128]{2,1,0:T(8,128)(2,1)S(1)}, bf16[16,24,128]{2,1,0:T(8,128)(2,1)S(1)}, u32[]{:S(2)}, u32[]{:S(2)}) collective-permute-start(bf16[16,24,128]{2,1,0:T(8,128)(2,1)S(1)} %get-tuple-element.19.refs_7_), channel_id=1, source_target_pairs={{0,64},{16,80},{32,96},{48,112},{64,0},{80,16},{96,32},{112,48},{1... | collective-permute-start | bytes 294920 | tf_op jit(solution)/shard_map/ppermute | solution.py:26
  73.0 2.6 %collective-permute-start.12 = (bf16[16,24,128]{2,1,0:T(8,128)(2,1)S(1)}, bf16[16,24,128]{2,1,0:T(8,128)(2,1)S(1)}, u32[]{:S(2)}, u32[]{:S(2)}) collective-permute-start(bf16[16,24,128]{2,1,0:T(8,128)(2,1)S(1)} %get-tuple-element.19.refs_7_), channel_id=1, source_target_pairs={{0,80},{16,64},{32,112},{48,96},{64,16},{80,0},{96,48},{112,32},{1... | collective-permute-start | bytes 294920 | tf_op jit(solution)/shard_map/ppermute | solution.py:26
  75.6 2.2 %collective-permute-start.13 = (bf16[16,24,128]{2,1,0:T(8,128)(2,1)S(1)}, bf16[16,24,128]{2,1,0:T(8,128)(2,1)S(1)}, u32[]{:S(2)}, u32[]{:S(2)}) collective-permute-start(bf16[16,24,128]{2,1,0:T(8,128)(2,1)S(1)} %get-tuple-element.19.refs_7_), channel_id=1, source_target_pairs={{0,96},{16,112},{32,64},{48,80},{64,32},{80,48},{96,0},{112,16},{1... | collective-permute-start | bytes 294920 | tf_op jit(solution)/shard_map/ppermute | solution.py:26
  77.8 0.0 collective-permute-done.10.refs_10_
  77.8 1.7 %collective-permute-start.14 = (bf16[16,24,128]{2,1,0:T(8,128)(2,1)S(1)}, bf16[16,24,128]{2,1,0:T(8,128)(2,1)S(1)}, u32[]{:S(2)}, u32[]{:S(2)}) collective-permute-start(bf16[16,24,128]{2,1,0:T(8,128)(2,1)S(1)} %get-tuple-element.19.refs_7_), channel_id=1, source_target_pairs={{0,112},{16,96},{32,80},{48,64},{64,48},{80,32},{96,16},{112,0},{1... | collective-permute-start | bytes 294920 | tf_op jit(solution)/shard_map/ppermute | solution.py:26
  79.5 0.1 collective-permute-done.11.refs_11_
  79.6 0.8 collective-permute-start.8
  80.4 6.2 %collective-permute-done.12.refs_12_ = bf16[16,24,128]{2,1,0:T(8,128)(2,1)S(1)} collective-permute-done((bf16[16,24,128]{2,1,0:T(8,128)(2,1)S(1)}, bf16[16,24,128]{2,1,0:T(8,128)(2,1)S(1)}, u32[]{:S(2)}, u32[]{:S(2)}) %collective-permute-start.12) | collective-permute-done | bytes 98336 | tf_op jit(solution)/shard_map/ppermute | solution.py:26
  86.6 0.0 collective-permute-start.9
  86.6 0.0 collective-permute-done.13.refs_13_
  86.6 6.2 %collective-permute-done.14.refs_14_ = bf16[16,24,128]{2,1,0:T(8,128)(2,1)S(1)} collective-permute-done((bf16[16,24,128]{2,1,0:T(8,128)(2,1)S(1)}, bf16[16,24,128]{2,1,0:T(8,128)(2,1)S(1)}, u32[]{:S(2)}, u32[]{:S(2)}) %collective-permute-start.14) | collective-permute-done | bytes 98336 | tf_op jit(solution)/shard_map/ppermute | solution.py:26
  92.8 0.0 collective-permute-done.8.refs_8_
  92.8 0.0 collective-permute-done.9.refs_9_
  92.8 0.0 collective-permute-done.3.refs_1_
  92.8 1.0 shard_map.134
  93.8 14.5 %all_to_all.20.refs_0_ = bf16[8,200,128]{2,1,0:T(8,128)(2,1)S(1)} all-to-all(bf16[8,200,128]{2,1,0:T(8,128)(2,1)S(1)} %get-tuple-element.20), channel_id=1, replica_groups=mesh['parts'=2,'y'=8,'x'=8,'c'=2] {'y'}, dimensions={0} | all-to-all | bytes 819200 | tf_op jit(solution)/shard_map/all_to_all | solution.py:22
  108.3 0.8 shard_map.135
  109.0 10.9 %all-to-all-start.3 = ((bf16[16,40,128]{2,1,0:T(8,128)(2,1)}), bf16[16,40,128]{2,1,0:T(8,128)(2,1)S(1)}, u32[]{:S(2)}, u32[]{:S(2)}) async-start(bf16[16,40,128]{2,1,0:T(8,128)(2,1)} %shard_map.135), calls=%async_computation.3 | async-start | bytes 327680 | tf_op jit(solution)/shard_map/all_to_all | solution.py:22
  119.9 0.8 shard_map.136
  120.7 8.7 %all-to-all-done.3.refs_0_ = bf16[16,40,128]{2,1,0:T(8,128)(2,1)S(1)} async-done(((bf16[16,40,128]{2,1,0:T(8,128)(2,1)}), bf16[16,40,128]{2,1,0:T(8,128)(2,1)S(1)}, u32[]{:S(2)}, u32[]{:S(2)}) %all-to-all-start.3) | async-done | bytes 163872 | tf_op jit(solution)/shard_map/all_to_all | solution.py:22
  129.4 0.7 shard_map.137
  (5 shorter events, 0.1 us)
Async XLA Ops:
  2.4 8.6 %collective-permute-start = (bf16[40,1024]{1,0:T(8,128)(2,1)S(1)}, bf16[40,1024]{1,0:T(8,128)(2,1)S(1)}, u32[]{:S(2)}, u32[]{:S(2)}) collective-permute-start(bf16[40,1024]{1,0:T(8,128)(2,1)S(1)} %get-tuple-element.15.own), channel_id=1, source_target_pairs={{0,8},{2,10},{4,12},{6,14},{8,0},{10,2},{12,4},{14,6},{1,9},{3,11}... | collective-permute-start | bytes 245768 | tf_op jit(solution)/shard_map/ppermute | solution.py:26
  11.1 9.4 %collective-permute-start.1 = (bf16[2,40,1024]{2,1,0:T(8,128)(2,1)S(1)}, bf16[2,40,1024]{2,1,0:T(8,128)(2,1)S(1)}, u32[]{:S(2)}, u32[]{:S(2)}) collective-permute-start(bf16[2,40,1024]{2,1,0:T(8,128)(2,1)S(1)} %shard_map.129.own), channel_id=1, source_target_pairs={{0,4},{2,6},{4,0},{6,2},{8,12},{10,14},{12,8},{14,10},{1,5},{3,7},... | collective-permute-start | bytes 491528 | tf_op jit(solution)/shard_map/ppermute | solution.py:26
  20.5 41.2 %collective-permute-start.2 = (bf16[4,40,1024]{2,1,0:T(8,128)(2,1)S(1)}, bf16[4,40,1024]{2,1,0:T(8,128)(2,1)S(1)}, u32[]{:S(2)}, u32[]{:S(2)}) collective-permute-start(bf16[4,40,1024]{2,1,0:T(8,128)(2,1)S(1)} %shard_map.130), channel_id=1, source_target_pairs={{0,2},{2,0},{4,6},{6,4},{8,10},{10,8},{12,14},{14,12},{1,3},{3,1},... | collective-permute-start | bytes 983048 | tf_op jit(solution)/shard_map/ppermute | solution.py:26
  20.6 36.6 %all-to-all-start = ((bf16[16,32,128]{2,1,0:T(8,128)(2,1)}), bf16[16,32,128]{2,1,0:T(8,128)(2,1)S(1)}, u32[]{:S(2)}, u32[]{:S(2)}) async-start(bf16[16,32,128]{2,1,0:T(8,128)(2,1)} %get-tuple-element.17), calls=%async_computation | async-start | bytes 262144 | tf_op jit(solution)/shard_map/all_to_all | solution.py:22
  42.1 10.0 %collective-permute-start.4 = (bf16[16,1024]{1,0:T(8,128)(2,1)S(1)}, bf16[16,1024]{1,0:T(8,128)(2,1)S(1)}, u32[]{:S(2)}, u32[]{:S(2)}) collective-permute-start(bf16[16,1024]{1,0:T(8,128)(2,1)S(1)} %get-tuple-element.16), channel_id=1, source_target_pairs={{0,8},{2,10},{4,12},{6,14},{8,0},{10,2},{12,4},{14,6},{1,9},{3,11}... | collective-permute-start | bytes 98312 | tf_op jit(solution)/shard_map/ppermute | solution.py:26
  52.1 4.8 %collective-permute-start.5 = (bf16[2,16,1024]{2,1,0:T(8,128)(2,1)S(1)}, bf16[2,16,1024]{2,1,0:T(8,128)(2,1)S(1)}, u32[]{:S(2)}, u32[]{:S(2)}) collective-permute-start(bf16[2,16,1024]{2,1,0:T(8,128)(2,1)S(1)} %pad_maximum_fusion.2.own), channel_id=1, source_target_pairs={{0,4},{2,6},{4,0},{6,2},{8,12},{10,14},{12,8},{14,10},{1,5},{3,7},... | collective-permute-start | bytes 196616 | tf_op jit(solution)/shard_map/ppermute | solution.py:26
  56.9 7.3 %collective-permute-start.6 = (bf16[4,16,1024]{2,1,0:T(8,128)(2,1)S(1)}, bf16[4,16,1024]{2,1,0:T(8,128)(2,1)S(1)}, u32[]{:S(2)}, u32[]{:S(2)}) collective-permute-start(bf16[4,16,1024]{2,1,0:T(8,128)(2,1)S(1)} %shard_map.131), channel_id=1, source_target_pairs={{0,2},{2,0},{4,6},{6,4},{8,10},{10,8},{12,14},{14,12},{1,3},{3,1},... | collective-permute-start | bytes 393224 | tf_op jit(solution)/shard_map/ppermute | solution.py:26
  58.0 12.8 %all-to-all-start.1 = ((bf16[8,16,8,128]{3,2,1,0:T(8,128)(2,1)}), bf16[8,16,8,128]{3,2,1,0:T(8,128)(2,1)S(1)}, u32[]{:S(2)}, u32[]{:S(2)}) async-start(bf16[8,16,8,128]{3,2,1,0:T(8,128)(2,1)} %shard_map.132), calls=%async_computation.1 | async-start | bytes 524288 | tf_op jit(solution)/shard_map/all_to_all | solution.py:22
  61.7 31.1 %collective-permute-start.3 = (bf16[8,40,1024]{2,1,0:T(8,128)(2,1)S(1)}, bf16[8,40,1024]{2,1,0:T(8,128)(2,1)S(1)}, u32[]{:S(2)}, u32[]{:S(2)}) collective-permute-start(bf16[8,40,1024]{2,1,0:T(8,128)(2,1)S(1)} %pad_maximum_fusion.refs_0_), channel_id=1, source_target_pairs={{0,1},{1,0},{2,3},{3,2},{4,5},{5,4},{6,7},{7,6},{8,9},{9,8},{10,11... | collective-permute-start | bytes 1966088 | tf_op jit(solution)/shard_map/ppermute | solution.py:26
  64.3 2.1 %collective-permute-start.7 = (bf16[8,16,1024]{2,1,0:T(8,128)(2,1)S(1)}, bf16[8,16,1024]{2,1,0:T(8,128)(2,1)S(1)}, u32[]{:S(2)}, u32[]{:S(2)}) collective-permute-start(bf16[8,16,1024]{2,1,0:T(8,128)(2,1)S(1)} %pad_maximum_fusion.1.refs_2_), channel_id=1, source_target_pairs={{0,1},{1,0},{2,3},{3,2},{4,5},{5,4},{6,7},{7,6},{8,9},{9,8},{10,11... | collective-permute-start | bytes 786440 | tf_op jit(solution)/shard_map/ppermute | solution.py:26
  71.1 6.7 %collective-permute-start.10 = (bf16[16,24,128]{2,1,0:T(8,128)(2,1)S(1)}, bf16[16,24,128]{2,1,0:T(8,128)(2,1)S(1)}, u32[]{:S(2)}, u32[]{:S(2)}) collective-permute-start(bf16[16,24,128]{2,1,0:T(8,128)(2,1)S(1)} %get-tuple-element.19.refs_7_), channel_id=1, source_target_pairs={{0,48},{16,32},{32,16},{48,0},{64,112},{80,96},{96,80},{112,64},{1... | collective-permute-start | bytes 294920 | tf_op jit(solution)/shard_map/ppermute | solution.py:26
  71.5 8.2 %collective-permute-start.11 = (bf16[16,24,128]{2,1,0:T(8,128)(2,1)S(1)}, bf16[16,24,128]{2,1,0:T(8,128)(2,1)S(1)}, u32[]{:S(2)}, u32[]{:S(2)}) collective-permute-start(bf16[16,24,128]{2,1,0:T(8,128)(2,1)S(1)} %get-tuple-element.19.refs_7_), channel_id=1, source_target_pairs={{0,64},{16,80},{32,96},{48,112},{64,0},{80,16},{96,32},{112,48},{1... | collective-permute-start | bytes 294920 | tf_op jit(solution)/shard_map/ppermute | solution.py:26
  73.0 13.6 %collective-permute-start.12 = (bf16[16,24,128]{2,1,0:T(8,128)(2,1)S(1)}, bf16[16,24,128]{2,1,0:T(8,128)(2,1)S(1)}, u32[]{:S(2)}, u32[]{:S(2)}) collective-permute-start(bf16[16,24,128]{2,1,0:T(8,128)(2,1)S(1)} %get-tuple-element.19.refs_7_), channel_id=1, source_target_pairs={{0,80},{16,64},{32,112},{48,96},{64,16},{80,0},{96,48},{112,32},{1... | collective-permute-start | bytes 294920 | tf_op jit(solution)/shard_map/ppermute | solution.py:26
  75.6 11.0 %collective-permute-start.13 = (bf16[16,24,128]{2,1,0:T(8,128)(2,1)S(1)}, bf16[16,24,128]{2,1,0:T(8,128)(2,1)S(1)}, u32[]{:S(2)}, u32[]{:S(2)}) collective-permute-start(bf16[16,24,128]{2,1,0:T(8,128)(2,1)S(1)} %get-tuple-element.19.refs_7_), channel_id=1, source_target_pairs={{0,96},{16,112},{32,64},{48,80},{64,32},{80,48},{96,0},{112,16},{1... | collective-permute-start | bytes 294920 | tf_op jit(solution)/shard_map/ppermute | solution.py:26
  77.8 15.0 %collective-permute-start.14 = (bf16[16,24,128]{2,1,0:T(8,128)(2,1)S(1)}, bf16[16,24,128]{2,1,0:T(8,128)(2,1)S(1)}, u32[]{:S(2)}, u32[]{:S(2)}) collective-permute-start(bf16[16,24,128]{2,1,0:T(8,128)(2,1)S(1)} %get-tuple-element.19.refs_7_), channel_id=1, source_target_pairs={{0,112},{16,96},{32,80},{48,64},{64,48},{80,32},{96,16},{112,0},{1... | collective-permute-start | bytes 294920 | tf_op jit(solution)/shard_map/ppermute | solution.py:26
  79.6 13.2 %collective-permute-start.8 = (bf16[16,24,128]{2,1,0:T(8,128)(2,1)S(1)}, bf16[16,24,128]{2,1,0:T(8,128)(2,1)S(1)}, u32[]{:S(2)}, u32[]{:S(2)}) collective-permute-start(bf16[16,24,128]{2,1,0:T(8,128)(2,1)S(1)} %get-tuple-element.19.refs_7_), channel_id=1, source_target_pairs={{0,16},{16,0},{32,48},{48,32},{64,80},{80,64},{96,112},{112,96},{1... | collective-permute-start | bytes 294920 | tf_op jit(solution)/shard_map/ppermute | solution.py:26
  86.6 6.2 %collective-permute-start.9 = (bf16[16,24,128]{2,1,0:T(8,128)(2,1)S(1)}, bf16[16,24,128]{2,1,0:T(8,128)(2,1)S(1)}, u32[]{:S(2)}, u32[]{:S(2)}) collective-permute-start(bf16[16,24,128]{2,1,0:T(8,128)(2,1)S(1)} %get-tuple-element.19.refs_7_), channel_id=1, source_target_pairs={{0,32},{16,48},{32,0},{48,16},{64,96},{80,112},{96,64},{112,80},{1... | collective-permute-start | bytes 294920 | tf_op jit(solution)/shard_map/ppermute | solution.py:26
  109.0 20.4 %all-to-all-start.3 = ((bf16[16,40,128]{2,1,0:T(8,128)(2,1)}), bf16[16,40,128]{2,1,0:T(8,128)(2,1)S(1)}, u32[]{:S(2)}, u32[]{:S(2)}) async-start(bf16[16,40,128]{2,1,0:T(8,128)(2,1)} %shard_map.135), calls=%async_computation.3 | async-start | bytes 327680 | tf_op jit(solution)/shard_map/all_to_all | solution.py:22

commit v9 on v8

--- a/solution.py
+++ b/solution.py
@@ -114,16 +114,14 @@
     rows[2 * rt : 2 * rt + rp, :] = dinv[...].astype(BF16)
 
 
-def copy_kernel(*refs):
-    sources, results, scratch, done = refs[:2], refs[2:4], refs[4:6], refs[6]
-    fetched(sources, scratch, done)
-    for result, value in zip(results, scratch):
-        result[...] = value[...]
-
-
-def stack_kernel(own, other, stacked):
-    stacked[0] = own[...]
-    stacked[1] = other[...]
+def copy_kernel(source_hbm, result, scratch, done):
+    fetched((source_hbm,), (scratch,), done)
+    result[...] = scratch[...]
+
+
+def stack_kernel(own, other, *refs):
+    refs[-1][0] = own[...]
+    refs[-1][1] = other[...]
 
 
 def join_kernel(own, other, joined):
@@ -305,10 +303,14 @@
     cols = exchanged(slots, XC)
     par_far = swapped(par_rows, "x", 4)
     far_rows = swapped(rows, "x", 4)
-    pair = (dvar_kid, dinv_par)
-    dvar_kid, dinv_par = fetching(copy_kernel, [(a.shape, F32) for a in pair], pair)
+    (dvar_kid,) = fetching(copy_kernel, [(dvar_kid.shape, F32)], (dvar_kid,))
     (tall_send,) = call(repeat_kernel, [((ny, nj, rp, LANES), BF16)], (cols,))
-    par_rows = jnp.stack([par_rows, par_far])
+    (par_rows,) = call(
+        stack_kernel,
+        [((2, rt, w1), BF16)],
+        (par_rows, par_far, tall_send),
+        [VMEM, VMEM, pl.BlockSpec(memory_space=pl.ANY)],
+    )
     par_far = swapped(par_rows, "x", 2)
     tall = exchanged(tall_send, "y")
     (rows,) = call(stack_kernel, [((2, 2 * rt + rp, w1), BF16)], (rows, far_rows))

time: 131 us -> 129 us (0.985)
  waiting for transfers between devices: 44.3 us -> 35.4 us
  blocking collectives: 14.5 us -> 19.2 us
  starting transfers between devices: 64.4 us -> 67 us
    ppermute x15, waiting for transfers between devices: 31.1 us -> 19.6 us  [swapped(): lax.ppermute(x, axis, [(i, i ^ bit) for i in range(lax.axis_size(axis))])]
    ppermute x15, starting transfers between devices: 28.5 us -> 36.2 us  [swapped(): lax.ppermute(x, axis, [(i, i ^ bit) for i in range(lax.axis_size(axis))])]
    all_to_all x3, starting transfers between devices: 35.9 us -> 30.9 us  [exchanged(): return lax.all_to_all(x, axes, split_axis=0, concat_axis=0, tiled=True)]
    all_to_all x1, blocking collectives: 14.5 us -> 19.2 us  [exchanged(): return lax.all_to_all(x, axes, split_axis=0, concat_axis=0, tiled=True)]
    all_to_all x3, waiting for transfers between devices: 13.2 us -> 15.7 us  [exchanged(): return lax.all_to_all(x, axes, split_axis=0, concat_axis=0, tiled=True)]
    pallas_call x10 -> x11, Pallas kernels: 6.12 us -> 6.04 us  [call(): pl.pallas_call(kernel, out_shape=tuple((jax.ShapeDtypeStruct(s, d) for s,...]
where the time goes in v9:
time: 129 us
  starting transfers between devices  67 us (52%)
  waiting for transfers between devices  35.4 us (27%)
  blocking collectives  19.2 us (15%)
  Pallas kernels  6.04 us (5%)
    ppermute x15, starting transfers between devices, swapped(): lax.ppermute(x, axis, [(i, i ^ bit) for i in range(lax.axis_size(axis))])  36.2 us
    all_to_all x3, starting transfers between devices, exchanged(): return lax.all_to_all(x, axes, split_axis=0, concat_axis=0, tiled=True)  30.9 us
    ppermute x15, waiting for transfers between devices, swapped(): lax.ppermute(x, axis, [(i, i ^ bit) for i in range(lax.axis_size(axis))])  19.6 us
    all_to_all x1, blocking collectives, exchanged(): return lax.all_to_all(x, axes, split_axis=0, concat_axis=0, tiled=True)  19.2 us
    all_to_all x3, waiting for transfers between devices, exchanged(): return lax.all_to_all(x, axes, split_axis=0, concat_axis=0, tiled=True)  15.7 us
    pallas_call x11, Pallas kernels, call(): pl.pallas_call(kernel, out_shape=tuple((jax.ShapeDtypeStruct(s, d) for s,...  6.04 us
  transfers between devices with their start and end apart: 18, of which 10 were waited for; matrix products, arithmetic and copies ran while one was open for 0% of the time, Pallas kernels for 1%

profile of v9, /device:TPU:513, one launch (start us, length us, event | category | flops | bytes accessed | tf_op | source)
XLA Modules:
  0.0 128.5 jit_solution(16177469836975686420)
XLA Ops:
  0.6 1.8 %shard_map.128 = (bf16[16,32,128]{2,1,0:T(8,128)(2,1)}, bf16[16,1024]{1,0:T(8,128)(2,1)S(1)}, bf16[40,1024]{1,0:T(8,128)(2,1)S(1)}) custom-call(bf16[16,2048]{1,0:T(8,128)(2,1)} %refs_0_.1, bf16[16,1024]{1,0:T(8,128)(2,1)} %refs_1_.2, f32[8,1024]{1,0:T(8,128)} %refs_1_.3, bf16[2,16,1024]{2,1,0:T(8,128)(2,1)} %refs_3_.1, bf16[2,8,1024]{2,1,0:T(8,128)(2,1)} %refs_4_.1, ...), custom_call_target="tpu_custom_call" | custom-call | tf_op jit(solution)/shard_map/pallas_call | solution.py:56
  2.4 6.7 %collective-permute-start = (bf16[40,1024]{1,0:T(8,128)(2,1)S(1)}, bf16[40,1024]{1,0:T(8,128)(2,1)S(1)}, u32[]{:S(2)}, u32[]{:S(2)}) collective-permute-start(bf16[40,1024]{1,0:T(8,128)(2,1)S(1)} %get-tuple-element.13.own), channel_id=1, source_target_pairs={{0,8},{2,10},{4,12},{6,14},{8,0},{10,2},{12,4},{14,6},{1,9},{3,11}... | collective-permute-start | bytes 245768 | tf_op jit(solution)/shard_map/ppermute | solution.py:26
  9.1 1.9 %collective-permute-done.other = bf16[40,1024]{1,0:T(8,128)(2,1)S(1)} collective-permute-done((bf16[40,1024]{1,0:T(8,128)(2,1)S(1)}, bf16[40,1024]{1,0:T(8,128)(2,1)S(1)}, u32[]{:S(2)}, u32[]{:S(2)}) %collective-permute-start) | collective-permute-done | bytes 81952 | tf_op jit(solution)/shard_map/ppermute | solution.py:26
  11.1 3.9 %collective-permute-start.1 = (bf16[2,40,1024]{2,1,0:T(8,128)(2,1)S(1)}, bf16[2,40,1024]{2,1,0:T(8,128)(2,1)S(1)}, u32[]{:S(2)}, u32[]{:S(2)}) collective-permute-start(bf16[2,40,1024]{2,1,0:T(8,128)(2,1)S(1)} %shard_map.129.own), channel_id=1, source_target_pairs={{0,4},{2,6},{4,0},{6,2},{8,12},{10,14},{12,8},{14,10},{1,5},{3,7},... | collective-permute-start | bytes 491528 | tf_op jit(solution)/shard_map/ppermute | solution.py:26
  15.0 5.5 %collective-permute-done.1.other = bf16[2,40,1024]{2,1,0:T(8,128)(2,1)S(1)} collective-permute-done((bf16[2,40,1024]{2,1,0:T(8,128)(2,1)S(1)}, bf16[2,40,1024]{2,1,0:T(8,128)(2,1)S(1)}, u32[]{:S(2)}, u32[]{:S(2)}) %collective-permute-start.1) | collective-permute-done | bytes 163872 | tf_op jit(solution)/shard_map/ppermute | solution.py:26
  20.5 0.1 collective-permute-start.2
  20.6 21.4 %all-to-all-start = ((bf16[16,32,128]{2,1,0:T(8,128)(2,1)}), bf16[16,32,128]{2,1,0:T(8,128)(2,1)S(1)}, u32[]{:S(2)}, u32[]{:S(2)}) async-start(bf16[16,32,128]{2,1,0:T(8,128)(2,1)} %get-tuple-element.15), calls=%async_computation | async-start | bytes 262144 | tf_op jit(solution)/shard_map/all_to_all | solution.py:22
  42.1 5.4 %collective-permute-start.4 = (bf16[16,1024]{1,0:T(8,128)(2,1)S(1)}, bf16[16,1024]{1,0:T(8,128)(2,1)S(1)}, u32[]{:S(2)}, u32[]{:S(2)}) collective-permute-start(bf16[16,1024]{1,0:T(8,128)(2,1)S(1)} %get-tuple-element.14.own), channel_id=1, source_target_pairs={{0,8},{2,10},{4,12},{6,14},{8,0},{10,2},{12,4},{14,6},{1,9},{3,11}... | collective-permute-start | bytes 98312 | tf_op jit(solution)/shard_map/ppermute | solution.py:26
  47.5 4.1 %all-to-all-done.cols.refs_0_.refs_5_ = bf16[16,32,128]{2,1,0:T(8,128)(2,1)S(1)} async-done(((bf16[16,32,128]{2,1,0:T(8,128)(2,1)}), bf16[16,32,128]{2,1,0:T(8,128)(2,1)S(1)}, u32[]{:S(2)}, u32[]{:S(2)}) %all-to-all-start) | async-done | bytes 131104 | tf_op jit(solution)/shard_map/all_to_all | solution.py:22
  51.5 0.7 shard_map.131.refs_0_
  52.3 0.0 collective-permute-done.4.other
  52.3 0.5 collective-permute-start.5
  52.8 3.6 %all-to-all-start.1 = ((bf16[8,16,8,128]{3,2,1,0:T(8,128)(2,1)}), bf16[8,16,8,128]{3,2,1,0:T(8,128)(2,1)S(1)}, u32[]{:S(2)}, u32[]{:S(2)}) async-start(bf16[8,16,8,128]{3,2,1,0:T(8,128)(2,1)} %shard_map.131.refs_0_), calls=%async_computation.1 | async-start | bytes 524288 | tf_op jit(solution)/shard_map/all_to_all | solution.py:22
  56.4 1.2 collective-permute-done.5.other
  57.7 0.1 collective-permute-start.6
  57.8 0.0 collective-permute-done.2
  57.8 0.1 pad_maximum_fusion.refs_0_
  57.9 1.8 %collective-permute-start.3 = (bf16[8,40,1024]{2,1,0:T(8,128)(2,1)S(1)}, bf16[8,40,1024]{2,1,0:T(8,128)(2,1)S(1)}, u32[]{:S(2)}, u32[]{:S(2)}) collective-permute-start(bf16[8,40,1024]{2,1,0:T(8,128)(2,1)S(1)} %pad_maximum_fusion.refs_0_), channel_id=1, source_target_pairs={{0,1},{1,0},{2,3},{3,2},{4,5},{5,4},{6,7},{7,6},{8,9},{9,8},{10,11... | collective-permute-start | bytes 1966088 | tf_op jit(solution)/shard_map/ppermute | solution.py:26
  59.7 1.9 %collective-permute-done.6 = bf16[4,16,1024]{2,1,0:T(8,128)(2,1)S(1)} collective-permute-done((bf16[4,16,1024]{2,1,0:T(8,128)(2,1)S(1)}, bf16[4,16,1024]{2,1,0:T(8,128)(2,1)S(1)}, u32[]{:S(2)}, u32[]{:S(2)}) %collective-permute-start.6) | collective-permute-done | bytes 131104 | tf_op jit(solution)/shard_map/ppermute | solution.py:26
  61.6 2.9 %collective-permute-start.7 = (bf16[8,16,1024]{2,1,0:T(8,128)(2,1)S(1)}, bf16[8,16,1024]{2,1,0:T(8,128)(2,1)S(1)}, u32[]{:S(2)}, u32[]{:S(2)}) collective-permute-start(bf16[8,16,1024]{2,1,0:T(8,128)(2,1)S(1)} %pad_maximum_fusion.1.refs_2_), channel_id=1, source_target_pairs={{0,1},{1,0},{2,3},{3,2},{4,5},{5,4},{6,7},{7,6},{8,9},{9,8},{10,11... | collective-permute-start | bytes 786440 | tf_op jit(solution)/shard_map/ppermute | solution.py:26
  64.5 1.2 collective-permute-done.7.refs_3_
  65.6 2.4 %all-to-all-done.1.refs_1_.refs_4_ = bf16[8,16,8,128]{3,2,1,0:T(8,128)(2,1)S(1)} async-done(((bf16[8,16,8,128]{3,2,1,0:T(8,128)(2,1)}), bf16[8,16,8,128]{3,2,1,0:T(8,128)(2,1)S(1)}, u32[]{:S(2)}, u32[]{:S(2)}) %all-to-all-start.1) | async-done | bytes 262176 | tf_op jit(solution)/shard_map/all_to_all | solution.py:22
  68.1 0.3 shard_map.134
  68.4 0.1 collective-permute-start.10
  68.5 1.2 collective-permute-start.11
  69.7 2.0 %collective-permute-start.12 = (bf16[16,24,128]{2,1,0:T(8,128)(2,1)S(1)}, bf16[16,24,128]{2,1,0:T(8,128)(2,1)S(1)}, u32[]{:S(2)}, u32[]{:S(2)}) collective-permute-start(bf16[16,24,128]{2,1,0:T(8,128)(2,1)S(1)} %get-tuple-element.17.refs_7_), channel_id=1, source_target_pairs={{0,80},{16,64},{32,112},{48,96},{64,16},{80,0},{96,48},{112,32},{1... | collective-permute-start | bytes 294920 | tf_op jit(solution)/shard_map/ppermute | solution.py:26
  71.7 3.3 %collective-permute-start.13 = (bf16[16,24,128]{2,1,0:T(8,128)(2,1)S(1)}, bf16[16,24,128]{2,1,0:T(8,128)(2,1)S(1)}, u32[]{:S(2)}, u32[]{:S(2)}) collective-permute-start(bf16[16,24,128]{2,1,0:T(8,128)(2,1)S(1)} %get-tuple-element.17.refs_7_), channel_id=1, source_target_pairs={{0,96},{16,112},{32,64},{48,80},{64,32},{80,48},{96,0},{112,16},{1... | collective-permute-start | bytes 294920 | tf_op jit(solution)/shard_map/ppermute | solution.py:26
  75.0 0.0 collective-permute-done.10.refs_10_
  75.0 1.7 %collective-permute-start.14 = (bf16[16,24,128]{2,1,0:T(8,128)(2,1)S(1)}, bf16[16,24,128]{2,1,0:T(8,128)(2,1)S(1)}, u32[]{:S(2)}, u32[]{:S(2)}) collective-permute-start(bf16[16,24,128]{2,1,0:T(8,128)(2,1)S(1)} %get-tuple-element.17.refs_7_), channel_id=1, source_target_pairs={{0,112},{16,96},{32,80},{48,64},{64,48},{80,32},{96,16},{112,0},{1... | collective-permute-start | bytes 294920 | tf_op jit(solution)/shard_map/ppermute | solution.py:26
  76.7 0.0 collective-permute-done.11.refs_11_
  76.7 0.6 collective-permute-start.8
  77.3 4.7 %collective-permute-done.12.refs_12_ = bf16[16,24,128]{2,1,0:T(8,128)(2,1)S(1)} collective-permute-done((bf16[16,24,128]{2,1,0:T(8,128)(2,1)S(1)}, bf16[16,24,128]{2,1,0:T(8,128)(2,1)S(1)}, u32[]{:S(2)}, u32[]{:S(2)}) %collective-permute-start.12) | collective-permute-done | bytes 98336 | tf_op jit(solution)/shard_map/ppermute | solution.py:26
  82.0 5.8 %collective-permute-start.9 = (bf16[16,24,128]{2,1,0:T(8,128)(2,1)S(1)}, bf16[16,24,128]{2,1,0:T(8,128)(2,1)S(1)}, u32[]{:S(2)}, u32[]{:S(2)}) collective-permute-start(bf16[16,24,128]{2,1,0:T(8,128)(2,1)S(1)} %get-tuple-element.17.refs_7_), channel_id=1, source_target_pairs={{0,32},{16,48},{32,0},{48,16},{64,96},{80,112},{96,64},{112,80},{1... | collective-permute-start | bytes 294920 | tf_op jit(solution)/shard_map/ppermute | solution.py:26
  87.8 0.0 collective-permute-done.13.refs_13_
  87.8 3.2 %collective-permute-done.14.refs_14_ = bf16[16,24,128]{2,1,0:T(8,128)(2,1)S(1)} collective-permute-done((bf16[16,24,128]{2,1,0:T(8,128)(2,1)S(1)}, bf16[16,24,128]{2,1,0:T(8,128)(2,1)S(1)}, u32[]{:S(2)}, u32[]{:S(2)}) %collective-permute-start.14) | collective-permute-done | bytes 98336 | tf_op jit(solution)/shard_map/ppermute | solution.py:26
  91.0 0.0 collective-permute-done.8.refs_8_
  91.0 0.0 collective-permute-done.9.refs_9_
  91.0 0.0 collective-permute-done.3.refs_1_
  91.0 1.0 shard_map.135
  92.0 19.2 %all_to_all.20.refs_0_ = bf16[8,200,128]{2,1,0:T(8,128)(2,1)S(1)} all-to-all(bf16[8,200,128]{2,1,0:T(8,128)(2,1)S(1)} %get-tuple-element.18), channel_id=1, replica_groups=mesh['parts'=2,'y'=8,'x'=8,'c'=2] {'y'}, dimensions={0} | all-to-all | bytes 819200 | tf_op jit(solution)/shard_map/all_to_all | solution.py:22
  111.2 0.8 shard_map.136
  112.0 0.0 copy-start
  112.0 5.8 %all-to-all-start.3 = ((bf16[16,40,128]{2,1,0:T(8,128)(2,1)}), bf16[16,40,128]{2,1,0:T(8,128)(2,1)S(1)}, u32[]{:S(2)}, u32[]{:S(2)}) async-start(bf16[16,40,128]{2,1,0:T(8,128)(2,1)} %shard_map.136), calls=%async_computation.3 | async-start | bytes 327680 | tf_op jit(solution)/shard_map/all_to_all | solution.py:22
  117.8 0.7 shard_map.137.refs_2_
  118.5 9.3 %all-to-all-done.3.refs_0_ = bf16[16,40,128]{2,1,0:T(8,128)(2,1)S(1)} async-done(((bf16[16,40,128]{2,1,0:T(8,128)(2,1)}), bf16[16,40,128]{2,1,0:T(8,128)(2,1)S(1)}, u32[]{:S(2)}, u32[]{:S(2)}) %all-to-all-start.3) | async-done | bytes 163872 | tf_op jit(solution)/shard_map/all_to_all | solution.py:22
  127.8 0.0 copy-done
  127.8 0.7 shard_map.138
  (5 shorter events, 0.1 us)
Async XLA Ops:
  2.4 8.6 %collective-permute-start = (bf16[40,1024]{1,0:T(8,128)(2,1)S(1)}, bf16[40,1024]{1,0:T(8,128)(2,1)S(1)}, u32[]{:S(2)}, u32[]{:S(2)}) collective-permute-start(bf16[40,1024]{1,0:T(8,128)(2,1)S(1)} %get-tuple-element.13.own), channel_id=1, source_target_pairs={{0,8},{2,10},{4,12},{6,14},{8,0},{10,2},{12,4},{14,6},{1,9},{3,11}... | collective-permute-start | bytes 245768 | tf_op jit(solution)/shard_map/ppermute | solution.py:26
  11.1 9.4 %collective-permute-start.1 = (bf16[2,40,1024]{2,1,0:T(8,128)(2,1)S(1)}, bf16[2,40,1024]{2,1,0:T(8,128)(2,1)S(1)}, u32[]{:S(2)}, u32[]{:S(2)}) collective-permute-start(bf16[2,40,1024]{2,1,0:T(8,128)(2,1)S(1)} %shard_map.129.own), channel_id=1, source_target_pairs={{0,4},{2,6},{4,0},{6,2},{8,12},{10,14},{12,8},{14,10},{1,5},{3,7},... | collective-permute-start | bytes 491528 | tf_op jit(solution)/shard_map/ppermute | solution.py:26
  20.5 37.3 %collective-permute-start.2 = (bf16[4,40,1024]{2,1,0:T(8,128)(2,1)S(1)}, bf16[4,40,1024]{2,1,0:T(8,128)(2,1)S(1)}, u32[]{:S(2)}, u32[]{:S(2)}) collective-permute-start(bf16[4,40,1024]{2,1,0:T(8,128)(2,1)S(1)} %shard_map.130), channel_id=1, source_target_pairs={{0,2},{2,0},{4,6},{6,4},{8,10},{10,8},{12,14},{14,12},{1,3},{3,1},... | collective-permute-start | bytes 983048 | tf_op jit(solution)/shard_map/ppermute | solution.py:26
  20.6 30.9 %all-to-all-start = ((bf16[16,32,128]{2,1,0:T(8,128)(2,1)}), bf16[16,32,128]{2,1,0:T(8,128)(2,1)S(1)}, u32[]{:S(2)}, u32[]{:S(2)}) async-start(bf16[16,32,128]{2,1,0:T(8,128)(2,1)} %get-tuple-element.15), calls=%async_computation | async-start | bytes 262144 | tf_op jit(solution)/shard_map/all_to_all | solution.py:22
  42.1 10.2 %collective-permute-start.4 = (bf16[16,1024]{1,0:T(8,128)(2,1)S(1)}, bf16[16,1024]{1,0:T(8,128)(2,1)S(1)}, u32[]{:S(2)}, u32[]{:S(2)}) collective-permute-start(bf16[16,1024]{1,0:T(8,128)(2,1)S(1)} %get-tuple-element.14.own), channel_id=1, source_target_pairs={{0,8},{2,10},{4,12},{6,14},{8,0},{10,2},{12,4},{14,6},{1,9},{3,11}... | collective-permute-start | bytes 98312 | tf_op jit(solution)/shard_map/ppermute | solution.py:26
  52.3 5.3 %collective-permute-start.5 = (bf16[2,16,1024]{2,1,0:T(8,128)(2,1)S(1)}, bf16[2,16,1024]{2,1,0:T(8,128)(2,1)S(1)}, u32[]{:S(2)}, u32[]{:S(2)}) collective-permute-start(bf16[2,16,1024]{2,1,0:T(8,128)(2,1)S(1)} %shard_map.132.own), channel_id=1, source_target_pairs={{0,4},{2,6},{4,0},{6,2},{8,12},{10,14},{12,8},{14,10},{1,5},{3,7},... | collective-permute-start | bytes 196616 | tf_op jit(solution)/shard_map/ppermute | solution.py:26
  52.8 15.3 %all-to-all-start.1 = ((bf16[8,16,8,128]{3,2,1,0:T(8,128)(2,1)}), bf16[8,16,8,128]{3,2,1,0:T(8,128)(2,1)S(1)}, u32[]{:S(2)}, u32[]{:S(2)}) async-start(bf16[8,16,8,128]{3,2,1,0:T(8,128)(2,1)} %shard_map.131.refs_0_), calls=%async_computation.1 | async-start | bytes 524288 | tf_op jit(solution)/shard_map/all_to_all | solution.py:22
  57.7 3.9 %collective-permute-start.6 = (bf16[4,16,1024]{2,1,0:T(8,128)(2,1)S(1)}, bf16[4,16,1024]{2,1,0:T(8,128)(2,1)S(1)}, u32[]{:S(2)}, u32[]{:S(2)}) collective-permute-start(bf16[4,16,1024]{2,1,0:T(8,128)(2,1)S(1)} %shard_map.133), channel_id=1, source_target_pairs={{0,2},{2,0},{4,6},{6,4},{8,10},{10,8},{12,14},{14,12},{1,3},{3,1},... | collective-permute-start | bytes 393224 | tf_op jit(solution)/shard_map/ppermute | solution.py:26
  57.9 33.1 %collective-permute-start.3 = (bf16[8,40,1024]{2,1,0:T(8,128)(2,1)S(1)}, bf16[8,40,1024]{2,1,0:T(8,128)(2,1)S(1)}, u32[]{:S(2)}, u32[]{:S(2)}) collective-permute-start(bf16[8,40,1024]{2,1,0:T(8,128)(2,1)S(1)} %pad_maximum_fusion.refs_0_), channel_id=1, source_target_pairs={{0,1},{1,0},{2,3},{3,2},{4,5},{5,4},{6,7},{7,6},{8,9},{9,8},{10,11... | collective-permute-start | bytes 1966088 | tf_op jit(solution)/shard_map/ppermute | solution.py:26
  61.6 4.0 %collective-permute-start.7 = (bf16[8,16,1024]{2,1,0:T(8,128)(2,1)S(1)}, bf16[8,16,1024]{2,1,0:T(8,128)(2,1)S(1)}, u32[]{:S(2)}, u32[]{:S(2)}) collective-permute-start(bf16[8,16,1024]{2,1,0:T(8,128)(2,1)S(1)} %pad_maximum_fusion.1.refs_2_), channel_id=1, source_target_pairs={{0,1},{1,0},{2,3},{3,2},{4,5},{5,4},{6,7},{7,6},{8,9},{9,8},{10,11... | collective-permute-start | bytes 786440 | tf_op jit(solution)/shard_map/ppermute | solution.py:26
  68.4 6.6 %collective-permute-start.10 = (bf16[16,24,128]{2,1,0:T(8,128)(2,1)S(1)}, bf16[16,24,128]{2,1,0:T(8,128)(2,1)S(1)}, u32[]{:S(2)}, u32[]{:S(2)}) collective-permute-start(bf16[16,24,128]{2,1,0:T(8,128)(2,1)S(1)} %get-tuple-element.17.refs_7_), channel_id=1, source_target_pairs={{0,48},{16,32},{32,16},{48,0},{64,112},{80,96},{96,80},{112,64},{1... | collective-permute-start | bytes 294920 | tf_op jit(solution)/shard_map/ppermute | solution.py:26
  68.5 8.2 %collective-permute-start.11 = (bf16[16,24,128]{2,1,0:T(8,128)(2,1)S(1)}, bf16[16,24,128]{2,1,0:T(8,128)(2,1)S(1)}, u32[]{:S(2)}, u32[]{:S(2)}) collective-permute-start(bf16[16,24,128]{2,1,0:T(8,128)(2,1)S(1)} %get-tuple-element.17.refs_7_), channel_id=1, source_target_pairs={{0,64},{16,80},{32,96},{48,112},{64,0},{80,16},{96,32},{112,48},{1... | collective-permute-start | bytes 294920 | tf_op jit(solution)/shard_map/ppermute | solution.py:26
  69.7 12.3 %collective-permute-start.12 = (bf16[16,24,128]{2,1,0:T(8,128)(2,1)S(1)}, bf16[16,24,128]{2,1,0:T(8,128)(2,1)S(1)}, u32[]{:S(2)}, u32[]{:S(2)}) collective-permute-start(bf16[16,24,128]{2,1,0:T(8,128)(2,1)S(1)} %get-tuple-element.17.refs_7_), channel_id=1, source_target_pairs={{0,80},{16,64},{32,112},{48,96},{64,16},{80,0},{96,48},{112,32},{1... | collective-permute-start | bytes 294920 | tf_op jit(solution)/shard_map/ppermute | solution.py:26
  71.7 16.1 %collective-permute-start.13 = (bf16[16,24,128]{2,1,0:T(8,128)(2,1)S(1)}, bf16[16,24,128]{2,1,0:T(8,128)(2,1)S(1)}, u32[]{:S(2)}, u32[]{:S(2)}) collective-permute-start(bf16[16,24,128]{2,1,0:T(8,128)(2,1)S(1)} %get-tuple-element.17.refs_7_), channel_id=1, source_target_pairs={{0,96},{16,112},{32,64},{48,80},{64,32},{80,48},{96,0},{112,16},{1... | collective-permute-start | bytes 294920 | tf_op jit(solution)/shard_map/ppermute | solution.py:26
  75.0 16.0 %collective-permute-start.14 = (bf16[16,24,128]{2,1,0:T(8,128)(2,1)S(1)}, bf16[16,24,128]{2,1,0:T(8,128)(2,1)S(1)}, u32[]{:S(2)}, u32[]{:S(2)}) collective-permute-start(bf16[16,24,128]{2,1,0:T(8,128)(2,1)S(1)} %get-tuple-element.17.refs_7_), channel_id=1, source_target_pairs={{0,112},{16,96},{32,80},{48,64},{64,48},{80,32},{96,16},{112,0},{1... | collective-permute-start | bytes 294920 | tf_op jit(solution)/shard_map/ppermute | solution.py:26
  76.7 14.3 %collective-permute-start.8 = (bf16[16,24,128]{2,1,0:T(8,128)(2,1)S(1)}, bf16[16,24,128]{2,1,0:T(8,128)(2,1)S(1)}, u32[]{:S(2)}, u32[]{:S(2)}) collective-permute-start(bf16[16,24,128]{2,1,0:T(8,128)(2,1)S(1)} %get-tuple-element.17.refs_7_), channel_id=1, source_target_pairs={{0,16},{16,0},{32,48},{48,32},{64,80},{80,64},{96,112},{112,96},{1... | collective-permute-start | bytes 294920 | tf_op jit(solution)/shard_map/ppermute | solution.py:26
  82.0 9.0 %collective-permute-start.9 = (bf16[16,24,128]{2,1,0:T(8,128)(2,1)S(1)}, bf16[16,24,128]{2,1,0:T(8,128)(2,1)S(1)}, u32[]{:S(2)}, u32[]{:S(2)}) collective-permute-start(bf16[16,24,128]{2,1,0:T(8,128)(2,1)S(1)} %get-tuple-element.17.refs_7_), channel_id=1, source_target_pairs={{0,32},{16,48},{32,0},{48,16},{64,96},{80,112},{96,64},{112,80},{1... | collective-permute-start | bytes 294920 | tf_op jit(solution)/shard_map/ppermute | solution.py:26
  112.0 15.8 %copy-start = (f32[8,1024]{1,0:T(8,128)S(1)}, f32[8,1024]{1,0:T(8,128)}, u32[]{:S(2)}) copy-start(f32[8,1024]{1,0:T(8,128)} %refs_1_.3) | copy-start | bytes 98308
  112.0 15.8 %all-to-all-start.3 = ((bf16[16,40,128]{2,1,0:T(8,128)(2,1)}), bf16[16,40,128]{2,1,0:T(8,128)(2,1)S(1)}, u32[]{:S(2)}, u32[]{:S(2)}) async-start(bf16[16,40,128]{2,1,0:T(8,128)(2,1)} %shard_map.136), calls=%async_computation.3 | async-start | bytes 327680 | tf_op jit(solution)/shard_map/all_to_all | solution.py:22

commit v10 on v9

--- a/solution.py
+++ b/solution.py
@@ -161,7 +161,7 @@
 
 
 def main_kernel(rt, rp, near, far, par_own, par_other, tall, cols, step, *refs):
-    steps, (slots, part, db, step_j, par_j) = refs[:-5], refs[-5:]
+    steps, slots, (part, db, step_j, par_j) = refs[:8], refs[8:16], refs[16:]
     for k, rows in enumerate(steps):
         y = jnp.bitwise_xor(lax.axis_index("y"), k)
         step_j[y] = rows[:, 0:rt, :]
@@ -198,26 +198,26 @@
         xs.append(x.astype(BF16))
 
     x = jnp.concatenate(xs, axis=0)
-    p = jnp.concatenate([p[...].reshape(nj // 2 * rt, w1) for p in (par_own, par_other)], axis=0)
-    for y in range(ny):
-        partial = dot_t(p[:, y * LANES : (y + 1) * LANES], x)
+    var_rows = jnp.concatenate(split3(var) + [jnp.zeros((5, LANES), F32)], axis=0)
+    for k, slot in enumerate(slots):
+        y = jnp.bitwise_xor(lax.axis_index("y"), k)
+        at = pl.ds(pl.multiple_of(y * LANES, LANES), LANES)
+        p = [p[:, :, at].reshape(nj // 2 * rt, LANES) for p in (par_own, par_other)]
+        partial = dot_t(jnp.concatenate(p, axis=0), x)
         rows = partial.shape[0]
-        slots[y, 0:rows, :] = partial[:, :LANES].astype(BF16)
+        slot[0:rows, :] = partial[:, :LANES].astype(BF16)
         q = partial[:, LANES:]
         q = low_high(q[: rows // 2], turned(q[rows // 2 :]))
-        slots[y, rows : rows + rows // 2, :] = q.astype(BF16)
-    var_rows = jnp.concatenate(split3(var) + [jnp.zeros((5, LANES), F32)], axis=0).astype(BF16)
-    for y in range(ny):
-        slots[y, rows + rows // 2 : rows + rows // 2 + 8, :] = var_rows
-
-
-def sum_kernel(rt, rp, received, db, part, out):
-    ny = received.shape[0]
+        slot[rows : rows + rows // 2 + 8, :] = jnp.concatenate([q, var_rows], axis=0).astype(BF16)
+
+
+def sum_kernel(rt, rp, *refs):
+    received, (db, part, out) = refs[:-3], refs[-3:]
     nj = out.shape[0]
     rows = nj * rp
-    total = received[0].astype(F32)
-    for y in range(1, ny):
-        total = total + received[y].astype(F32)
+    total = received[0][...].astype(F32)
+    for one in received[1:]:
+        total = total + one[...].astype(F32)
     q = total[rows : rows + rows // 2]
     q = jnp.concatenate([q, turned(q)], axis=0)
     first = rows + rows // 2
@@ -334,19 +334,19 @@
     for k in range(1, ny):
         steps.append(swapped(rounded, "y", k))
     rows4 = nj * rp + nj * rp // 2 + 8
-    slots4, part, db = call(
+    *partials, part, db = call(
         sized(main_kernel),
-        [((ny, rows4, LANES), BF16), ((nj, rt + rp, LANES), BF16), ((nj, rp, LANES), F32)],
+        [((rows4, LANES), BF16)] * ny
+        + [((nj, rt + rp, LANES), BF16), ((nj, rp, LANES), F32)],
         (near, far, par_own, par_other, tall, cols, step, *steps),
         scratch=[
             pltpu.VMEM((ny, nj, rt, LANES), BF16),
             pltpu.VMEM((ny, nj, rp, LANES), F32),
         ],
     )
-    received = exchanged(slots4, "y")
-    (out,) = call(
-        sized(sum_kernel), [((nj, rt + 3 * rp, LANES), BF16)], (received, db, part)
-    )
+    for k in range(1, ny):
+        partials[k] = swapped(partials[k], "y", k)
+    (out,) = call(sized(sum_kernel), [((nj, rt + 3 * rp, LANES), BF16)], (*partials, db, part))
     got = exchanged(out, XC)
     return call(
         sized(final_kernel),

time: 129 us -> 127 us (0.984)
  blocking collectives: 19.2 us -> 0 us
  starting transfers between devices: 67 us -> 79.8 us
  waiting for transfers between devices: 35.4 us -> 40.2 us
    all_to_all x1 -> x0, blocking collectives: 19.2 us -> none  [exchanged(): return lax.all_to_all(x, axes, split_axis=0, concat_axis=0, tiled=True)]
    ppermute x15 -> x22, starting transfers between devices: 36.2 us -> 49.4 us  [swapped(): lax.ppermute(x, axis, [(i, i ^ bit) for i in range(lax.axis_size(axis))])]
    ppermute x15 -> x22, waiting for transfers between devices: 19.6 us -> 24.9 us  [swapped(): lax.ppermute(x, axis, [(i, i ^ bit) for i in range(lax.axis_size(axis))])]
  transfers between devices with their start and end apart: 18 -> 25, of which waited for: 10 -> 13; matrix products, arithmetic and copies ran while one was open for 0% -> 0% of each run, Pallas kernels for 1% -> 1%
where the time goes in v10:
time: 127 us
  starting transfers between devices  79.8 us (63%)
  waiting for transfers between devices  40.2 us (32%)
  Pallas kernels  6.06 us (5%)
    ppermute x22, starting transfers between devices, swapped(): lax.ppermute(x, axis, [(i, i ^ bit) for i in range(lax.axis_size(axis))])  49.4 us
    all_to_all x3, starting transfers between devices, exchanged(): return lax.all_to_all(x, axes, split_axis=0, concat_axis=0, tiled=True)  30.4 us
    ppermute x22, waiting for transfers between devices, swapped(): lax.ppermute(x, axis, [(i, i ^ bit) for i in range(lax.axis_size(axis))])  24.9 us
    all_to_all x3, waiting for transfers between devices, exchanged(): return lax.all_to_all(x, axes, split_axis=0, concat_axis=0, tiled=True)  15.3 us
    pallas_call x11, Pallas kernels, call(): pl.pallas_call(kernel, out_shape=tuple((jax.ShapeDtypeStruct(s, d) for s,...  6.06 us
  transfers between devices with their start and end apart: 25, of which 13 were waited for; matrix products, arithmetic and copies ran while one was open for 0% of the time, Pallas kernels for 1%

profile of v10, /device:TPU:513, one launch (start us, length us, event | category | flops | bytes accessed | tf_op | source)
XLA Modules:
  0.0 126.9 jit_solution(3217301158512040921)
XLA Ops:
  0.6 1.8 %shard_map.128 = (bf16[16,32,128]{2,1,0:T(8,128)(2,1)}, bf16[16,1024]{1,0:T(8,128)(2,1)S(1)}, bf16[40,1024]{1,0:T(8,128)(2,1)S(1)}) custom-call(bf16[16,2048]{1,0:T(8,128)(2,1)} %refs_0_.1, bf16[16,1024]{1,0:T(8,128)(2,1)} %refs_1_.2, f32[8,1024]{1,0:T(8,128)} %refs_1_.3, bf16[2,16,1024]{2,1,0:T(8,128)(2,1)} %refs_3_.1, bf16[2,8,1024]{2,1,0:T(8,128)(2,1)} %refs_4_.1, ...), custom_call_target="tpu_custom_call" | custom-call | tf_op jit(solution)/shard_map/pallas_call | solution.py:56
  2.5 6.7 %collective-permute-start = (bf16[40,1024]{1,0:T(8,128)(2,1)S(1)}, bf16[40,1024]{1,0:T(8,128)(2,1)S(1)}, u32[]{:S(2)}, u32[]{:S(2)}) collective-permute-start(bf16[40,1024]{1,0:T(8,128)(2,1)S(1)} %get-tuple-element.20.own), channel_id=1, source_target_pairs={{0,8},{2,10},{4,12},{6,14},{8,0},{10,2},{12,4},{14,6},{1,9},{3,11}... | collective-permute-start | bytes 245768 | tf_op jit(solution)/shard_map/ppermute | solution.py:26
  9.1 1.9 %collective-permute-done.other = bf16[40,1024]{1,0:T(8,128)(2,1)S(1)} collective-permute-done((bf16[40,1024]{1,0:T(8,128)(2,1)S(1)}, bf16[40,1024]{1,0:T(8,128)(2,1)S(1)}, u32[]{:S(2)}, u32[]{:S(2)}) %collective-permute-start) | collective-permute-done | bytes 81952 | tf_op jit(solution)/shard_map/ppermute | solution.py:26
  11.1 3.9 %collective-permute-start.1 = (bf16[2,40,1024]{2,1,0:T(8,128)(2,1)S(1)}, bf16[2,40,1024]{2,1,0:T(8,128)(2,1)S(1)}, u32[]{:S(2)}, u32[]{:S(2)}) collective-permute-start(bf16[2,40,1024]{2,1,0:T(8,128)(2,1)S(1)} %shard_map.129.own), channel_id=1, source_target_pairs={{0,4},{2,6},{4,0},{6,2},{8,12},{10,14},{12,8},{14,10},{1,5},{3,7},... | collective-permute-start | bytes 491528 | tf_op jit(solution)/shard_map/ppermute | solution.py:26
  15.0 5.5 %collective-permute-done.1.other = bf16[2,40,1024]{2,1,0:T(8,128)(2,1)S(1)} collective-permute-done((bf16[2,40,1024]{2,1,0:T(8,128)(2,1)S(1)}, bf16[2,40,1024]{2,1,0:T(8,128)(2,1)S(1)}, u32[]{:S(2)}, u32[]{:S(2)}) %collective-permute-start.1) | collective-permute-done | bytes 163872 | tf_op jit(solution)/shard_map/ppermute | solution.py:26
  20.5 0.1 collective-permute-start.2
  20.6 21.4 %all-to-all-start = ((bf16[16,32,128]{2,1,0:T(8,128)(2,1)}), bf16[16,32,128]{2,1,0:T(8,128)(2,1)S(1)}, u32[]{:S(2)}, u32[]{:S(2)}) async-start(bf16[16,32,128]{2,1,0:T(8,128)(2,1)} %get-tuple-element.22), calls=%async_computation | async-start | bytes 262144 | tf_op jit(solution)/shard_map/all_to_all | solution.py:22
  42.1 5.4 %collective-permute-start.4 = (bf16[16,1024]{1,0:T(8,128)(2,1)S(1)}, bf16[16,1024]{1,0:T(8,128)(2,1)S(1)}, u32[]{:S(2)}, u32[]{:S(2)}) collective-permute-start(bf16[16,1024]{1,0:T(8,128)(2,1)S(1)} %get-tuple-element.21.own), channel_id=1, source_target_pairs={{0,8},{2,10},{4,12},{6,14},{8,0},{10,2},{12,4},{14,6},{1,9},{3,11}... | collective-permute-start | bytes 98312 | tf_op jit(solution)/shard_map/ppermute | solution.py:26
  47.5 4.1 %all-to-all-done.cols.refs_0_.refs_5_ = bf16[16,32,128]{2,1,0:T(8,128)(2,1)S(1)} async-done(((bf16[16,32,128]{2,1,0:T(8,128)(2,1)}), bf16[16,32,128]{2,1,0:T(8,128)(2,1)S(1)}, u32[]{:S(2)}, u32[]{:S(2)}) %all-to-all-start) | async-done | bytes 131104 | tf_op jit(solution)/shard_map/all_to_all | solution.py:22
  51.5 0.7 shard_map.131.refs_0_
  52.3 0.0 collective-permute-done.4.other
  52.3 0.5 collective-permute-start.5
  52.8 3.6 %all-to-all-start.1 = ((bf16[8,16,8,128]{3,2,1,0:T(8,128)(2,1)}), bf16[8,16,8,128]{3,2,1,0:T(8,128)(2,1)S(1)}, u32[]{:S(2)}, u32[]{:S(2)}) async-start(bf16[8,16,8,128]{3,2,1,0:T(8,128)(2,1)} %shard_map.131.refs_0_), calls=%async_computation.1 | async-start | bytes 524288 | tf_op jit(solution)/shard_map/all_to_all | solution.py:22
  56.4 1.2 collective-permute-done.5.other
  57.6 0.1 collective-permute-start.6
  57.8 0.0 collective-permute-done.2
  57.8 0.1 pad_maximum_fusion.refs_0_
  57.9 1.9 %collective-permute-start.3 = (bf16[8,40,1024]{2,1,0:T(8,128)(2,1)S(1)}, bf16[8,40,1024]{2,1,0:T(8,128)(2,1)S(1)}, u32[]{:S(2)}, u32[]{:S(2)}) collective-permute-start(bf16[8,40,1024]{2,1,0:T(8,128)(2,1)S(1)} %pad_maximum_fusion.refs_0_), channel_id=1, source_target_pairs={{0,1},{1,0},{2,3},{3,2},{4,5},{5,4},{6,7},{7,6},{8,9},{9,8},{10,11... | collective-permute-start | bytes 1966088 | tf_op jit(solution)/shard_map/ppermute | solution.py:26
  59.7 1.8 %collective-permute-done.6 = bf16[4,16,1024]{2,1,0:T(8,128)(2,1)S(1)} collective-permute-done((bf16[4,16,1024]{2,1,0:T(8,128)(2,1)S(1)}, bf16[4,16,1024]{2,1,0:T(8,128)(2,1)S(1)}, u32[]{:S(2)}, u32[]{:S(2)}) %collective-permute-start.6) | collective-permute-done | bytes 131104 | tf_op jit(solution)/shard_map/ppermute | solution.py:26
  61.6 2.9 %collective-permute-start.7 = (bf16[8,16,1024]{2,1,0:T(8,128)(2,1)S(1)}, bf16[8,16,1024]{2,1,0:T(8,128)(2,1)S(1)}, u32[]{:S(2)}, u32[]{:S(2)}) collective-permute-start(bf16[8,16,1024]{2,1,0:T(8,128)(2,1)S(1)} %pad_maximum_fusion.1.refs_2_), channel_id=1, source_target_pairs={{0,1},{1,0},{2,3},{3,2},{4,5},{5,4},{6,7},{7,6},{8,9},{9,8},{10,11... | collective-permute-start | bytes 786440 | tf_op jit(solution)/shard_map/ppermute | solution.py:26
  64.5 1.2 collective-permute-done.7.refs_3_
  65.6 2.4 %all-to-all-done.1.refs_1_.refs_4_ = bf16[8,16,8,128]{3,2,1,0:T(8,128)(2,1)S(1)} async-done(((bf16[8,16,8,128]{3,2,1,0:T(8,128)(2,1)}), bf16[8,16,8,128]{3,2,1,0:T(8,128)(2,1)S(1)}, u32[]{:S(2)}, u32[]{:S(2)}) %all-to-all-start.1) | async-done | bytes 262176 | tf_op jit(solution)/shard_map/all_to_all | solution.py:22
  68.1 0.3 shard_map.134
  68.3 0.1 collective-permute-start.10
  68.5 1.2 collective-permute-start.11
  69.7 2.0 %collective-permute-start.12 = (bf16[16,24,128]{2,1,0:T(8,128)(2,1)S(1)}, bf16[16,24,128]{2,1,0:T(8,128)(2,1)S(1)}, u32[]{:S(2)}, u32[]{:S(2)}) collective-permute-start(bf16[16,24,128]{2,1,0:T(8,128)(2,1)S(1)} %get-tuple-element.24.refs_7_), channel_id=1, source_target_pairs={{0,80},{16,64},{32,112},{48,96},{64,16},{80,0},{96,48},{112,32},{1... | collective-permute-start | bytes 294920 | tf_op jit(solution)/shard_map/ppermute | solution.py:26
  71.7 3.3 %collective-permute-start.13 = (bf16[16,24,128]{2,1,0:T(8,128)(2,1)S(1)}, bf16[16,24,128]{2,1,0:T(8,128)(2,1)S(1)}, u32[]{:S(2)}, u32[]{:S(2)}) collective-permute-start(bf16[16,24,128]{2,1,0:T(8,128)(2,1)S(1)} %get-tuple-element.24.refs_7_), channel_id=1, source_target_pairs={{0,96},{16,112},{32,64},{48,80},{64,32},{80,48},{96,0},{112,16},{1... | collective-permute-start | bytes 294920 | tf_op jit(solution)/shard_map/ppermute | solution.py:26
  75.0 0.0 collective-permute-done.10.refs_10_
  75.0 1.7 %collective-permute-start.14 = (bf16[16,24,128]{2,1,0:T(8,128)(2,1)S(1)}, bf16[16,24,128]{2,1,0:T(8,128)(2,1)S(1)}, u32[]{:S(2)}, u32[]{:S(2)}) collective-permute-start(bf16[16,24,128]{2,1,0:T(8,128)(2,1)S(1)} %get-tuple-element.24.refs_7_), channel_id=1, source_target_pairs={{0,112},{16,96},{32,80},{48,64},{64,48},{80,32},{96,16},{112,0},{1... | collective-permute-start | bytes 294920 | tf_op jit(solution)/shard_map/ppermute | solution.py:26
  76.7 0.0 collective-permute-done.11.refs_11_
  76.7 0.6 collective-permute-start.8
  77.3 4.7 %collective-permute-done.12.refs_12_ = bf16[16,24,128]{2,1,0:T(8,128)(2,1)S(1)} collective-permute-done((bf16[16,24,128]{2,1,0:T(8,128)(2,1)S(1)}, bf16[16,24,128]{2,1,0:T(8,128)(2,1)S(1)}, u32[]{:S(2)}, u32[]{:S(2)}) %collective-permute-start.12) | collective-permute-done | bytes 98336 | tf_op jit(solution)/shard_map/ppermute | solution.py:26
  82.0 5.7 %collective-permute-start.9 = (bf16[16,24,128]{2,1,0:T(8,128)(2,1)S(1)}, bf16[16,24,128]{2,1,0:T(8,128)(2,1)S(1)}, u32[]{:S(2)}, u32[]{:S(2)}) collective-permute-start(bf16[16,24,128]{2,1,0:T(8,128)(2,1)S(1)} %get-tuple-element.24.refs_7_), channel_id=1, source_target_pairs={{0,32},{16,48},{32,0},{48,16},{64,96},{80,112},{96,64},{112,80},{1... | collective-permute-start | bytes 294920 | tf_op jit(solution)/shard_map/ppermute | solution.py:26
  87.7 0.0 collective-permute-done.13.refs_13_
  87.7 3.2 %collective-permute-done.14.refs_14_ = bf16[16,24,128]{2,1,0:T(8,128)(2,1)S(1)} collective-permute-done((bf16[16,24,128]{2,1,0:T(8,128)(2,1)S(1)}, bf16[16,24,128]{2,1,0:T(8,128)(2,1)S(1)}, u32[]{:S(2)}, u32[]{:S(2)}) %collective-permute-start.14) | collective-permute-done | bytes 98336 | tf_op jit(solution)/shard_map/ppermute | solution.py:26
  91.0 0.0 collective-permute-done.8.refs_8_
  91.0 0.0 collective-permute-done.9.refs_9_
  91.0 0.0 collective-permute-done.3.refs_1_
  91.0 1.0 shard_map.135
  91.9 2.1 %collective-permute-start.15 = (bf16[200,128]{1,0:T(8,128)(2,1)S(1)}, bf16[200,128]{1,0:T(8,128)(2,1)S(1)}, u32[]{:S(2)}, u32[]{:S(2)}) collective-permute-start(bf16[200,128]{1,0:T(8,128)(2,1)S(1)} %get-tuple-element.26), channel_id=1, source_target_pairs={{0,16},{16,0},{32,48},{48,32},{64,80},{80,64},{96,112},{112,96},{1... | collective-permute-start | bytes 153608 | tf_op jit(solution)/shard_map/ppermute | solution.py:26
  94.1 2.9 %collective-permute-start.16 = (bf16[200,128]{1,0:T(8,128)(2,1)S(1)}, bf16[200,128]{1,0:T(8,128)(2,1)S(1)}, u32[]{:S(2)}, u32[]{:S(2)}) collective-permute-start(bf16[200,128]{1,0:T(8,128)(2,1)S(1)} %get-tuple-element.27), channel_id=1, source_target_pairs={{0,32},{16,48},{32,0},{48,16},{64,96},{80,112},{96,64},{112,80},{1... | collective-permute-start | bytes 153608 | tf_op jit(solution)/shard_map/ppermute | solution.py:26
  97.0 0.2 collective-permute-start.17
  97.2 1.1 collective-permute-start.18
  98.2 3.2 %collective-permute-start.19 = (bf16[200,128]{1,0:T(8,128)(2,1)S(1)}, bf16[200,128]{1,0:T(8,128)(2,1)S(1)}, u32[]{:S(2)}, u32[]{:S(2)}) collective-permute-start(bf16[200,128]{1,0:T(8,128)(2,1)S(1)} %get-tuple-element.30), channel_id=1, source_target_pairs={{0,80},{16,64},{32,112},{48,96},{64,16},{80,0},{96,48},{112,32},{1... | collective-permute-start | bytes 153608 | tf_op jit(solution)/shard_map/ppermute | solution.py:26
  101.5 0.0 collective-permute-done.15.refs_1_
  101.5 1.1 collective-permute-start.20
  102.6 0.0 collective-permute-done.16.refs_2_
  102.6 2.6 %collective-permute-start.21 = (bf16[200,128]{1,0:T(8,128)(2,1)S(1)}, bf16[200,128]{1,0:T(8,128)(2,1)S(1)}, u32[]{:S(2)}, u32[]{:S(2)}) collective-permute-start(bf16[200,128]{1,0:T(8,128)(2,1)S(1)} %get-tuple-element.32), channel_id=1, source_target_pairs={{0,112},{16,96},{32,80},{48,64},{64,48},{80,32},{96,16},{112,0},{1... | collective-permute-start | bytes 153608 | tf_op jit(solution)/shard_map/ppermute | solution.py:26
  105.2 0.0 collective-permute-done.17.refs_3_
  105.2 0.0 collective-permute-done.18.refs_4_
  105.2 0.1 collective-permute-done.19.refs_5_
  105.3 1.6 %collective-permute-done.20.refs_6_ = bf16[200,128]{1,0:T(8,128)(2,1)S(1)} collective-permute-done((bf16[200,128]{1,0:T(8,128)(2,1)S(1)}, bf16[200,128]{1,0:T(8,128)(2,1)S(1)}, u32[]{:S(2)}, u32[]{:S(2)}) %collective-permute-start.20) | collective-permute-done | bytes 51232 | tf_op jit(solution)/shard_map/ppermute | solution.py:26
  106.8 3.6 %collective-permute-done.21.refs_7_ = bf16[200,128]{1,0:T(8,128)(2,1)S(1)} collective-permute-done((bf16[200,128]{1,0:T(8,128)(2,1)S(1)}, bf16[200,128]{1,0:T(8,128)(2,1)S(1)}, u32[]{:S(2)}, u32[]{:S(2)}) %collective-permute-start.21) | collective-permute-done | bytes 51232 | tf_op jit(solution)/shard_map/ppermute | solution.py:26
  110.5 0.8 shard_map.136
  111.3 0.0 copy-start
  111.3 5.4 %all-to-all-start.2 = ((bf16[16,40,128]{2,1,0:T(8,128)(2,1)}), bf16[16,40,128]{2,1,0:T(8,128)(2,1)S(1)}, u32[]{:S(2)}, u32[]{:S(2)}) async-start(bf16[16,40,128]{2,1,0:T(8,128)(2,1)} %shard_map.136), calls=%async_computation.2 | async-start | bytes 327680 | tf_op jit(solution)/shard_map/all_to_all | solution.py:22
  116.6 0.7 shard_map.137.refs_2_
  117.3 8.8 %all-to-all-done.2.refs_0_ = bf16[16,40,128]{2,1,0:T(8,128)(2,1)S(1)} async-done(((bf16[16,40,128]{2,1,0:T(8,128)(2,1)}), bf16[16,40,128]{2,1,0:T(8,128)(2,1)S(1)}, u32[]{:S(2)}, u32[]{:S(2)}) %all-to-all-start.2) | async-done | bytes 163872 | tf_op jit(solution)/shard_map/all_to_all | solution.py:22
  126.2 0.0 copy-done
  126.2 0.7 shard_map.138
  (5 shorter events, 0.1 us)
Async XLA Ops:
  2.5 8.6 %collective-permute-start = (bf16[40,1024]{1,0:T(8,128)(2,1)S(1)}, bf16[40,1024]{1,0:T(8,128)(2,1)S(1)}, u32[]{:S(2)}, u32[]{:S(2)}) collective-permute-start(bf16[40,1024]{1,0:T(8,128)(2,1)S(1)} %get-tuple-element.20.own), channel_id=1, source_target_pairs={{0,8},{2,10},{4,12},{6,14},{8,0},{10,2},{12,4},{14,6},{1,9},{3,11}... | collective-permute-start | bytes 245768 | tf_op jit(solution)/shard_map/ppermute | solution.py:26
  11.1 9.4 %collective-permute-start.1 = (bf16[2,40,1024]{2,1,0:T(8,128)(2,1)S(1)}, bf16[2,40,1024]{2,1,0:T(8,128)(2,1)S(1)}, u32[]{:S(2)}, u32[]{:S(2)}) collective-permute-start(bf16[2,40,1024]{2,1,0:T(8,128)(2,1)S(1)} %shard_map.129.own), channel_id=1, source_target_pairs={{0,4},{2,6},{4,0},{6,2},{8,12},{10,14},{12,8},{14,10},{1,5},{3,7},... | collective-permute-start | bytes 491528 | tf_op jit(solution)/shard_map/ppermute | solution.py:26
  20.5 37.3 %collective-permute-start.2 = (bf16[4,40,1024]{2,1,0:T(8,128)(2,1)S(1)}, bf16[4,40,1024]{2,1,0:T(8,128)(2,1)S(1)}, u32[]{:S(2)}, u32[]{:S(2)}) collective-permute-start(bf16[4,40,1024]{2,1,0:T(8,128)(2,1)S(1)} %shard_map.130), channel_id=1, source_target_pairs={{0,2},{2,0},{4,6},{6,4},{8,10},{10,8},{12,14},{14,12},{1,3},{3,1},... | collective-permute-start | bytes 983048 | tf_op jit(solution)/shard_map/ppermute | solution.py:26
  20.6 30.9 %all-to-all-start = ((bf16[16,32,128]{2,1,0:T(8,128)(2,1)}), bf16[16,32,128]{2,1,0:T(8,128)(2,1)S(1)}, u32[]{:S(2)}, u32[]{:S(2)}) async-start(bf16[16,32,128]{2,1,0:T(8,128)(2,1)} %get-tuple-element.22), calls=%async_computation | async-start | bytes 262144 | tf_op jit(solution)/shard_map/all_to_all | solution.py:22
  42.1 10.2 %collective-permute-start.4 = (bf16[16,1024]{1,0:T(8,128)(2,1)S(1)}, bf16[16,1024]{1,0:T(8,128)(2,1)S(1)}, u32[]{:S(2)}, u32[]{:S(2)}) collective-permute-start(bf16[16,1024]{1,0:T(8,128)(2,1)S(1)} %get-tuple-element.21.own), channel_id=1, source_target_pairs={{0,8},{2,10},{4,12},{6,14},{8,0},{10,2},{12,4},{14,6},{1,9},{3,11}... | collective-permute-start | bytes 98312 | tf_op jit(solution)/shard_map/ppermute | solution.py:26
  52.3 5.3 %collective-permute-start.5 = (bf16[2,16,1024]{2,1,0:T(8,128)(2,1)S(1)}, bf16[2,16,1024]{2,1,0:T(8,128)(2,1)S(1)}, u32[]{:S(2)}, u32[]{:S(2)}) collective-permute-start(bf16[2,16,1024]{2,1,0:T(8,128)(2,1)S(1)} %shard_map.132.own), channel_id=1, source_target_pairs={{0,4},{2,6},{4,0},{6,2},{8,12},{10,14},{12,8},{14,10},{1,5},{3,7},... | collective-permute-start | bytes 196616 | tf_op jit(solution)/shard_map/ppermute | solution.py:26
  52.8 15.2 %all-to-all-start.1 = ((bf16[8,16,8,128]{3,2,1,0:T(8,128)(2,1)}), bf16[8,16,8,128]{3,2,1,0:T(8,128)(2,1)S(1)}, u32[]{:S(2)}, u32[]{:S(2)}) async-start(bf16[8,16,8,128]{3,2,1,0:T(8,128)(2,1)} %shard_map.131.refs_0_), calls=%async_computation.1 | async-start | bytes 524288 | tf_op jit(solution)/shard_map/all_to_all | solution.py:22
  57.6 3.9 %collective-permute-start.6 = (bf16[4,16,1024]{2,1,0:T(8,128)(2,1)S(1)}, bf16[4,16,1024]{2,1,0:T(8,128)(2,1)S(1)}, u32[]{:S(2)}, u32[]{:S(2)}) collective-permute-start(bf16[4,16,1024]{2,1,0:T(8,128)(2,1)S(1)} %shard_map.133), channel_id=1, source_target_pairs={{0,2},{2,0},{4,6},{6,4},{8,10},{10,8},{12,14},{14,12},{1,3},{3,1},... | collective-permute-start | bytes 393224 | tf_op jit(solution)/shard_map/ppermute | solution.py:26
  57.9 33.1 %collective-permute-start.3 = (bf16[8,40,1024]{2,1,0:T(8,128)(2,1)S(1)}, bf16[8,40,1024]{2,1,0:T(8,128)(2,1)S(1)}, u32[]{:S(2)}, u32[]{:S(2)}) collective-permute-start(bf16[8,40,1024]{2,1,0:T(8,128)(2,1)S(1)} %pad_maximum_fusion.refs_0_), channel_id=1, source_target_pairs={{0,1},{1,0},{2,3},{3,2},{4,5},{5,4},{6,7},{7,6},{8,9},{9,8},{10,11... | collective-permute-start | bytes 1966088 | tf_op jit(solution)/shard_map/ppermute | solution.py:26
  61.6 4.0 %collective-permute-start.7 = (bf16[8,16,1024]{2,1,0:T(8,128)(2,1)S(1)}, bf16[8,16,1024]{2,1,0:T(8,128)(2,1)S(1)}, u32[]{:S(2)}, u32[]{:S(2)}) collective-permute-start(bf16[8,16,1024]{2,1,0:T(8,128)(2,1)S(1)} %pad_maximum_fusion.1.refs_2_), channel_id=1, source_target_pairs={{0,1},{1,0},{2,3},{3,2},{4,5},{5,4},{6,7},{7,6},{8,9},{9,8},{10,11... | collective-permute-start | bytes 786440 | tf_op jit(solution)/shard_map/ppermute | solution.py:26
  68.3 6.7 %collective-permute-start.10 = (bf16[16,24,128]{2,1,0:T(8,128)(2,1)S(1)}, bf16[16,24,128]{2,1,0:T(8,128)(2,1)S(1)}, u32[]{:S(2)}, u32[]{:S(2)}) collective-permute-start(bf16[16,24,128]{2,1,0:T(8,128)(2,1)S(1)} %get-tuple-element.24.refs_7_), channel_id=1, source_target_pairs={{0,48},{16,32},{32,16},{48,0},{64,112},{80,96},{96,80},{112,64},{1... | collective-permute-start | bytes 294920 | tf_op jit(solution)/shard_map/ppermute | solution.py:26
  68.5 8.2 %collective-permute-start.11 = (bf16[16,24,128]{2,1,0:T(8,128)(2,1)S(1)}, bf16[16,24,128]{2,1,0:T(8,128)(2,1)S(1)}, u32[]{:S(2)}, u32[]{:S(2)}) collective-permute-start(bf16[16,24,128]{2,1,0:T(8,128)(2,1)S(1)} %get-tuple-element.24.refs_7_), channel_id=1, source_target_pairs={{0,64},{16,80},{32,96},{48,112},{64,0},{80,16},{96,32},{112,48},{1... | collective-permute-start | bytes 294920 | tf_op jit(solution)/shard_map/ppermute | solution.py:26
  69.7 12.3 %collective-permute-start.12 = (bf16[16,24,128]{2,1,0:T(8,128)(2,1)S(1)}, bf16[16,24,128]{2,1,0:T(8,128)(2,1)S(1)}, u32[]{:S(2)}, u32[]{:S(2)}) collective-permute-start(bf16[16,24,128]{2,1,0:T(8,128)(2,1)S(1)} %get-tuple-element.24.refs_7_), channel_id=1, source_target_pairs={{0,80},{16,64},{32,112},{48,96},{64,16},{80,0},{96,48},{112,32},{1... | collective-permute-start | bytes 294920 | tf_op jit(solution)/shard_map/ppermute | solution.py:26
  71.7 16.0 %collective-permute-start.13 = (bf16[16,24,128]{2,1,0:T(8,128)(2,1)S(1)}, bf16[16,24,128]{2,1,0:T(8,128)(2,1)S(1)}, u32[]{:S(2)}, u32[]{:S(2)}) collective-permute-start(bf16[16,24,128]{2,1,0:T(8,128)(2,1)S(1)} %get-tuple-element.24.refs_7_), channel_id=1, source_target_pairs={{0,96},{16,112},{32,64},{48,80},{64,32},{80,48},{96,0},{112,16},{1... | collective-permute-start | bytes 294920 | tf_op jit(solution)/shard_map/ppermute | solution.py:26
  75.0 15.9 %collective-permute-start.14 = (bf16[16,24,128]{2,1,0:T(8,128)(2,1)S(1)}, bf16[16,24,128]{2,1,0:T(8,128)(2,1)S(1)}, u32[]{:S(2)}, u32[]{:S(2)}) collective-permute-start(bf16[16,24,128]{2,1,0:T(8,128)(2,1)S(1)} %get-tuple-element.24.refs_7_), channel_id=1, source_target_pairs={{0,112},{16,96},{32,80},{48,64},{64,48},{80,32},{96,16},{112,0},{1... | collective-permute-start | bytes 294920 | tf_op jit(solution)/shard_map/ppermute | solution.py:26
  76.7 14.3 %collective-permute-start.8 = (bf16[16,24,128]{2,1,0:T(8,128)(2,1)S(1)}, bf16[16,24,128]{2,1,0:T(8,128)(2,1)S(1)}, u32[]{:S(2)}, u32[]{:S(2)}) collective-permute-start(bf16[16,24,128]{2,1,0:T(8,128)(2,1)S(1)} %get-tuple-element.24.refs_7_), channel_id=1, source_target_pairs={{0,16},{16,0},{32,48},{48,32},{64,80},{80,64},{96,112},{112,96},{1... | collective-permute-start | bytes 294920 | tf_op jit(solution)/shard_map/ppermute | solution.py:26
  82.0 8.9 %collective-permute-start.9 = (bf16[16,24,128]{2,1,0:T(8,128)(2,1)S(1)}, bf16[16,24,128]{2,1,0:T(8,128)(2,1)S(1)}, u32[]{:S(2)}, u32[]{:S(2)}) collective-permute-start(bf16[16,24,128]{2,1,0:T(8,128)(2,1)S(1)} %get-tuple-element.24.refs_7_), channel_id=1, source_target_pairs={{0,32},{16,48},{32,0},{48,16},{64,96},{80,112},{96,64},{112,80},{1... | collective-permute-start | bytes 294920 | tf_op jit(solution)/shard_map/ppermute | solution.py:26
  91.9 9.5 %collective-permute-start.15 = (bf16[200,128]{1,0:T(8,128)(2,1)S(1)}, bf16[200,128]{1,0:T(8,128)(2,1)S(1)}, u32[]{:S(2)}, u32[]{:S(2)}) collective-permute-start(bf16[200,128]{1,0:T(8,128)(2,1)S(1)} %get-tuple-element.26), channel_id=1, source_target_pairs={{0,16},{16,0},{32,48},{48,32},{64,80},{80,64},{96,112},{112,96},{1... | collective-permute-start | bytes 153608 | tf_op jit(solution)/shard_map/ppermute | solution.py:26
  94.1 8.6 %collective-permute-start.16 = (bf16[200,128]{1,0:T(8,128)(2,1)S(1)}, bf16[200,128]{1,0:T(8,128)(2,1)S(1)}, u32[]{:S(2)}, u32[]{:S(2)}) collective-permute-start(bf16[200,128]{1,0:T(8,128)(2,1)S(1)} %get-tuple-element.27), channel_id=1, source_target_pairs={{0,32},{16,48},{32,0},{48,16},{64,96},{80,112},{96,64},{112,80},{1... | collective-permute-start | bytes 153608 | tf_op jit(solution)/shard_map/ppermute | solution.py:26
  97.0 8.3 %collective-permute-start.17 = (bf16[200,128]{1,0:T(8,128)(2,1)S(1)}, bf16[200,128]{1,0:T(8,128)(2,1)S(1)}, u32[]{:S(2)}, u32[]{:S(2)}) collective-permute-start(bf16[200,128]{1,0:T(8,128)(2,1)S(1)} %get-tuple-element.28), channel_id=1, source_target_pairs={{0,48},{16,32},{32,16},{48,0},{64,112},{80,96},{96,80},{112,64},{1... | collective-permute-start | bytes 153608 | tf_op jit(solution)/shard_map/ppermute | solution.py:26
  97.2 8.1 %collective-permute-start.18 = (bf16[200,128]{1,0:T(8,128)(2,1)S(1)}, bf16[200,128]{1,0:T(8,128)(2,1)S(1)}, u32[]{:S(2)}, u32[]{:S(2)}) collective-permute-start(bf16[200,128]{1,0:T(8,128)(2,1)S(1)} %get-tuple-element.29), channel_id=1, source_target_pairs={{0,64},{16,80},{32,96},{48,112},{64,0},{80,16},{96,32},{112,48},{1... | collective-permute-start | bytes 153608 | tf_op jit(solution)/shard_map/ppermute | solution.py:26
  98.2 7.0 %collective-permute-start.19 = (bf16[200,128]{1,0:T(8,128)(2,1)S(1)}, bf16[200,128]{1,0:T(8,128)(2,1)S(1)}, u32[]{:S(2)}, u32[]{:S(2)}) collective-permute-start(bf16[200,128]{1,0:T(8,128)(2,1)S(1)} %get-tuple-element.30), channel_id=1, source_target_pairs={{0,80},{16,64},{32,112},{48,96},{64,16},{80,0},{96,48},{112,32},{1... | collective-permute-start | bytes 153608 | tf_op jit(solution)/shard_map/ppermute | solution.py:26
  101.5 5.4 %collective-permute-start.20 = (bf16[200,128]{1,0:T(8,128)(2,1)S(1)}, bf16[200,128]{1,0:T(8,128)(2,1)S(1)}, u32[]{:S(2)}, u32[]{:S(2)}) collective-permute-start(bf16[200,128]{1,0:T(8,128)(2,1)S(1)} %get-tuple-element.31), channel_id=1, source_target_pairs={{0,96},{16,112},{32,64},{48,80},{64,32},{80,48},{96,0},{112,16},{1... | collective-permute-start | bytes 153608 | tf_op jit(solution)/shard_map/ppermute | solution.py:26
  102.6 7.9 %collective-permute-start.21 = (bf16[200,128]{1,0:T(8,128)(2,1)S(1)}, bf16[200,128]{1,0:T(8,128)(2,1)S(1)}, u32[]{:S(2)}, u32[]{:S(2)}) collective-permute-start(bf16[200,128]{1,0:T(8,128)(2,1)S(1)} %get-tuple-element.32), channel_id=1, source_target_pairs={{0,112},{16,96},{32,80},{48,64},{64,48},{80,32},{96,16},{112,0},{1... | collective-permute-start | bytes 153608 | tf_op jit(solution)/shard_map/ppermute | solution.py:26
  111.3 14.9 %copy-start = (f32[8,1024]{1,0:T(8,128)S(1)}, f32[8,1024]{1,0:T(8,128)}, u32[]{:S(2)}) copy-start(f32[8,1024]{1,0:T(8,128)} %refs_1_.3) | copy-start | bytes 98308
  111.3 14.9 %all-to-all-start.2 = ((bf16[16,40,128]{2,1,0:T(8,128)(2,1)}), bf16[16,40,128]{2,1,0:T(8,128)(2,1)S(1)}, u32[]{:S(2)}, u32[]{:S(2)}) async-start(bf16[16,40,128]{2,1,0:T(8,128)(2,1)} %shard_map.136), calls=%async_computation.2 | async-start | bytes 327680 | tf_op jit(solution)/shard_map/all_to_all | solution.py:22

commit v11 on v10

--- a/solution.py
+++ b/solution.py
@@ -114,9 +114,8 @@
     rows[2 * rt : 2 * rt + rp, :] = dinv[...].astype(BF16)
 
 
-def copy_kernel(source_hbm, result, scratch, done):
-    fetched((source_hbm,), (scratch,), done)
-    result[...] = scratch[...]
+def copy_kernel(source, result):
+    result[...] = source[...]
 
 
 def stack_kernel(own, other, *refs):
@@ -303,7 +302,7 @@
     cols = exchanged(slots, XC)
     par_far = swapped(par_rows, "x", 4)
     far_rows = swapped(rows, "x", 4)
-    (dvar_kid,) = fetching(copy_kernel, [(dvar_kid.shape, F32)], (dvar_kid,))
+    (rows,) = call(copy_kernel, [(rows.shape, BF16)], (rows,))
     (tall_send,) = call(repeat_kernel, [((ny, nj, rp, LANES), BF16)], (cols,))
     (par_rows,) = call(
         stack_kernel,

time: 127 us -> 129 us (1.016)
  blocking collectives: 0 us -> 16.4 us
  waiting for transfers between devices: 40.2 us -> 32.4 us
  starting transfers between devices: 79.8 us -> 74.3 us
  Pallas kernels: 6.06 us -> 4.71 us
    all_to_all x0 -> x1, blocking collectives: none -> 16.4 us  [exchanged(): return lax.all_to_all(x, axes, split_axis=0, concat_axis=0, tiled=True)]
    all_to_all x3 -> x2, waiting for transfers between devices: 15.3 us -> 7.64 us  [exchanged(): return lax.all_to_all(x, axes, split_axis=0, concat_axis=0, tiled=True)]
    all_to_all x3 -> x2, starting transfers between devices: 30.4 us -> 25 us  [exchanged(): return lax.all_to_all(x, axes, split_axis=0, concat_axis=0, tiled=True)]
    pallas_call x11, Pallas kernels: 6.06 us -> 4.71 us  [call(): pl.pallas_call(kernel, out_shape=tuple((jax.ShapeDtypeStruct(s, d) for s,...]
  transfers between devices with their start and end apart: 25 -> 24, of which waited for: 13 -> 11; matrix products, arithmetic and copies ran while one was open for 0% -> 0% of each run, Pallas kernels for 1% -> 1%
where the time goes in v11:
time: 129 us
  starting transfers between devices  74.3 us (58%)
  waiting for transfers between devices  32.4 us (25%)
  blocking collectives  16.4 us (13%)
  Pallas kernels  4.71 us (4%)
    ppermute x22, starting transfers between devices, swapped(): lax.ppermute(x, axis, [(i, i ^ bit) for i in range(lax.axis_size(axis))])  49.3 us
    all_to_all x2, starting transfers between devices, exchanged(): return lax.all_to_all(x, axes, split_axis=0, concat_axis=0, tiled=True)  25 us
    ppermute x22, waiting for transfers between devices, swapped(): lax.ppermute(x, axis, [(i, i ^ bit) for i in range(lax.axis_size(axis))])  24.7 us
    all_to_all x1, blocking collectives, exchanged(): return lax.all_to_all(x, axes, split_axis=0, concat_axis=0, tiled=True)  16.4 us
    all_to_all x2, waiting for transfers between devices, exchanged(): return lax.all_to_all(x, axes, split_axis=0, concat_axis=0, tiled=True)  7.64 us
    pallas_call x11, Pallas kernels, call(): pl.pallas_call(kernel, out_shape=tuple((jax.ShapeDtypeStruct(s, d) for s,...  4.71 us
  transfers between devices with their start and end apart: 24, of which 11 were waited for; matrix products, arithmetic and copies ran while one was open for 0% of the time, Pallas kernels for 1%

profile of v11, /device:TPU:513, one launch (start us, length us, event | category | flops | bytes accessed | tf_op | source)
XLA Modules:
  0.0 128.6 jit_solution(3396418793211184913)
XLA Ops:
  0.6 1.8 %shard_map.128 = (bf16[16,32,128]{2,1,0:T(8,128)(2,1)}, bf16[16,1024]{1,0:T(8,128)(2,1)S(1)}, bf16[40,1024]{1,0:T(8,128)(2,1)S(1)}) custom-call(bf16[16,2048]{1,0:T(8,128)(2,1)} %refs_0_.1, bf16[16,1024]{1,0:T(8,128)(2,1)} %refs_1_.2, f32[8,1024]{1,0:T(8,128)} %refs_1_.3, bf16[2,16,1024]{2,1,0:T(8,128)(2,1)} %refs_3_.1, bf16[2,8,1024]{2,1,0:T(8,128)(2,1)} %refs_4_.1, ...), custom_call_target="tpu_custom_call" | custom-call | tf_op jit(solution)/shard_map/pallas_call | solution.py:56
  2.5 6.7 %collective-permute-start = (bf16[40,1024]{1,0:T(8,128)(2,1)S(1)}, bf16[40,1024]{1,0:T(8,128)(2,1)S(1)}, u32[]{:S(2)}, u32[]{:S(2)}) collective-permute-start(bf16[40,1024]{1,0:T(8,128)(2,1)S(1)} %get-tuple-element.20.source), channel_id=1, source_target_pairs={{0,8},{2,10},{4,12},{6,14},{8,0},{10,2},{12,4},{14,6},{1,9},{3,11}... | collective-permute-start | bytes 245768 | tf_op jit(solution)/shard_map/ppermute | solution.py:26
  9.1 1.9 %collective-permute-done.other = bf16[40,1024]{1,0:T(8,128)(2,1)S(1)} collective-permute-done((bf16[40,1024]{1,0:T(8,128)(2,1)S(1)}, bf16[40,1024]{1,0:T(8,128)(2,1)S(1)}, u32[]{:S(2)}, u32[]{:S(2)}) %collective-permute-start) | collective-permute-done | bytes 81952 | tf_op jit(solution)/shard_map/ppermute | solution.py:26
  11.1 3.9 %collective-permute-start.1 = (bf16[2,40,1024]{2,1,0:T(8,128)(2,1)S(1)}, bf16[2,40,1024]{2,1,0:T(8,128)(2,1)S(1)}, u32[]{:S(2)}, u32[]{:S(2)}) collective-permute-start(bf16[2,40,1024]{2,1,0:T(8,128)(2,1)S(1)} %shard_map.130.own), channel_id=1, source_target_pairs={{0,4},{2,6},{4,0},{6,2},{8,12},{10,14},{12,8},{14,10},{1,5},{3,7},... | collective-permute-start | bytes 491528 | tf_op jit(solution)/shard_map/ppermute | solution.py:26
  15.0 5.5 %collective-permute-done.1.other = bf16[2,40,1024]{2,1,0:T(8,128)(2,1)S(1)} collective-permute-done((bf16[2,40,1024]{2,1,0:T(8,128)(2,1)S(1)}, bf16[2,40,1024]{2,1,0:T(8,128)(2,1)S(1)}, u32[]{:S(2)}, u32[]{:S(2)}) %collective-permute-start.1) | collective-permute-done | bytes 163872 | tf_op jit(solution)/shard_map/ppermute | solution.py:26
  20.5 0.1 collective-permute-start.2
  20.6 21.4 %all-to-all-start = ((bf16[16,32,128]{2,1,0:T(8,128)(2,1)}), bf16[16,32,128]{2,1,0:T(8,128)(2,1)S(1)}, u32[]{:S(2)}, u32[]{:S(2)}) async-start(bf16[16,32,128]{2,1,0:T(8,128)(2,1)} %get-tuple-element.22), calls=%async_computation | async-start | bytes 262144 | tf_op jit(solution)/shard_map/all_to_all | solution.py:22
  42.1 5.4 %collective-permute-start.4 = (bf16[16,1024]{1,0:T(8,128)(2,1)S(1)}, bf16[16,1024]{1,0:T(8,128)(2,1)S(1)}, u32[]{:S(2)}, u32[]{:S(2)}) collective-permute-start(bf16[16,1024]{1,0:T(8,128)(2,1)S(1)} %get-tuple-element.21.own), channel_id=1, source_target_pairs={{0,8},{2,10},{4,12},{6,14},{8,0},{10,2},{12,4},{14,6},{1,9},{3,11}... | collective-permute-start | bytes 98312 | tf_op jit(solution)/shard_map/ppermute | solution.py:26
  47.5 4.1 %all-to-all-done.cols.refs_0_.refs_5_ = bf16[16,32,128]{2,1,0:T(8,128)(2,1)S(1)} async-done(((bf16[16,32,128]{2,1,0:T(8,128)(2,1)}), bf16[16,32,128]{2,1,0:T(8,128)(2,1)S(1)}, u32[]{:S(2)}, u32[]{:S(2)}) %all-to-all-start) | async-done | bytes 131104 | tf_op jit(solution)/shard_map/all_to_all | solution.py:22
  51.5 0.7 shard_map.132.refs_0_
  52.3 0.0 collective-permute-done.4.other
  52.3 0.5 collective-permute-start.5
  52.8 3.6 %all-to-all-start.1 = ((bf16[8,16,8,128]{3,2,1,0:T(8,128)(2,1)}), bf16[8,16,8,128]{3,2,1,0:T(8,128)(2,1)S(1)}, u32[]{:S(2)}, u32[]{:S(2)}) async-start(bf16[8,16,8,128]{3,2,1,0:T(8,128)(2,1)} %shard_map.132.refs_0_), calls=%async_computation.1 | async-start | bytes 524288 | tf_op jit(solution)/shard_map/all_to_all | solution.py:22
  56.4 1.2 collective-permute-done.5.other
  57.6 0.1 collective-permute-start.6
  57.8 0.0 collective-permute-done.2
  57.8 0.1 pad_maximum_fusion.refs_0_
  57.9 1.9 %collective-permute-start.3 = (bf16[8,40,1024]{2,1,0:T(8,128)(2,1)S(1)}, bf16[8,40,1024]{2,1,0:T(8,128)(2,1)S(1)}, u32[]{:S(2)}, u32[]{:S(2)}) collective-permute-start(bf16[8,40,1024]{2,1,0:T(8,128)(2,1)S(1)} %pad_maximum_fusion.refs_0_), channel_id=1, source_target_pairs={{0,1},{1,0},{2,3},{3,2},{4,5},{5,4},{6,7},{7,6},{8,9},{9,8},{10,11... | collective-permute-start | bytes 1966088 | tf_op jit(solution)/shard_map/ppermute | solution.py:26
  59.7 1.9 %collective-permute-done.6 = bf16[4,16,1024]{2,1,0:T(8,128)(2,1)S(1)} collective-permute-done((bf16[4,16,1024]{2,1,0:T(8,128)(2,1)S(1)}, bf16[4,16,1024]{2,1,0:T(8,128)(2,1)S(1)}, u32[]{:S(2)}, u32[]{:S(2)}) %collective-permute-start.6) | collective-permute-done | bytes 131104 | tf_op jit(solution)/shard_map/ppermute | solution.py:26
  61.6 2.9 %collective-permute-start.7 = (bf16[8,16,1024]{2,1,0:T(8,128)(2,1)S(1)}, bf16[8,16,1024]{2,1,0:T(8,128)(2,1)S(1)}, u32[]{:S(2)}, u32[]{:S(2)}) collective-permute-start(bf16[8,16,1024]{2,1,0:T(8,128)(2,1)S(1)} %pad_maximum_fusion.1.refs_2_), channel_id=1, source_target_pairs={{0,1},{1,0},{2,3},{3,2},{4,5},{5,4},{6,7},{7,6},{8,9},{9,8},{10,11... | collective-permute-start | bytes 786440 | tf_op jit(solution)/shard_map/ppermute | solution.py:26
  64.5 3.6 %all-to-all-done.1.refs_1_.refs_4_ = bf16[8,16,8,128]{3,2,1,0:T(8,128)(2,1)S(1)} async-done(((bf16[8,16,8,128]{3,2,1,0:T(8,128)(2,1)}), bf16[8,16,8,128]{3,2,1,0:T(8,128)(2,1)S(1)}, u32[]{:S(2)}, u32[]{:S(2)}) %all-to-all-start.1) | async-done | bytes 262176 | tf_op jit(solution)/shard_map/all_to_all | solution.py:22
  68.1 0.0 collective-permute-done.7.refs_3_
  68.1 0.3 shard_map.135
  68.4 0.1 collective-permute-start.14
  68.5 1.7 %collective-permute-start.13 = (bf16[16,24,128]{2,1,0:T(8,128)(2,1)S(1)}, bf16[16,24,128]{2,1,0:T(8,128)(2,1)S(1)}, u32[]{:S(2)}, u32[]{:S(2)}) collective-permute-start(bf16[16,24,128]{2,1,0:T(8,128)(2,1)S(1)} %get-tuple-element.24.refs_7_), channel_id=1, source_target_pairs={{0,96},{16,112},{32,64},{48,80},{64,32},{80,48},{96,0},{112,16},{1... | collective-permute-start | bytes 294920 | tf_op jit(solution)/shard_map/ppermute | solution.py:26
  70.2 1.9 %collective-permute-start.12 = (bf16[16,24,128]{2,1,0:T(8,128)(2,1)S(1)}, bf16[16,24,128]{2,1,0:T(8,128)(2,1)S(1)}, u32[]{:S(2)}, u32[]{:S(2)}) collective-permute-start(bf16[16,24,128]{2,1,0:T(8,128)(2,1)S(1)} %get-tuple-element.24.refs_7_), channel_id=1, source_target_pairs={{0,80},{16,64},{32,112},{48,96},{64,16},{80,0},{96,48},{112,32},{1... | collective-permute-start | bytes 294920 | tf_op jit(solution)/shard_map/ppermute | solution.py:26
  72.0 4.5 %collective-permute-start.11 = (bf16[16,24,128]{2,1,0:T(8,128)(2,1)S(1)}, bf16[16,24,128]{2,1,0:T(8,128)(2,1)S(1)}, u32[]{:S(2)}, u32[]{:S(2)}) collective-permute-start(bf16[16,24,128]{2,1,0:T(8,128)(2,1)S(1)} %get-tuple-element.24.refs_7_), channel_id=1, source_target_pairs={{0,64},{16,80},{32,96},{48,112},{64,0},{80,16},{96,32},{112,48},{1... | collective-permute-start | bytes 294920 | tf_op jit(solution)/shard_map/ppermute | solution.py:26
  76.5 0.0 collective-permute-done.14.refs_14_
  76.5 0.0 collective-permute-start.10
  76.5 4.8 %collective-permute-done.13.refs_13_ = bf16[16,24,128]{2,1,0:T(8,128)(2,1)S(1)} collective-permute-done((bf16[16,24,128]{2,1,0:T(8,128)(2,1)S(1)}, bf16[16,24,128]{2,1,0:T(8,128)(2,1)S(1)}, u32[]{:S(2)}, u32[]{:S(2)}) %collective-permute-start.13) | collective-permute-done | bytes 98336 | tf_op jit(solution)/shard_map/ppermute | solution.py:26
  81.3 4.7 %collective-permute-start.9 = (bf16[16,24,128]{2,1,0:T(8,128)(2,1)S(1)}, bf16[16,24,128]{2,1,0:T(8,128)(2,1)S(1)}, u32[]{:S(2)}, u32[]{:S(2)}) collective-permute-start(bf16[16,24,128]{2,1,0:T(8,128)(2,1)S(1)} %get-tuple-element.24.refs_7_), channel_id=1, source_target_pairs={{0,32},{16,48},{32,0},{48,16},{64,96},{80,112},{96,64},{112,80},{1... | collective-permute-start | bytes 294920 | tf_op jit(solution)/shard_map/ppermute | solution.py:26
  86.0 0.0 collective-permute-done.12.refs_12_
  86.0 2.1 %collective-permute-start.8 = (bf16[16,24,128]{2,1,0:T(8,128)(2,1)S(1)}, bf16[16,24,128]{2,1,0:T(8,128)(2,1)S(1)}, u32[]{:S(2)}, u32[]{:S(2)}) collective-permute-start(bf16[16,24,128]{2,1,0:T(8,128)(2,1)S(1)} %get-tuple-element.24.refs_7_), channel_id=1, source_target_pairs={{0,16},{16,0},{32,48},{48,32},{64,80},{80,64},{96,112},{112,96},{1... | collective-permute-start | bytes 294920 | tf_op jit(solution)/shard_map/ppermute | solution.py:26
  88.1 0.0 collective-permute-done.11.refs_11_
  88.2 0.0 collective-permute-done.10.refs_10_
  88.2 3.7 %collective-permute-done.9.refs_9_ = bf16[16,24,128]{2,1,0:T(8,128)(2,1)S(1)} collective-permute-done((bf16[16,24,128]{2,1,0:T(8,128)(2,1)S(1)}, bf16[16,24,128]{2,1,0:T(8,128)(2,1)S(1)}, u32[]{:S(2)}, u32[]{:S(2)}) %collective-permute-start.9) | collective-permute-done | bytes 98336 | tf_op jit(solution)/shard_map/ppermute | solution.py:26
  91.9 0.0 collective-permute-done.8.refs_8_
  91.9 0.0 collective-permute-done.3.refs_1_
  91.9 1.0 shard_map.136
  92.8 1.9 %collective-permute-start.15 = (bf16[200,128]{1,0:T(8,128)(2,1)S(1)}, bf16[200,128]{1,0:T(8,128)(2,1)S(1)}, u32[]{:S(2)}, u32[]{:S(2)}) collective-permute-start(bf16[200,128]{1,0:T(8,128)(2,1)S(1)} %get-tuple-element.26), channel_id=1, source_target_pairs={{0,16},{16,0},{32,48},{48,32},{64,80},{80,64},{96,112},{112,96},{1... | collective-permute-start | bytes 153608 | tf_op jit(solution)/shard_map/ppermute | solution.py:26
  94.8 2.6 %collective-permute-start.16 = (bf16[200,128]{1,0:T(8,128)(2,1)S(1)}, bf16[200,128]{1,0:T(8,128)(2,1)S(1)}, u32[]{:S(2)}, u32[]{:S(2)}) collective-permute-start(bf16[200,128]{1,0:T(8,128)(2,1)S(1)} %get-tuple-element.27), channel_id=1, source_target_pairs={{0,32},{16,48},{32,0},{48,16},{64,96},{80,112},{96,64},{112,80},{1... | collective-permute-start | bytes 153608 | tf_op jit(solution)/shard_map/ppermute | solution.py:26
  97.4 0.2 collective-permute-start.17
  97.6 2.1 %collective-permute-start.18 = (bf16[200,128]{1,0:T(8,128)(2,1)S(1)}, bf16[200,128]{1,0:T(8,128)(2,1)S(1)}, u32[]{:S(2)}, u32[]{:S(2)}) collective-permute-start(bf16[200,128]{1,0:T(8,128)(2,1)S(1)} %get-tuple-element.29), channel_id=1, source_target_pairs={{0,64},{16,80},{32,96},{48,112},{64,0},{80,16},{96,32},{112,48},{1... | collective-permute-start | bytes 153608 | tf_op jit(solution)/shard_map/ppermute | solution.py:26
  99.7 2.2 %collective-permute-start.19 = (bf16[200,128]{1,0:T(8,128)(2,1)S(1)}, bf16[200,128]{1,0:T(8,128)(2,1)S(1)}, u32[]{:S(2)}, u32[]{:S(2)}) collective-permute-start(bf16[200,128]{1,0:T(8,128)(2,1)S(1)} %get-tuple-element.30), channel_id=1, source_target_pairs={{0,80},{16,64},{32,112},{48,96},{64,16},{80,0},{96,48},{112,32},{1... | collective-permute-start | bytes 153608 | tf_op jit(solution)/shard_map/ppermute | solution.py:26
  101.9 0.0 collective-permute-done.15.refs_1_
  101.9 2.7 %collective-permute-start.20 = (bf16[200,128]{1,0:T(8,128)(2,1)S(1)}, bf16[200,128]{1,0:T(8,128)(2,1)S(1)}, u32[]{:S(2)}, u32[]{:S(2)}) collective-permute-start(bf16[200,128]{1,0:T(8,128)(2,1)S(1)} %get-tuple-element.31), channel_id=1, source_target_pairs={{0,96},{16,112},{32,64},{48,80},{64,32},{80,48},{96,0},{112,16},{1... | collective-permute-start | bytes 153608 | tf_op jit(solution)/shard_map/ppermute | solution.py:26
  104.6 0.0 collective-permute-done.16.refs_2_
  104.6 1.0 collective-permute-start.21
  105.6 0.0 collective-permute-done.17.refs_3_
  105.6 0.0 collective-permute-done.18.refs_4_
  105.6 0.5 collective-permute-done.19.refs_5_
  106.1 3.0 %collective-permute-done.20.refs_6_ = bf16[200,128]{1,0:T(8,128)(2,1)S(1)} collective-permute-done((bf16[200,128]{1,0:T(8,128)(2,1)S(1)}, bf16[200,128]{1,0:T(8,128)(2,1)S(1)}, u32[]{:S(2)}, u32[]{:S(2)}) %collective-permute-start.20) | collective-permute-done | bytes 51232 | tf_op jit(solution)/shard_map/ppermute | solution.py:26
  109.0 2.3 %collective-permute-done.21.refs_7_ = bf16[200,128]{1,0:T(8,128)(2,1)S(1)} collective-permute-done((bf16[200,128]{1,0:T(8,128)(2,1)S(1)}, bf16[200,128]{1,0:T(8,128)(2,1)S(1)}, u32[]{:S(2)}, u32[]{:S(2)}) %collective-permute-start.21) | collective-permute-done | bytes 51232 | tf_op jit(solution)/shard_map/ppermute | solution.py:26
  111.4 0.1 shard_map.137
  111.5 0.0 copy-start
  111.5 0.0 copy-start.1
  111.5 16.4 %all_to_all.15.refs_0_ = bf16[16,40,128]{2,1,0:T(8,128)(2,1)S(1)} all-to-all(bf16[16,40,128]{2,1,0:T(8,128)(2,1)S(1)} %shard_map.137), channel_id=1, replica_groups=mesh['parts'=2,'y'=8,'x'=8,'c'=2] {'x','c'}, dimensions={0} | all-to-all | bytes 327680 | tf_op jit(solution)/shard_map/all_to_all | solution.py:22
  127.9 0.0 copy-done
  127.9 0.0 copy-done.1
  127.9 0.7 shard_map.138
  (6 shorter events, 0.1 us)
Async XLA Ops:
  2.5 8.6 %collective-permute-start = (bf16[40,1024]{1,0:T(8,128)(2,1)S(1)}, bf16[40,1024]{1,0:T(8,128)(2,1)S(1)}, u32[]{:S(2)}, u32[]{:S(2)}) collective-permute-start(bf16[40,1024]{1,0:T(8,128)(2,1)S(1)} %get-tuple-element.20.source), channel_id=1, source_target_pairs={{0,8},{2,10},{4,12},{6,14},{8,0},{10,2},{12,4},{14,6},{1,9},{3,11}... | collective-permute-start | bytes 245768 | tf_op jit(solution)/shard_map/ppermute | solution.py:26
  11.1 9.4 %collective-permute-start.1 = (bf16[2,40,1024]{2,1,0:T(8,128)(2,1)S(1)}, bf16[2,40,1024]{2,1,0:T(8,128)(2,1)S(1)}, u32[]{:S(2)}, u32[]{:S(2)}) collective-permute-start(bf16[2,40,1024]{2,1,0:T(8,128)(2,1)S(1)} %shard_map.130.own), channel_id=1, source_target_pairs={{0,4},{2,6},{4,0},{6,2},{8,12},{10,14},{12,8},{14,10},{1,5},{3,7},... | collective-permute-start | bytes 491528 | tf_op jit(solution)/shard_map/ppermute | solution.py:26
  20.5 37.3 %collective-permute-start.2 = (bf16[4,40,1024]{2,1,0:T(8,128)(2,1)S(1)}, bf16[4,40,1024]{2,1,0:T(8,128)(2,1)S(1)}, u32[]{:S(2)}, u32[]{:S(2)}) collective-permute-start(bf16[4,40,1024]{2,1,0:T(8,128)(2,1)S(1)} %shard_map.131), channel_id=1, source_target_pairs={{0,2},{2,0},{4,6},{6,4},{8,10},{10,8},{12,14},{14,12},{1,3},{3,1},... | collective-permute-start | bytes 983048 | tf_op jit(solution)/shard_map/ppermute | solution.py:26
  20.6 30.9 %all-to-all-start = ((bf16[16,32,128]{2,1,0:T(8,128)(2,1)}), bf16[16,32,128]{2,1,0:T(8,128)(2,1)S(1)}, u32[]{:S(2)}, u32[]{:S(2)}) async-start(bf16[16,32,128]{2,1,0:T(8,128)(2,1)} %get-tuple-element.22), calls=%async_computation | async-start | bytes 262144 | tf_op jit(solution)/shard_map/all_to_all | solution.py:22
  42.1 10.2 %collective-permute-start.4 = (bf16[16,1024]{1,0:T(8,128)(2,1)S(1)}, bf16[16,1024]{1,0:T(8,128)(2,1)S(1)}, u32[]{:S(2)}, u32[]{:S(2)}) collective-permute-start(bf16[16,1024]{1,0:T(8,128)(2,1)S(1)} %get-tuple-element.21.own), channel_id=1, source_target_pairs={{0,8},{2,10},{4,12},{6,14},{8,0},{10,2},{12,4},{14,6},{1,9},{3,11}... | collective-permute-start | bytes 98312 | tf_op jit(solution)/shard_map/ppermute | solution.py:26
  52.3 5.3 %collective-permute-start.5 = (bf16[2,16,1024]{2,1,0:T(8,128)(2,1)S(1)}, bf16[2,16,1024]{2,1,0:T(8,128)(2,1)S(1)}, u32[]{:S(2)}, u32[]{:S(2)}) collective-permute-start(bf16[2,16,1024]{2,1,0:T(8,128)(2,1)S(1)} %shard_map.133.own), channel_id=1, source_target_pairs={{0,4},{2,6},{4,0},{6,2},{8,12},{10,14},{12,8},{14,10},{1,5},{3,7},... | collective-permute-start | bytes 196616 | tf_op jit(solution)/shard_map/ppermute | solution.py:26
  52.8 15.2 %all-to-all-start.1 = ((bf16[8,16,8,128]{3,2,1,0:T(8,128)(2,1)}), bf16[8,16,8,128]{3,2,1,0:T(8,128)(2,1)S(1)}, u32[]{:S(2)}, u32[]{:S(2)}) async-start(bf16[8,16,8,128]{3,2,1,0:T(8,128)(2,1)} %shard_map.132.refs_0_), calls=%async_computation.1 | async-start | bytes 524288 | tf_op jit(solution)/shard_map/all_to_all | solution.py:22
  57.6 3.9 %collective-permute-start.6 = (bf16[4,16,1024]{2,1,0:T(8,128)(2,1)S(1)}, bf16[4,16,1024]{2,1,0:T(8,128)(2,1)S(1)}, u32[]{:S(2)}, u32[]{:S(2)}) collective-permute-start(bf16[4,16,1024]{2,1,0:T(8,128)(2,1)S(1)} %shard_map.134), channel_id=1, source_target_pairs={{0,2},{2,0},{4,6},{6,4},{8,10},{10,8},{12,14},{14,12},{1,3},{3,1},... | collective-permute-start | bytes 393224 | tf_op jit(solution)/shard_map/ppermute | solution.py:26
  57.9 34.0 %collective-permute-start.3 = (bf16[8,40,1024]{2,1,0:T(8,128)(2,1)S(1)}, bf16[8,40,1024]{2,1,0:T(8,128)(2,1)S(1)}, u32[]{:S(2)}, u32[]{:S(2)}) collective-permute-start(bf16[8,40,1024]{2,1,0:T(8,128)(2,1)S(1)} %pad_maximum_fusion.refs_0_), channel_id=1, source_target_pairs={{0,1},{1,0},{2,3},{3,2},{4,5},{5,4},{6,7},{7,6},{8,9},{9,8},{10,11... | collective-permute-start | bytes 1966088 | tf_op jit(solution)/shard_map/ppermute | solution.py:26
  61.6 6.4 %collective-permute-start.7 = (bf16[8,16,1024]{2,1,0:T(8,128)(2,1)S(1)}, bf16[8,16,1024]{2,1,0:T(8,128)(2,1)S(1)}, u32[]{:S(2)}, u32[]{:S(2)}) collective-permute-start(bf16[8,16,1024]{2,1,0:T(8,128)(2,1)S(1)} %pad_maximum_fusion.1.refs_2_), channel_id=1, source_target_pairs={{0,1},{1,0},{2,3},{3,2},{4,5},{5,4},{6,7},{7,6},{8,9},{9,8},{10,11... | collective-permute-start | bytes 786440 | tf_op jit(solution)/shard_map/ppermute | solution.py:26
  68.4 8.2 %collective-permute-start.14 = (bf16[16,24,128]{2,1,0:T(8,128)(2,1)S(1)}, bf16[16,24,128]{2,1,0:T(8,128)(2,1)S(1)}, u32[]{:S(2)}, u32[]{:S(2)}) collective-permute-start(bf16[16,24,128]{2,1,0:T(8,128)(2,1)S(1)} %get-tuple-element.24.refs_7_), channel_id=1, source_target_pairs={{0,112},{16,96},{32,80},{48,64},{64,48},{80,32},{96,16},{112,0},{1... | collective-permute-start | bytes 294920 | tf_op jit(solution)/shard_map/ppermute | solution.py:26
  68.5 12.8 %collective-permute-start.13 = (bf16[16,24,128]{2,1,0:T(8,128)(2,1)S(1)}, bf16[16,24,128]{2,1,0:T(8,128)(2,1)S(1)}, u32[]{:S(2)}, u32[]{:S(2)}) collective-permute-start(bf16[16,24,128]{2,1,0:T(8,128)(2,1)S(1)} %get-tuple-element.24.refs_7_), channel_id=1, source_target_pairs={{0,96},{16,112},{32,64},{48,80},{64,32},{80,48},{96,0},{112,16},{1... | collective-permute-start | bytes 294920 | tf_op jit(solution)/shard_map/ppermute | solution.py:26
  70.2 15.9 %collective-permute-start.12 = (bf16[16,24,128]{2,1,0:T(8,128)(2,1)S(1)}, bf16[16,24,128]{2,1,0:T(8,128)(2,1)S(1)}, u32[]{:S(2)}, u32[]{:S(2)}) collective-permute-start(bf16[16,24,128]{2,1,0:T(8,128)(2,1)S(1)} %get-tuple-element.24.refs_7_), channel_id=1, source_target_pairs={{0,80},{16,64},{32,112},{48,96},{64,16},{80,0},{96,48},{112,32},{1... | collective-permute-start | bytes 294920 | tf_op jit(solution)/shard_map/ppermute | solution.py:26
  72.0 16.1 %collective-permute-start.11 = (bf16[16,24,128]{2,1,0:T(8,128)(2,1)S(1)}, bf16[16,24,128]{2,1,0:T(8,128)(2,1)S(1)}, u32[]{:S(2)}, u32[]{:S(2)}) collective-permute-start(bf16[16,24,128]{2,1,0:T(8,128)(2,1)S(1)} %get-tuple-element.24.refs_7_), channel_id=1, source_target_pairs={{0,64},{16,80},{32,96},{48,112},{64,0},{80,16},{96,32},{112,48},{1... | collective-permute-start | bytes 294920 | tf_op jit(solution)/shard_map/ppermute | solution.py:26
  76.5 11.6 %collective-permute-start.10 = (bf16[16,24,128]{2,1,0:T(8,128)(2,1)S(1)}, bf16[16,24,128]{2,1,0:T(8,128)(2,1)S(1)}, u32[]{:S(2)}, u32[]{:S(2)}) collective-permute-start(bf16[16,24,128]{2,1,0:T(8,128)(2,1)S(1)} %get-tuple-element.24.refs_7_), channel_id=1, source_target_pairs={{0,48},{16,32},{32,16},{48,0},{64,112},{80,96},{96,80},{112,64},{1... | collective-permute-start | bytes 294920 | tf_op jit(solution)/shard_map/ppermute | solution.py:26
  81.3 10.6 %collective-permute-start.9 = (bf16[16,24,128]{2,1,0:T(8,128)(2,1)S(1)}, bf16[16,24,128]{2,1,0:T(8,128)(2,1)S(1)}, u32[]{:S(2)}, u32[]{:S(2)}) collective-permute-start(bf16[16,24,128]{2,1,0:T(8,128)(2,1)S(1)} %get-tuple-element.24.refs_7_), channel_id=1, source_target_pairs={{0,32},{16,48},{32,0},{48,16},{64,96},{80,112},{96,64},{112,80},{1... | collective-permute-start | bytes 294920 | tf_op jit(solution)/shard_map/ppermute | solution.py:26
  86.0 5.8 %collective-permute-start.8 = (bf16[16,24,128]{2,1,0:T(8,128)(2,1)S(1)}, bf16[16,24,128]{2,1,0:T(8,128)(2,1)S(1)}, u32[]{:S(2)}, u32[]{:S(2)}) collective-permute-start(bf16[16,24,128]{2,1,0:T(8,128)(2,1)S(1)} %get-tuple-element.24.refs_7_), channel_id=1, source_target_pairs={{0,16},{16,0},{32,48},{48,32},{64,80},{80,64},{96,112},{112,96},{1... | collective-permute-start | bytes 294920 | tf_op jit(solution)/shard_map/ppermute | solution.py:26
  92.8 9.0 %collective-permute-start.15 = (bf16[200,128]{1,0:T(8,128)(2,1)S(1)}, bf16[200,128]{1,0:T(8,128)(2,1)S(1)}, u32[]{:S(2)}, u32[]{:S(2)}) collective-permute-start(bf16[200,128]{1,0:T(8,128)(2,1)S(1)} %get-tuple-element.26), channel_id=1, source_target_pairs={{0,16},{16,0},{32,48},{48,32},{64,80},{80,64},{96,112},{112,96},{1... | collective-permute-start | bytes 153608 | tf_op jit(solution)/shard_map/ppermute | solution.py:26
  94.8 9.9 %collective-permute-start.16 = (bf16[200,128]{1,0:T(8,128)(2,1)S(1)}, bf16[200,128]{1,0:T(8,128)(2,1)S(1)}, u32[]{:S(2)}, u32[]{:S(2)}) collective-permute-start(bf16[200,128]{1,0:T(8,128)(2,1)S(1)} %get-tuple-element.27), channel_id=1, source_target_pairs={{0,32},{16,48},{32,0},{48,16},{64,96},{80,112},{96,64},{112,80},{1... | collective-permute-start | bytes 153608 | tf_op jit(solution)/shard_map/ppermute | solution.py:26
  97.4 8.3 %collective-permute-start.17 = (bf16[200,128]{1,0:T(8,128)(2,1)S(1)}, bf16[200,128]{1,0:T(8,128)(2,1)S(1)}, u32[]{:S(2)}, u32[]{:S(2)}) collective-permute-start(bf16[200,128]{1,0:T(8,128)(2,1)S(1)} %get-tuple-element.28), channel_id=1, source_target_pairs={{0,48},{16,32},{32,16},{48,0},{64,112},{80,96},{96,80},{112,64},{1... | collective-permute-start | bytes 153608 | tf_op jit(solution)/shard_map/ppermute | solution.py:26
  97.6 8.1 %collective-permute-start.18 = (bf16[200,128]{1,0:T(8,128)(2,1)S(1)}, bf16[200,128]{1,0:T(8,128)(2,1)S(1)}, u32[]{:S(2)}, u32[]{:S(2)}) collective-permute-start(bf16[200,128]{1,0:T(8,128)(2,1)S(1)} %get-tuple-element.29), channel_id=1, source_target_pairs={{0,64},{16,80},{32,96},{48,112},{64,0},{80,16},{96,32},{112,48},{1... | collective-permute-start | bytes 153608 | tf_op jit(solution)/shard_map/ppermute | solution.py:26
  99.7 6.4 %collective-permute-start.19 = (bf16[200,128]{1,0:T(8,128)(2,1)S(1)}, bf16[200,128]{1,0:T(8,128)(2,1)S(1)}, u32[]{:S(2)}, u32[]{:S(2)}) collective-permute-start(bf16[200,128]{1,0:T(8,128)(2,1)S(1)} %get-tuple-element.30), channel_id=1, source_target_pairs={{0,80},{16,64},{32,112},{48,96},{64,16},{80,0},{96,48},{112,32},{1... | collective-permute-start | bytes 153608 | tf_op jit(solution)/shard_map/ppermute | solution.py:26
  101.9 7.1 %collective-permute-start.20 = (bf16[200,128]{1,0:T(8,128)(2,1)S(1)}, bf16[200,128]{1,0:T(8,128)(2,1)S(1)}, u32[]{:S(2)}, u32[]{:S(2)}) collective-permute-start(bf16[200,128]{1,0:T(8,128)(2,1)S(1)} %get-tuple-element.31), channel_id=1, source_target_pairs={{0,96},{16,112},{32,64},{48,80},{64,32},{80,48},{96,0},{112,16},{1... | collective-permute-start | bytes 153608 | tf_op jit(solution)/shard_map/ppermute | solution.py:26
  104.6 6.7 %collective-permute-start.21 = (bf16[200,128]{1,0:T(8,128)(2,1)S(1)}, bf16[200,128]{1,0:T(8,128)(2,1)S(1)}, u32[]{:S(2)}, u32[]{:S(2)}) collective-permute-start(bf16[200,128]{1,0:T(8,128)(2,1)S(1)} %get-tuple-element.32), channel_id=1, source_target_pairs={{0,112},{16,96},{32,80},{48,64},{64,48},{80,32},{96,16},{112,0},{1... | collective-permute-start | bytes 153608 | tf_op jit(solution)/shard_map/ppermute | solution.py:26
  111.5 16.4 %copy-start = (f32[8,1024]{1,0:T(8,128)S(1)}, f32[8,1024]{1,0:T(8,128)}, u32[]{:S(2)}) copy-start(f32[8,1024]{1,0:T(8,128)} %refs_1_.3) | copy-start | bytes 98308
  111.5 16.4 %copy-start.1 = (f32[2,1024]{1,0:T(2,128)S(1)}, f32[2,1024]{1,0:T(2,128)}, u32[]{:S(2)}) copy-start(f32[2,1024]{1,0:T(2,128)} %refs_2_.3) | copy-start | bytes 24580
